TPU v7x, 32 devices: a whole 2x2x4 slice. The times are simulated.
32 devices in a mesh: seq: 16 (over z, y, x), head: 2 (over core).
Axes of the slice: x: 2, y: 2, z: 4, core: 2. Of those that a mesh axis runs over, the one named last changes fastest.
Arguments:
- hidden: bfloat16 [8192, 1536], P('seq'), may hold values from -6 to 6
- cotangent: bfloat16 [8192, 1536], P('seq'), may hold values from -6 to 6
- norm_gain: float32 [1536], replicated, may hold values from 0.5 to 1.5
- proj_inner: bfloat16 [1536, 2, 3072], P(None, None, 'head'), may hold values from -0.15625 to 0.15625
- proj_step: bfloat16 [1536, 48], P(None, 'head'), may hold values from -0.15625 to 0.15625
- proj_shared: bfloat16 [1536, 256], replicated, may hold values from -0.15625 to 0.15625
- conv_values: float32 [5, 3072], P(None, 'head'), may hold values from -0.8 to 0.8
- conv_shared: float32 [5, 256], replicated, may hold values from -0.8 to 0.8
- step_bias: float32 [48], P('head'), may hold values from -4 to -2
- decay_log: float32 [48], P('head'), may hold values from -12 to 0
- skip_gain: float32 [48], P('head'), may hold values from 0.1 to 1.9
- gate_gain: float32 [3072], P('head'), may hold values from 0.5 to 1.5
- proj_out: bfloat16 [1536, 3072], P(None, 'head'), may hold values from -0.109375 to 0.109375
Outputs:
- block_out: float32 [8192, 1536], P('seq')
- grad_hidden: float32 [8192, 1536], P('seq')
- grad_norm_gain: float32 [1536], replicated
- grad_proj_inner: float32 [1536, 2, 3072], P('seq', None, 'head')
- grad_proj_step: float32 [1536, 48], P('seq', 'head')
- grad_proj_shared: float32 [1536, 256], P('seq', 'head')
- grad_conv_values: float32 [5, 3072], P(None, 'head')
- grad_conv_shared: float32 [5, 256], P(None, 'head')
- grad_step_bias: float32 [48], P('head')
- grad_decay_log: float32 [48], P('head')
- grad_skip_gain: float32 [48], P('head')
- grad_gate_gain: float32 [3072], P('head')
- grad_proj_out: float32 [1536, 3072], P('seq', 'head')
All inputs are finite; a program needn't handle non-finite values.
Results may differ from a plain program's by a relative error of at most 0.012.
The roundings to bfloat16 on the way count: a program that leaves them out, or rounds other values in their place, can miss the bound.
Values may be sent and summed in bfloat16 or wider, within the bound.
A program may use at most 192 MiB of HBM per device.

v0:
```python
import jax
import jax.numpy as jnp
from jax import lax
from jax.sharding import PartitionSpec as P

HEAD_DIM = 64
STATE = 128
CONV = 4
GROUP = 256
INNER = 3072


norm_eps = 1e-05
highest = lax.Precision.HIGHEST


def from_behind(shard, axis, by):
    size = lax.axis_size(axis)
    pairs = [(i, i + by) for i in range(size) if 0 <= i + by < size]
    return lax.ppermute(shard, axis, pairs)


def silu_grad(values):
    sigmoid = jax.nn.sigmoid(values)
    return sigmoid * (1.0 + values * (1.0 - sigmoid))


def within_groups(rates):
    group_count = rates.shape[0] // GROUP
    lower_mask = (jnp.arange(GROUP)[:, None] >= jnp.arange(GROUP)[None, :]).astype(rates.dtype)
    return jnp.einsum(
        "ij,cjh->cih",
        lower_mask,
        rates.reshape(group_count, GROUP, rates.shape[1]),
        precision=highest,
    )


def ssd_parts(values_f, step_raw, input_map, output_map, step_bias, decay_log, skip_gain):
    token_count, head_count, head_width = values_f.shape
    group_count = token_count // GROUP
    step_size = jax.nn.softplus(step_raw + step_bias)
    rates = -step_size * jnp.exp(decay_log)
    running = within_groups(rates)
    values_c = values_f.reshape(group_count, GROUP, head_count, head_width)
    weighted = values_c * step_size.reshape(group_count, GROUP, head_count)[..., None]
    inputs_c = input_map.reshape(group_count, GROUP, -1)
    outputs_c = output_map.reshape(group_count, GROUP, -1)
    scores = jnp.einsum("cin,cjn->cij", outputs_c, inputs_c, precision=highest)
    lower_mask = jnp.arange(GROUP)[:, None] >= jnp.arange(GROUP)[None, :]
    causal_mask = lower_mask[None, :, :, None]
    log_gap = running[:, :, None, :] - running[:, None, :, :]
    decay_mat = jnp.where(causal_mask, jnp.exp(jnp.where(causal_mask, log_gap, 0.0)), 0.0)
    within_part = jnp.einsum(
        "cijh,cjhp->cihp", scores[:, :, :, None] * decay_mat, weighted, precision=highest
    )
    group_total = running[:, -1, :]
    to_end = jnp.exp(group_total[:, None, :] - running)
    group_states = jnp.einsum(
        "cjhp,cjn->chpn", weighted * to_end[..., None], inputs_c, precision=highest
    )

    def carry_step(carry_state, group_item):
        gain_log, group_state = group_item
        return (jnp.exp(gain_log)[:, None, None] * carry_state + group_state, carry_state)

    zero_state = jnp.zeros((head_count, head_width, input_map.shape[1]), jnp.float32)
    state_final, entering = lax.scan(carry_step, zero_state, (group_total, group_states))
    from_state = jnp.exp(running)[..., None] * jnp.einsum(
        "cin,chpn->cihp", outputs_c, entering, precision=highest
    )
    local_part = (within_part + from_state).reshape(values_f.shape) + skip_gain[
        None, :, None
    ] * values_f
    offsets = jnp.cumsum(group_total, axis=0) - group_total
    running_log = (running + offsets[:, None, :]).reshape(token_count, head_count)
    return (local_part, state_final, running_log, jnp.sum(group_total, axis=0))


def ssd_full(values_f, step_raw, input_map, output_map, step_bias, decay_log, skip_gain, state_in):
    local_part, state_final, running_log, decay_total = ssd_parts(
        values_f, step_raw, input_map, output_map, step_bias, decay_log, skip_gain
    )
    carried = jnp.exp(running_log)[:, :, None] * jnp.einsum(
        "tn,hpn->thp", output_map, state_in, precision=highest
    )
    return (local_part + carried, jnp.exp(decay_total)[:, None, None] * state_in + state_final)


def causal_conv(padded, conv_taps):
    out_rows = padded.shape[0] - (CONV - 1)
    wide_ext = padded.astype(jnp.float32)
    result = conv_taps[CONV][None, :] + conv_taps[0][None, :] * wide_ext[0:out_rows]
    for offset in range(1, CONV):
        result = result + conv_taps[offset][None, :] * wide_ext[offset : offset + out_rows]
    return result


def conv_back(padded, conv_taps, conv_grad):
    out_rows = conv_grad.shape[0]
    wide_ext = padded.astype(jnp.float32)
    tap_rows = [
        jnp.sum(wide_ext[offset : offset + out_rows] * conv_grad, axis=0) for offset in range(CONV)
    ]
    tap_rows.append(jnp.sum(conv_grad, axis=0))
    spread = jnp.pad(conv_taps[0][None, :] * conv_grad, ((0, CONV - 1), (0, 0)))
    for offset in range(1, CONV):
        spread = spread + jnp.pad(
            conv_taps[offset][None, :] * conv_grad, ((offset, CONV - 1 - offset), (0, 0))
        )
    return (spread, jnp.stack(tap_rows))


def front(hidden, norm_gain, proj_inner, proj_step, proj_shared):
    wide_hidden = hidden.astype(jnp.float32)
    norm_scale = lax.rsqrt(jnp.mean(wide_hidden * wide_hidden, axis=1, keepdims=True) + norm_eps)
    normed = (wide_hidden * norm_scale * norm_gain).astype(jnp.bfloat16)
    both_inner = jnp.dot(
        normed, proj_inner.reshape(proj_inner.shape[0], -1), preferred_element_type=jnp.float32
    )
    both_inner = both_inner.reshape(hidden.shape[0], 2, -1)
    gate_in = both_inner[:, 0]
    values_in = both_inner[:, 1].astype(jnp.bfloat16)
    step_raw = jnp.dot(normed, proj_step, preferred_element_type=jnp.float32)
    shared_in = jnp.dot(normed, proj_shared, preferred_element_type=jnp.float32).astype(
        jnp.bfloat16
    )
    return (wide_hidden, norm_scale, normed, gate_in, values_in, step_raw, shared_in)


def spread_layout(totals, states, parts):
    heads_here = totals.shape[0]
    piece = states.shape[1] * states.shape[2] // parts
    state_layout = states.reshape(heads_here, 1, parts, piece)
    total_layout = jnp.broadcast_to(totals[:, None, None, None], (heads_here, 1, parts, 1))
    return (total_layout, state_layout)


def prefix_pieces(received, reverse):
    totals = received[0][:, :, 0, 0]
    states = received[1][:, :, 0, :]
    count = totals.shape[1]
    position = jnp.arange(count)
    target = position[:, None, None]
    source = position[None, :, None]
    middle = position[None, None, :]
    if reverse:
        between = (middle > target) & (middle < source)
        taken = position[None, :] > position[:, None]
    else:
        between = (middle < target) & (middle > source)
        taken = position[None, :] < position[:, None]
    exponent = jnp.einsum("jik,hk->hji", between.astype(jnp.float32), totals, precision=highest)
    weights = jnp.where(taken[None], jnp.exp(exponent), 0.0)
    mixed = jnp.einsum("hji,hip->hjp", weights, states, precision=highest)
    return mixed[:, :, None, :]


def earlier_pieces(received):
    return prefix_pieces(received, False)


def later_pieces(received):
    return prefix_pieces(received, True)


def body(
    hidden,
    cotangent,
    norm_gain,
    proj_inner,
    proj_step,
    proj_shared,
    conv_values,
    conv_shared,
    step_bias,
    decay_log,
    skip_gain,
    gate_gain,
    proj_out,
):
    tokens_here = hidden.shape[0]
    inner_here = proj_inner.shape[2]
    heads_here = proj_step.shape[1]
    shared_here = conv_shared.shape[1] // lax.axis_size("head")
    shared_start = lax.axis_index("head") * shared_here
    seq_count = lax.axis_size("seq")
    halo_rows = CONV - 1
    contract_cols = (((1,), (1,)), ((), ()))
    contract_rows = (((0,), (0,)), ((), ()))
    wide_hidden, norm_scale, normed, gate_in, values_in, step_raw, shared_in = front(
        hidden, norm_gain, proj_inner, proj_step, proj_shared
    )
    values_edge, shared_edge = from_behind(
        (values_in[-halo_rows:], shared_in[-halo_rows:]), "seq", 1
    )
    values_ext = jnp.concatenate([values_edge, values_in], axis=0)
    shared_ext = jnp.concatenate([shared_edge, shared_in], axis=0)
    values_conv = causal_conv(values_ext, conv_values)
    shared_conv = causal_conv(shared_ext, conv_shared)
    values_act = jax.nn.silu(values_conv).astype(jnp.bfloat16)
    shared_act = jax.nn.silu(shared_conv).astype(jnp.bfloat16)
    ssd_inputs = (
        values_act.astype(jnp.float32).reshape(tokens_here, heads_here, HEAD_DIM),
        step_raw,
        shared_act[:, :STATE].astype(jnp.float32),
        shared_act[:, STATE:].astype(jnp.float32),
        step_bias,
        decay_log,
        skip_gain,
    )
    local_part, state_final, running_log, decay_total = ssd_parts(*ssd_inputs)
    total_layout, state_layout = spread_layout(decay_total, state_final, seq_count)
    mixed_pieces = earlier_pieces(
        (
            lax.all_to_all(total_layout, "seq", split_axis=2, concat_axis=1, tiled=True),
            lax.all_to_all(state_layout, "seq", split_axis=2, concat_axis=1, tiled=True),
        )
    )
    state_in = lax.all_to_all(mixed_pieces, "seq", split_axis=1, concat_axis=2, tiled=True).reshape(
        state_final.shape
    )
    carried = jnp.exp(running_log)[:, :, None] * jnp.einsum(
        "tn,hpn->thp", ssd_inputs[3], state_in, precision=highest
    )
    output_y = (local_part + carried).reshape(tokens_here, inner_here)
    gate_act = jax.nn.silu(gate_in)
    gated_out = output_y * gate_act
    gated_w = (gated_out * gate_gain).astype(jnp.bfloat16)
    partial_mix = lax.dot_general(
        gated_w, proj_out, contract_cols, preferred_element_type=jnp.float32
    )
    mixed_sum, squares = lax.psum((partial_mix, jnp.sum(gated_out * gated_out, axis=1)), "head")
    inverse = lax.rsqrt(squares / INNER + norm_eps)
    block_out = wide_hidden + mixed_sum * inverse[:, None]
    wide_cot = cotangent.astype(jnp.float32)
    grad_mixed = (wide_cot * inverse[:, None]).astype(jnp.bfloat16)
    grad_inverse = jnp.sum(wide_cot * mixed_sum, axis=1)
    grad_gated_w = jnp.dot(grad_mixed, proj_out, preferred_element_type=jnp.float32)
    term_out = lax.dot_general(
        grad_mixed, gated_w, contract_rows, preferred_element_type=jnp.float32
    )
    grad_gated = grad_gated_w * gate_gain - (grad_inverse * inverse**3 / INNER)[:, None] * gated_out
    term_gate = jnp.sum(grad_gated_w * gated_out, axis=0)
    grad_y = grad_gated * gate_act
    grad_gate_in = grad_gated * output_y * silu_grad(gate_in)
    grad_y3 = grad_y.reshape(tokens_here, heads_here, HEAD_DIM)
    own_term = jnp.einsum(
        "thp,tn->hpn", grad_y3 * jnp.exp(running_log)[:, :, None], ssd_inputs[3], precision=highest
    )
    total_back, term_layout = spread_layout(decay_total, own_term, seq_count)
    later_mixed = later_pieces(
        (
            lax.all_to_all(total_back, "seq", split_axis=2, concat_axis=1, tiled=True),
            lax.all_to_all(term_layout, "seq", split_axis=2, concat_axis=1, tiled=True),
        )
    )
    grad_state = lax.all_to_all(
        later_mixed, "seq", split_axis=1, concat_axis=2, tiled=True
    ).reshape(own_term.shape)
    _, pullback = jax.vjp(ssd_full, *ssd_inputs, state_in)
    (
        grad_values_act,
        grad_step_raw,
        grad_bmat,
        grad_cmat,
        grad_step_bias,
        grad_decay,
        grad_skip,
        _,
    ) = pullback((grad_y3, grad_state))
    grad_values_conv = grad_values_act.reshape(tokens_here, inner_here) * silu_grad(values_conv)
    shared_full = jnp.concatenate([grad_bmat, grad_cmat], axis=1)
    shared_part = lax.psum_scatter(shared_full, "head", scatter_dimension=1, tiled=True)
    shared_conv_own = lax.dynamic_slice_in_dim(shared_conv, shared_start, shared_here, 1)
    grad_shared_conv = shared_part * silu_grad(shared_conv_own)
    shared_ext_own = lax.dynamic_slice_in_dim(shared_ext, shared_start, shared_here, 1)
    taps_own = lax.dynamic_slice_in_dim(conv_shared, shared_start, shared_here, 1)
    values_spread, term_conv_values = conv_back(values_ext, conv_values, grad_values_conv)
    shared_spread, term_conv_shared = conv_back(shared_ext_own, taps_own, grad_shared_conv)
    values_back, shared_back = from_behind(
        (values_spread[:halo_rows], shared_spread[:halo_rows]), "seq", -1
    )
    grad_values_in = values_spread[halo_rows:] + jnp.pad(
        values_back, ((tokens_here - halo_rows, 0), (0, 0))
    )
    grad_shared_in = shared_spread[halo_rows:] + jnp.pad(
        shared_back, ((tokens_here - halo_rows, 0), (0, 0))
    )
    grad_inner = (
        jnp.stack([grad_gate_in, grad_values_in], axis=1)
        .astype(jnp.bfloat16)
        .reshape(tokens_here, 2 * inner_here)
    )
    grad_step_w = grad_step_raw.astype(jnp.bfloat16)
    grad_shared_w = grad_shared_in.astype(jnp.bfloat16)
    shared_proj_own = lax.dynamic_slice_in_dim(proj_shared, shared_start, shared_here, 1)
    partial_normed = lax.dot_general(
        grad_inner,
        proj_inner.reshape(proj_inner.shape[0], -1),
        contract_cols,
        preferred_element_type=jnp.float32,
    )
    partial_normed = partial_normed + lax.dot_general(
        grad_step_w, proj_step, contract_cols, preferred_element_type=jnp.float32
    )
    partial_normed = partial_normed + lax.dot_general(
        grad_shared_w, shared_proj_own, contract_cols, preferred_element_type=jnp.float32
    )
    grad_normed = lax.psum(partial_normed, "head")
    normal_hat = wide_hidden * norm_scale
    term_norm = jnp.sum(grad_normed * normal_hat, axis=0)
    grad_hat = grad_normed * norm_gain
    grad_hidden = wide_cot + norm_scale * (
        grad_hat - normal_hat * jnp.mean(grad_hat * normal_hat, axis=1, keepdims=True)
    )
    term_inner = lax.dot_general(
        normed, grad_inner, contract_rows, preferred_element_type=jnp.float32
    ).reshape(normed.shape[1], 2, inner_here)
    term_small = lax.dot_general(
        normed,
        jnp.concatenate([grad_step_w, grad_shared_w], axis=1),
        contract_rows,
        preferred_element_type=jnp.float32,
    )
    summed_inner, summed_small, summed_out = (
        lax.psum_scatter(term_inner, "seq", scatter_dimension=0, tiled=True),
        lax.psum_scatter(term_small, "seq", scatter_dimension=0, tiled=True),
        lax.psum_scatter(term_out, "seq", scatter_dimension=0, tiled=True),
    )
    head_terms = jnp.stack([grad_step_bias, grad_decay, grad_skip])
    sum_conv_values, sum_conv_shared, sum_heads, sum_gate, sum_norm = lax.psum(
        (term_conv_values, term_conv_shared, head_terms, term_gate, term_norm), "seq"
    )
    return (
        block_out,
        grad_hidden,
        sum_norm,
        summed_inner,
        summed_small[:, :heads_here],
        summed_small[:, heads_here:],
        sum_conv_values,
        sum_conv_shared,
        sum_heads[0],
        sum_heads[1],
        sum_heads[2],
        sum_gate,
        summed_out,
    )


def solution(mesh):
    return jax.shard_map(
        body,
        mesh=mesh,
        in_specs=(
            P("seq", None),
            P("seq", None),
            P(),
            P(None, None, "head"),
            P(None, "head"),
            P(),
            P(None, "head"),
            P(),
            P("head"),
            P("head"),
            P("head"),
            P("head"),
            P(None, "head"),
        ),
        out_specs=(
            P("seq", None),
            P("seq", None),
            P(),
            P("seq", None, "head"),
            P("seq", "head"),
            P("seq", "head"),
            P(None, "head"),
            P(None, "head"),
            P("head"),
            P("head"),
            P("head"),
            P("head"),
            P("seq", "head"),
        ),
        check_vma=False,
    )
```

profile of v0, /device:TPU:0, one launch (start us, length us, event | category | flops | bytes accessed | tf_op | source)
XLA Modules:
  0.0 1035.8 jit_solution(14457197964105308952)
XLA Ops:
  13.6 8.3 all-to-all-start
  22.7 3.8 collective-permute-start.1
  26.5 9.8 copy.242
  36.3 12.6 %copy.173 = bf16[3072,1536]{1,0:T(8,128)(2,1)} copy(bf16[3072,1536]{0,1:T(8,128)(2,1)} %bitcast.291) | data formatting | bytes 18874368 | tf_op jit(solution)/shard_map/dot_general | solution.py:118
  48.9 10.8 %fusion.175 = (bf16[512,2,1536]{2,0,1:T(8,128)(2,1)S(1)}, f32[512,2,1536]{2,0,1:T(8,128)}) fusion(bf16[2,1536,1536]{2,1,0:T(8,128)(2,1)} %bitcast.299, f32[1536]{0:T(1024)S(1)} %copy-done.75, f32[512]{0:T(512)S(1)} %add_rsqrt_fusion.1, bf16[512,1536]{1,0:T(8,128)(2,1)S(1)} %copy-done.15), kind=kOutput, calls=%fused_computation.281 | convolution fusion | flops 4836556800 | bytes 20455424 | tf_op jit(solution)/shard_map/dot_general | solution.py:118
  60.3 4.2 collective-permute-start
  71.0 3.7 fusion.73
  78.2 5.2 reshape_reshape.7
  94.1 4.9 all-to-all-start.1
  99.7 3.8 slice.197
  110.2 7.4 all-to-all-done.1
  121.1 5.0 all-to-all-start.2
  130.2 14.1 %fusion.55 = f32[2,24,8,8,256]{4,3,2,1,0:T(8,128)S(1)} fusion(f32[2,256,24,64]{1,3,2,0:T(8,128)S(1)} %fusion.178, f32[2,256,24]{1,2,0:T(8,128)S(1)} %convolution_bitcast_fusion.4, f32[2,256,256]{2,1,0:T(8,128)S(1)} %fusion.177, pred[256,256]{1,0:T(8,128)(4,1)S(1)} %copy-done.68, f32[2,256,24,64]{1,0,3,2:T(2,128)S(1)} %copy-done.6, ...), kind=kOutput, calls=%fused_computation.82 | convolution fusion | flops 2430861312 | bytes 10174464 | tf_op jit(solution)/shard_map/cijh,cjhp->cihp/dot_general | solution.py:54
  152.6 6.9 multiply_reduce_fusion.10
  165.6 9.8 multiply_reduce_fusion
  177.0 6.7 fusion.101
  197.1 7.2 while.50
  204.3 4.2 all-reduce.15.cloned.1.call-done
  208.5 5.3 fusion.44
  215.3 5.3 multiply_reduce_fusion.1
  224.1 5.2 reshape_reshape.8
  234.3 7.3 all-to-all-start.3
  241.6 21.2 %fusion.19 = (f32[2,256,24]{1,2,0:T(8,128)}, f32[2,256,24]{1,2,0:T(8,128)}, f32[2,256,256]{2,1,0:T(8,128)S(1)}) fusion(f32[2,256,24]{1,2,0:T(8,128)S(1)} %copy-done.35, f32[2,256,256]{2,1,0:T(8,128)S(1)} %copy-done.45, pred[256,256]{1,0:T(8,128)(4,1)S(1)} %copy-done.69, f32[2,256,24,64]{1,0,3,2:T(2,128)} %reshape_reshape.7, ...), kind=kOutput, calls=%fused_computation.32 | convolution fusion | flops 2451152896 | bytes 7602176 | tf_op jit(solution)/shard_map/transpose(jvp(cijh,cjhp->cihp))/dot_general | solution.py:54
  265.1 7.1 fusion.86
  279.3 7.0 all-to-all-start.4
  286.3 4.8 fusion.66
  291.2 5.7 fusion.54
  296.8 9.1 all-to-all-done.4
  311.2 9.7 while.48
  320.9 7.7 fusion.87
  331.6 12.7 %multiply_reduce_fusion.6 = (f32[2,256,24]{1,2,0:T(8,128)S(1)}, f32[2,256,24]{1,2,0:T(8,128)S(1)}, f32[2,256,24,64]{1,3,2,0:T(8,128)}) fusion(f32[2,256,24,64]{1,3,2,0:T(8,128)S(1)} %fusion.179, f32[2,256,24,64]{1,0,3,2:T(2,128)S(1)} %copy-done.7, f32[2,256,24]{1,2,0:T(8,128)S(1)} %bitcast.318, f32[2,256,24]{1,2,0:T(8,128)S(1)} %copy-done.37, ...), kind=kOutput, calls=%fused_computation.89 | convolution fusion | flops 2434768896 | bytes 13418496 | tf_op jit(solution)/shard_map/transpose(jvp(cijh,cjhp->cihp))/dot_general | solution.py:54
  344.9 6.0 copy.226
  350.9 6.2 reshape.351
  357.1 13.0 %multiply_reduce_fusion.2 = (f32[1536]{0:T(1024)}, f32[1536]{0:T(1024)}, f32[1536]{0:T(1024)S(1)}, f32[1536]{0:T(1024)S(1)}, f32[1536]{0:T(1024)S(1)}, /*index=5*/f32[512,1536]{1,0:T(8,128)}, f32[512,1536]{1,0:T(8,128)}) fusion(f32[515,1536]{1,0:T(8,128)} %copy-done.1, f32[512,1536]{1,0:T(8,128)} %get-tuple-element.437, f32[512,1536]{1,0:T(8,128)} %reshape.351, ...), kind=kLoop, calls=%fused_computation.85 | loop fusion | flops 15720960 | bytes 31494144 | tf_op jit(solution)/shard_map/reduce_sum | solution.py:103
  370.1 3.7 copy.212
  373.8 7.0 fusion.90
  398.5 4.3 collective-permute-done.3
  404.9 9.3 fusion.34
  417.1 3.8 maximum_convert_fusion
  420.9 4.7 copy.214
  425.6 11.3 %fusion.46 = f32[1536,2,1536]{2,0,1:T(8,128)} fusion(bf16[512,2,1536]{0,2,1:T(8,128)(2,1)} %copy.214, bf16[512,1536]{1,0:T(8,128)(2,1)S(1)} %copy-done.16, f32[1536]{0:T(1024)S(1)} %copy-done.76, f32[512]{0:T(512)S(1)} %copy-done.86), kind=kOutput, calls=%fused_computation.68 | convolution fusion | flops 4834983936 | bytes 23601152 | tf_op jit(solution)/shard_map/dot_general | solution.py:317
  437.6 8.9 fusion.97
  447.6 85.2 %reduce-scatter.13.cloned.1.call-done = f32[96,152]{1,0:T(8,128)} async-done(((f32[1536,152]{1,0:T(8,128)}), f32[96,152]{1,0:T(8,128)}) %reduce-scatter.13.cloned.1.call-update) | async-done | bytes 58384
  535.9 22.0 %all-reduce.17.cloned.1.call-done = f32[512,1536]{1,0:T(8,128)} async-done(((f32[512,1536]{1,0:T(8,128)}), f32[512,1536]{1,0:T(8,128)}) %all-reduce.17.cloned.1.call-update) | async-done | bytes 3145744 | tf_op jit(solution)/shard_map/psum | solution.py:310
  560.7 83.5 %all-reduce.11 = (f32[1536]{0:T(1024)}, f32[5,1536]{1,0:T(8,128)}, f32[5,128]{1,0:T(8,128)}, f32[3,24]{1,0:T(4,128)S(1)}, f32[1536]{0:T(1024)}) all-reduce(f32[1536]{0:T(1024)S(1)} %get-tuple-element.362, f32[5,1536]{1,0:T(8,128)S(1)} %stack.63, f32[5,128]{1,0:T(8,128)S(1)} %stack.69, ...), channel_id=1, replica_groups=mesh['seq'=16,'head'=2] {'seq'}, use_global_device_ids=true, to_apply=%region_29.30 | all-reduce | flops 11464 | bytes 91712 | tf_op jit(solution)/shard_map/psum | solution.py:332
  644.7 5.0 convert_add_fusion
  649.7 202.4 %reduce-scatter.9.cloned.1.call-done = f32[96,2,1536]{2,0,1:T(8,128)} async-done(((f32[1536,2,1536]{2,0,1:T(8,128)}), f32[96,2,1536]{2,0,1:T(8,128)}) %reduce-scatter.9.cloned.1.call-update) | async-done | bytes 1179664 | tf_op jit(solution)/shard_map/reduce_scatter | solution.py:327
  855.3 173.4 %reduce-scatter.11.cloned.1.call-done = f32[96,1536]{1,0:T(8,128)} async-done(((f32[1536,1536]{1,0:T(8,128)}), f32[96,1536]{1,0:T(8,128)}) %reduce-scatter.11.cloned.1.call-update) | async-done | bytes 589840 | tf_op jit(solution)/shard_map/reduce_scatter | solution.py:329
  (407 shorter events, 152.9 us)
Async XLA Ops:
  7.2 14.8 %copy-start = (bf16[1536,256]{1,0:T(8,128)(2,1)S(1)}, bf16[1536,256]{1,0:T(8,128)(2,1)}, u32[]{:S(2)}) copy-start(bf16[1536,256]{1,0:T(8,128)(2,1)} %param.24) | copy-start | bytes 2359300
  7.2 14.8 %copy-start.15 = (bf16[512,1536]{1,0:T(8,128)(2,1)S(1)}, bf16[512,1536]{1,0:T(8,128)(2,1)}, u32[]{:S(2)}) copy-start(bf16[512,1536]{1,0:T(8,128)(2,1)} %param.19) | copy-start | bytes 4718596
  7.2 14.8 %copy-start.75 = (f32[1536]{0:T(1024)S(1)}, f32[1536]{0:T(1024)}, u32[]{:S(2)}) copy-start(f32[1536]{0:T(1024)} %param.21) | copy-start | bytes 18436
  8.0 14.6 %copy-start.118 = (f32[24]{0:T(128)}, f32[24]{0:T(128)S(1)}, u32[]{:S(2)}) copy-start(f32[24]{0:T(128)S(1)} %exp.101) | copy-start | bytes 292
  9.8 39.1 %copy-start.85 = (f32[512]{0:T(512)}, f32[512]{0:T(512)S(1)}, u32[]{:S(2)}) copy-start(f32[512]{0:T(512)S(1)} %add_rsqrt_fusion.1) | copy-start | bytes 6148
  12.8 117.3 %copy-start.34 = (f32[2,256,24]{1,2,0:T(8,128)}, f32[2,256,24]{1,2,0:T(8,128)S(1)}, u32[]{:S(2)}) copy-start(f32[2,256,24]{1,2,0:T(8,128)S(1)} %convolution_bitcast_fusion.4) | copy-start | bytes 147460
  13.0 23.3 %copy-start.110 = (f32[24]{0:T(128)}, f32[24]{0:T(128)S(1)}, u32[]{:S(2)}) copy-start(f32[24]{0:T(128)S(1)} %get-tuple-element.378) | copy-start | bytes 292
  13.6 80.5 %all-to-all-start = ((f32[24,1,16,1]{0,3,1,2:T(1,128)}), f32[24,1,16,1]{0,3,1,2:T(1,128)S(1)}, u32[]{:S(2)}, u32[]{:S(2)}) async-start(f32[24,1,16,1]{0,3,1,2:T(1,128)} %broadcast_in_dim.92), calls=%async_computation | async-start | bytes 16384 | tf_op jit(solution)/shard_map/all_to_all | solution.py:216
  22.6 13.7 %copy-start.39 = (bf16[512,256]{1,0:T(8,128)(2,1)}, bf16[512,256]{1,0:T(8,128)(2,1)S(1)}, u32[]{:S(2)}) copy-start(bf16[512,256]{1,0:T(8,128)(2,1)S(1)} %convolution_convert_fusion) | copy-start | bytes 786436
  22.7 44.2 %collective-permute-start.1 = (bf16[3,256]{1,0:T(4,128)(2,1)S(1)}, bf16[3,256]{1,0:T(4,128)(2,1)S(1)}, u32[]{:S(2)}, u32[]{:S(2)}) collective-permute-start(bf16[3,256]{1,0:T(4,128)(2,1)S(1)} %slice.189), channel_id=1, source_target_pairs={{0,2},{2,4},{4,6},{6,8},{8,10},{10,12},{12,14},{14,16},{16,18},{18... | collective-permute-start | bytes 4616 | tf_op jit(solution)/shard_map/ppermute | solution.py:20
  60.3 9.4 collective-permute-start
  65.6 17.8 %copy-start.32 = (f32[2,256,24]{1,2,0:T(8,128)}, f32[2,256,24]{1,2,0:T(8,128)S(1)}, u32[]{:S(2)}) copy-start(f32[2,256,24]{1,2,0:T(8,128)S(1)} %get-tuple-element.459) | copy-start | bytes 147460
  69.7 57.0 %copy-start.24 = (bf16[512,128]{1,0:T(8,128)(2,1)}, bf16[512,128]{1,0:T(8,128)(2,1)S(1)}, u32[]{:S(2)}) copy-start(bf16[512,128]{1,0:T(8,128)(2,1)S(1)} %get-tuple-element.455) | copy-start | bytes 393220
  90.6 12.8 %copy-start.83 = (f32[2,24]{1,0:T(2,128)}, f32[2,24]{1,0:T(2,128)S(1)}, u32[]{:S(2)}) copy-start(f32[2,24]{1,0:T(2,128)S(1)} %get-tuple-element.728) | copy-start | bytes 580
  94.1 13.6 %copy-start.66 = (f32[24,1,16,1]{0,3,1,2:T(1,128)}, f32[24,1,16,1]{0,3,1,2:T(1,128)S(1)}, u32[]{:S(2)}) copy-start(f32[24,1,16,1]{0,3,1,2:T(1,128)S(1)} %all-to-all-done) | copy-start | bytes 4612
  94.1 23.6 %all-to-all-start.1 = ((f32[24,1,16,512]{3,0,1,2:T(8,128)}), f32[24,1,16,512]{3,0,1,2:T(8,128)S(1)}, u32[]{:S(2)}, u32[]{:S(2)}) async-start(f32[24,1,16,512]{3,0,1,2:T(8,128)} %copy.181), calls=%async_computation.1 | async-start | bytes 1572864 | tf_op jit(solution)/shard_map/all_to_all | solution.py:217
  107.0 23.1 %copy-start.88 = (pred[16,16]{1,0:T(8,128)(4,1)}, pred[16,16]{1,0:T(8,128)(4,1)S(1)}, u32[]{:S(2)}) copy-start(pred[16,16]{1,0:T(8,128)(4,1)S(1)} %get-tuple-element.478) | copy-start | bytes 772
  107.0 23.1 %copy-start.90 = (pred[16,16]{1,0:T(8,128)(4,1)}, pred[16,16]{1,0:T(8,128)(4,1)S(1)}, u32[]{:S(2)}) copy-start(pred[16,16]{1,0:T(8,128)(4,1)S(1)} %get-tuple-element.479) | copy-start | bytes 772
  121.1 25.3 %all-to-all-start.2 = ((f32[24,16,1,512]{3,0,2,1:T(8,128)}), f32[24,16,1,512]{3,0,2,1:T(8,128)S(1)}, u32[]{:S(2)}, u32[]{:S(2)}) async-start(f32[24,16,1,512]{3,0,2,1:T(8,128)} %copy.184), calls=%async_computation.2 | async-start | bytes 1572864 | tf_op jit(solution)/shard_map/all_to_all | solution.py:220
  126.0 82.5 %all-reduce.15.cloned.1.call-start = ((), (), s32[]{:S(2)}) async-start(), calls=%async_computation.9 | async-start | bytes 6291456 | tf_op jit(solution)/shard_map/psum | solution.py:233
  127.0 17.4 %copy-start.44 = (f32[2,256,256]{2,1,0:T(8,128)}, f32[2,256,256]{2,1,0:T(8,128)S(1)}, u32[]{:S(2)}) copy-start(f32[2,256,256]{2,1,0:T(8,128)S(1)} %fusion.177) | copy-start | bytes 1572868
  165.5 9.8 copy-start.81
  165.6 11.5 %copy-start.57 = (f32[1536]{0:T(1024)S(1)}, f32[1536]{0:T(1024)}, u32[]{:S(2)}) copy-start(f32[1536]{0:T(1024)} %param.30) | copy-start | bytes 18436
  204.3 9.5 copy-start.92
  234.3 41.2 %all-to-all-start.3 = ((f32[24,1,16,512]{3,0,1,2:T(8,128)}), f32[24,1,16,512]{3,0,1,2:T(8,128)}, u32[]{:S(2)}, u32[]{:S(2)}) async-start(f32[24,1,16,512]{3,0,1,2:T(8,128)} %copy.190), calls=%async_computation.3 | async-start | bytes 1572864 | tf_op jit(solution)/shard_map/all_to_all | solution.py:255
  241.6 21.2 %copy-start.4 = (f32[512,1536]{0,1:T(8,128)S(1)}, f32[512,1536]{0,1:T(8,128)}, u32[]{:S(2)}) copy-start(f32[512,1536]{0,1:T(8,128)} %copy.189) | copy-start | bytes 9437188
  241.6 21.2 %copy-start.14 = (f32[512,24,64]{0,2,1:T(8,128)S(1)}, f32[512,24,64]{0,2,1:T(8,128)}, u32[]{:S(2)}) copy-start(f32[512,24,64]{0,2,1:T(8,128)} %copy-done.13) | copy-start | bytes 9437188
  262.8 9.5 copy-start.30
  264.5 11.0 %copy-start.98 = (f32[2,24]{1,0:T(2,128)}, f32[2,24]{1,0:T(2,128)S(1)}, u32[]{:S(2)}) copy-start(f32[2,24]{1,0:T(2,128)S(1)} %fusion.150) | copy-start | bytes 580
  279.3 26.6 %all-to-all-start.4 = ((f32[24,16,1,512]{3,0,2,1:T(8,128)}), f32[24,16,1,512]{3,0,2,1:T(8,128)S(1)}, u32[]{:S(2)}, u32[]{:S(2)}) async-start(f32[24,16,1,512]{3,0,2,1:T(8,128)} %copy.193), calls=%async_computation.4 | async-start | bytes 1572864 | tf_op jit(solution)/shard_map/all_to_all | solution.py:258
  286.3 108.4 %reduce-scatter.7.cloned.1.call-start = ((), (), s32[]{:S(2)}) async-start(), calls=%async_computation.10 | async-start | bytes 786432 | tf_op jit(solution)/shard_map/reduce_scatter | solution.py:274
  320.9 9.5 copy-start.31
  331.6 12.9 %copy-start.99 = (f32[2,24]{1,0:T(2,128)S(1)}, f32[2,24]{1,0:T(2,128)}, u32[]{:S(2)}) copy-start(f32[2,24]{1,0:T(2,128)} %copy-done.98) | copy-start | bytes 580
  331.6 12.9 %copy-start.103 = (f32[2,24]{1,0:T(2,128)S(1)}, f32[2,24]{1,0:T(2,128)}, u32[]{:S(2)}) copy-start(f32[2,24]{1,0:T(2,128)} %reduce_window_sum.25) | copy-start | bytes 580
  331.6 12.9 %copy-start.117 = (f32[2,24]{1,0:T(2,128)S(1)}, f32[2,24]{1,0:T(2,128)}, u32[]{:S(2)}) copy-start(f32[2,24]{1,0:T(2,128)} %get-tuple-element.247) | copy-start | bytes 580
  331.6 13.0 %copy-start.53 = (f32[512,24]{0,1:T(8,128)S(1)}, f32[512,24]{0,1:T(8,128)}, u32[]{:S(2)}) copy-start(f32[512,24]{0,1:T(8,128)} %copy-done.52) | copy-start | bytes 147460
  331.6 13.0 %copy-start.54 = (f32[2,256,24]{1,2,0:T(8,128)S(1)}, f32[2,256,24]{1,2,0:T(8,128)}, u32[]{:S(2)}) copy-start(f32[2,256,24]{1,2,0:T(8,128)} %multiply_reduce_fusion.7) | copy-start | bytes 147460
  331.6 13.0 %copy-start.71 = (f32[2,256,24]{1,2,0:T(8,128)S(1)}, f32[2,256,24]{1,2,0:T(8,128)}, u32[]{:S(2)}) copy-start(f32[2,256,24]{1,2,0:T(8,128)} %get-tuple-element.355) | copy-start | bytes 147460
  331.6 13.0 %copy-start.72 = (f32[2,256,24]{1,2,0:T(8,128)S(1)}, f32[2,256,24]{1,2,0:T(8,128)}, u32[]{:S(2)}) copy-start(f32[2,256,24]{1,2,0:T(8,128)} %get-tuple-element.356) | copy-start | bytes 147460
  331.6 13.0 %copy-start.95 = (f32[2,24]{1,0:T(2,128)S(1)}, f32[2,24]{1,0:T(2,128)}, u32[]{:S(2)}) copy-start(f32[2,24]{1,0:T(2,128)} %copy-done.93) | copy-start | bytes 580
  381.7 151.2 %reduce-scatter.13.cloned.1.call-start = ((), (), s32[]{:S(2)}) async-start(), calls=%async_computation.14 | async-start | bytes 1671168
  385.3 6.0 collective-permute-start.2
  396.7 6.1 collective-permute-start.3
  404.9 153.1 %all-reduce.17.cloned.1.call-start = ((), (), s32[]{:S(2)}) async-start(), calls=%async_computation.11 | async-start | bytes 6291456 | tf_op jit(solution)/shard_map/psum | solution.py:310
  417.1 435.1 %reduce-scatter.9.cloned.1.call-start = ((), (), s32[]{:S(2)}) async-start(), calls=%async_computation.12 | async-start | bytes 20054016 | tf_op jit(solution)/shard_map/reduce_scatter | solution.py:327
  436.9 591.8 %reduce-scatter.11.cloned.1.call-start = ((), (), s32[]{:S(2)}) async-start(), calls=%async_computation.13 | async-start | bytes 10027008 | tf_op jit(solution)/shard_map/reduce_scatter | solution.py:329
  446.6 111.4 %copy-start.87 = (f32[512]{0:T(512)S(1)}, f32[512]{0:T(512)}, u32[]{:S(2)}) copy-start(f32[512]{0:T(512)} %copy-done.85) | copy-start | bytes 6148
  446.6 114.1 %copy-start.101 = (f32[1536]{0:T(1024)S(1)}, f32[1536]{0:T(1024)}, u32[]{:S(2)}) copy-start(f32[1536]{0:T(1024)} %get-tuple-element.426) | copy-start | bytes 18436
  (90 other events, 404.5 us)
Sparse Core Ops, SparseCore 0:
  183.9 24.5 all-reduce.14
  381.8 7.2 reduce-scatter.6
  405.0 127.8 reduce-scatter.12
  535.6 22.2 all-reduce.16
  563.6 288.5 reduce-scatter.8
  858.3 170.4 reduce-scatter.10
where the time goes:
time: 1040 us
  waiting for transfers between devices  508 us (49%)
  matrix products  165 us (16%)
  local copies, waits for them, and re-layouts  132 us (13%)
  blocking collectives  85.9 us (8%)
  other arithmetic  83.6 us (8%)
  starting transfers between devices  44.4 us (4%)
  between operations  15.9 us (2%)
    reduce_scatter x1, waiting for transfers between devices, body(): lax.psum_scatter(term_inner, 'seq', scatter_dimension=0, tiled=True)  202 us
    reduce_scatter x1, waiting for transfers between devices, body(): lax.psum_scatter(term_out, 'seq', scatter_dimension=0, tiled=True)  173 us
    unnamed x7, waiting for transfers between devices  85.3 us
    psum x1, blocking collectives, body(): lax.psum((term_conv_values, term_conv_shared, head_terms, term_gate, term...  83.5 us
    dot_general x3, matrix products, ssd_parts(): jnp.einsum('cijh,cjhp->cihp', scores[:, :, :, None] * decay_mat, weighted...  48 us
    psum x1, waiting for transfers between devices, body(): grad_normed = lax.psum(partial_normed, 'head')  22 us
    unnamed x245, local copies, waits for them, and re-layouts  21.1 us
  transfers between devices with their start and end apart: 15, of which 8 were waited for; matrix products, arithmetic and copies ran while one was open for 22% of the time, Pallas kernels for 0%

commit v1 on v0

v1 whole, which is shorter than its diff:
```python
import functools

import jax
import jax.numpy as jnp
from jax import lax
from jax.experimental import pallas as pl
from jax.experimental.pallas import tpu as pltpu
from jax.sharding import PartitionSpec as P

HEAD_DIM = 64
STATE = 128
CONV = 4
INNER = 3072
CHUNK = 128
LANES = 128
BLOCK = 256
HALO = 16
BLOCK_HEADS = BLOCK // HEAD_DIM

norm_eps = 1e-05
highest = lax.Precision.HIGHEST
f32 = jnp.float32
bf16 = jnp.bfloat16
NN = (((1,), (0,)), ((), ()))
NT = (((1,), (1,)), ((), ()))
TN = (((0,), (0,)), ((), ()))


def flip(shard, bit):
    size = lax.axis_size("seq")
    return lax.ppermute(shard, "seq", [(i, i ^ (1 << bit)) for i in range(size)])


def swap(shard):
    return lax.ppermute(shard, "head", [(0, 1), (1, 0)])


def from_behind(shard, by):
    size = lax.axis_size("seq")
    pairs = [(i, i + by) for i in range(size) if 0 <= i + by < size]
    return lax.ppermute(shard, "seq", pairs)


def silu_grad(values):
    sigmoid = 1.0 / (1.0 + jnp.exp(-values))
    return sigmoid * (1.0 + values * (1.0 - sigmoid))


def silu(values):
    return values / (1.0 + jnp.exp(-values))


def mm(a, b, dims=NN):
    return lax.dot_general(a, b, dims, preferred_element_type=f32)


def parts(a):
    high = a.astype(bf16)
    return high, (a - high.astype(f32)).astype(bf16)


def mm_left(a, b, dims=NN):
    high, low = parts(a)
    return mm(high, b, dims) + mm(low, b, dims)


def mm_right(a, b, dims=NN):
    high, low = parts(b)
    return mm(a, high, dims) + mm(a, low, dims)


def mm_both(a, b, dims=NN):
    a_high, a_low = parts(a)
    b_high, b_low = parts(b)
    return mm(a_high, b_high, dims) + mm(a_low, b_high, dims) + mm(a_high, b_low, dims)


def mm_exact(a, b, dims=NN):
    return lax.dot_general(a, b, dims, precision=highest, preferred_element_type=f32)


def widen(cols):
    rows = cols.shape[0]
    lane = lax.broadcasted_iota(jnp.int32, (rows, LANES), 1)
    pieces = []
    for pair in range(BLOCK // LANES):
        first = jnp.broadcast_to(cols[:, 2 * pair : 2 * pair + 1], (rows, LANES))
        second = jnp.broadcast_to(cols[:, 2 * pair + 1 : 2 * pair + 2], (rows, LANES))
        pieces.append(jnp.where(lane < HEAD_DIM, first, second))
    return jnp.concatenate(pieces, axis=1)


def rolled(full, step):
    shift = lax.rem(LANES - BLOCK_HEADS * step, LANES)
    return pltpu.roll(full, shift, 1)


def causal():
    rows = lax.broadcasted_iota(jnp.int32, (CHUNK, CHUNK), 0)
    cols = lax.broadcasted_iota(jnp.int32, (CHUNK, CHUNK), 1)
    return rows >= cols


def conv_rows(ext, taps, first, rows):
    out = taps[CONV : CONV + 1, :]
    for k in range(CONV):
        out = out + taps[k : k + 1, :] * ext[first + k : first + k + rows, :]
    return out


def stack_pair(block):
    lane = lax.broadcasted_iota(jnp.int32, block.shape, 1)
    low = jnp.where(lane < HEAD_DIM, block, jnp.zeros_like(block))
    return low, block - low


def front_kernel(
    hid_ref,
    halo_ref,
    gain_ref,
    wg_ref,
    wv_ref,
    wstep_ref,
    wshared_ref,
    cv_ref,
    cs_ref,
    bias_ref,
    decay_ref,
    skip_ref,
    normed_ref,
    scale_ref,
    gate_ref,
    vext_ref,
    yloc_ref,
    after_ref,
    step_ref,
    slope_ref,
    run_ref,
    runt_ref,
    stept_ref,
    sext_ref,
    bc_ref,
    nx,
    scores,
    bt,
    end_w,
    vwide,
):
    j = pl.program_id(0)
    tokens = hid_ref.shape[0]
    chunks = tokens // CHUNK

    @pl.when(j == 0)
    def _():
        def norm_rows(rows):
            wide = rows.astype(f32)
            scale = lax.rsqrt(jnp.mean(wide * wide, axis=1, keepdims=True) + norm_eps)
            return (wide * scale * gain_ref[...]).astype(bf16), scale

        nx[0:HALO, :] = norm_rows(halo_ref[...])[0]

        @pl.loop(0, tokens // 64)
        def _(i):
            start = pl.multiple_of(i * 64, 64)
            rows, scale = norm_rows(hid_ref[pl.ds(start, 64), :])
            nx[pl.ds(pl.multiple_of(HALO + start, HALO), 64), :] = rows
            normed_ref[pl.ds(start, 64), :] = rows
            scale_ref[pl.ds(start, 64), :] = jnp.broadcast_to(scale, (64, LANES))

        shared = mm(nx[...], wshared_ref[...]).astype(bf16)
        sext_ref[0] = shared[:, :STATE]
        sext_ref[1] = shared[:, STATE:]
        conv = conv_rows(shared.astype(f32), cs_ref[...], HALO - CONV + 1, tokens)
        act = silu(conv).astype(bf16)
        bc_ref[...] = act
        raw = mm(nx[HALO:, :], wstep_ref[...]) + bias_ref[...]
        small = jnp.exp(-jnp.abs(raw))
        step = jnp.maximum(raw, 0.0) + jnp.log1p(small)
        step_ref[...] = step
        slope_ref[...] = 1.0 / (1.0 + jnp.exp(-raw))
        rate = -step * jnp.exp(decay_ref[...])
        tri = causal().astype(f32)
        for c in range(chunks):
            rows = slice(c * CHUNK, (c + 1) * CHUNK)
            run = mm_exact(tri, rate[rows, :])
            run_ref[rows, :] = run
            run_t = run.T
            step_t = step[rows, :].T
            for b in range(runt_ref.shape[0]):
                heads = slice(BLOCK_HEADS * b, BLOCK_HEADS * (b + 1))
                runt_ref[b, 0:BLOCK_HEADS, rows] = run_t[heads, :]
                stept_ref[b, 0:BLOCK_HEADS, rows] = step_t[heads, :]
            end_w[rows, :] = step[rows, :] * jnp.exp(run[CHUNK - 1 :, :] - run)
            b_rows = act[rows, :STATE]
            c_rows = act[rows, STATE:]
            scores[c] = mm(c_rows, b_rows, NT)
            bt[:, rows] = b_rows.astype(f32).T.astype(bf16)

    gate_ref[...] = mm(nx[HALO:, :], wg_ref[0])
    values = mm(nx[...], wv_ref[0]).astype(bf16)
    vext_ref[...] = values
    vwide[...] = values.astype(f32)
    conv = conv_rows(vwide, cv_ref[...], HALO - CONV + 1, tokens)
    act = silu(conv).astype(bf16)
    run_cols = rolled(run_ref[...], j)
    end_cols = rolled(end_w[...], j)
    mask = causal()
    skip = widen(rolled(skip_ref[...], j)[:, :BLOCK_HEADS])
    state = jnp.zeros((STATE, BLOCK), f32)
    for c in range(chunks):
        rows = slice(c * CHUNK, (c + 1) * CHUNK)
        cols = run_cols[rows, :BLOCK_HEADS]
        x = act[rows, :]
        y_pairs = []
        for pair in range(BLOCK // LANES):
            mats = []
            for k in range(2):
                head = 2 * pair + k
                gap = cols[:, head : head + 1] - runt_ref[j, head : head + 1, rows]
                keep = jnp.exp(jnp.where(mask, gap, -1e30))
                mats.append(scores[c] * keep * stept_ref[j, head : head + 1, rows])
            low, high = stack_pair(x[:, pair * LANES : (pair + 1) * LANES])
            y_pairs.append(
                mm_left(jnp.concatenate(mats, axis=1), jnp.concatenate([low, high], axis=0))
            )
        wide_x = x.astype(f32)
        y = jnp.concatenate(y_pairs, axis=1) + skip * wide_x
        if c:
            y = y + widen(jnp.exp(cols)) * mm_right(bc_ref[rows, STATE:], state)
        yloc_ref[rows, :] = y
        weighted = wide_x * widen(end_cols[rows, :BLOCK_HEADS])
        last = widen(jnp.exp(cols[CHUNK - 1 :, :]))
        state = last * state + mm_right(bt[:, rows], weighted)
        after_ref[c] = state


def front_call(hid, halo, gain, both, wstep, wshared, conv_values, conv_shared, bias, decay, skip):
    tokens, width = hid.shape
    inner = both.shape[2]
    chunks = tokens // CHUNK
    full = lambda shape: pl.BlockSpec(shape, lambda j: (0,) * len(shape))
    block = lambda rows: pl.BlockSpec((rows, BLOCK), lambda j: (0, j))
    shapes = [
        ((tokens, width), bf16, full((tokens, width))),
        ((tokens, LANES), f32, full((tokens, LANES))),
        ((tokens, inner), f32, block(tokens)),
        ((HALO + tokens, inner), bf16, block(HALO + tokens)),
        ((tokens, inner), f32, block(tokens)),
        ((chunks, STATE, inner), f32, pl.BlockSpec((chunks, STATE, BLOCK), lambda j: (0, 0, j))),
        ((tokens, LANES), f32, full((tokens, LANES))),
        ((tokens, LANES), f32, full((tokens, LANES))),
        ((tokens, LANES), f32, full((tokens, LANES))),
        ((inner // BLOCK, 8, tokens), f32, full((inner // BLOCK, 8, tokens))),
        ((inner // BLOCK, 8, tokens), f32, full((inner // BLOCK, 8, tokens))),
        ((2, HALO + tokens, STATE), bf16, full((2, HALO + tokens, STATE))),
        ((tokens, 2 * STATE), bf16, full((tokens, 2 * STATE))),
    ]
    return pl.pallas_call(
        front_kernel,
        grid=(inner // BLOCK,),
        in_specs=[
            full((tokens, width)),
            full((HALO, width)),
            full((1, width)),
            pl.BlockSpec((1, width, BLOCK), lambda j: (0, 0, j)),
            pl.BlockSpec((1, width, BLOCK), lambda j: (1, 0, j)),
            full((width, LANES)),
            full((width, 2 * STATE)),
            block(CONV + 1),
            full((CONV + 1, 2 * STATE)),
            full((1, LANES)),
            full((1, LANES)),
            full((1, LANES)),
        ],
        out_shape=[jax.ShapeDtypeStruct(s, d) for s, d, _ in shapes],
        out_specs=[spec for _, _, spec in shapes],
        scratch_shapes=[
            pltpu.VMEM((HALO + tokens, width), bf16),
            pltpu.VMEM((chunks, CHUNK, CHUNK), f32),
            pltpu.VMEM((STATE, tokens), bf16),
            pltpu.VMEM((tokens, LANES), f32),
            pltpu.VMEM((HALO + tokens, BLOCK), f32),
        ],
        name="front",
    )(hid, halo, gain, both, both, wstep, wshared, conv_values, conv_shared, bias, decay, skip)


def offsets_of(run_ref, chunks):
    rows = [jnp.zeros((1, LANES), f32)]
    for c in range(chunks):
        rows.append(rows[-1] + run_ref[(c + 1) * CHUNK - 1 : (c + 1) * CHUNK, :])
    return rows


def mix_kernel(
    yloc_ref, gate_ref, in_ref, run_ref, bc_ref, gain_ref, wout_ref, y_ref, gw_ref, mix_ref, sq_ref
):
    j = pl.program_id(0)
    tokens = yloc_ref.shape[0]
    chunks = tokens // CHUNK
    offsets = offsets_of(run_ref, chunks)
    gated = []
    for c in range(chunks):
        rows = slice(c * CHUNK, (c + 1) * CHUNK)
        grow = rolled(jnp.exp(run_ref[rows, :] + offsets[c]), j)[:, :BLOCK_HEADS]
        y = yloc_ref[rows, :] + widen(grow) * mm_right(bc_ref[rows, STATE:], in_ref[...])
        y_ref[rows, :] = y
        out = y * silu(gate_ref[rows, :])
        gw_ref[rows, :] = (out * gain_ref[...]).astype(bf16)
        gated.append(jnp.broadcast_to(jnp.sum(out * out, axis=1, keepdims=True), (CHUNK, LANES)))
    part = mm(gw_ref[...], wout_ref[...], NT)
    squares = jnp.concatenate(gated, axis=0)

    @pl.when(j == 0)
    def _():
        mix_ref[...] = part
        sq_ref[...] = squares

    @pl.when(j > 0)
    def _():
        mix_ref[...] += part
        sq_ref[...] += squares


def mix_call(yloc, gate, state_in, run, bc, gain, wout):
    tokens, inner = yloc.shape
    width = wout.shape[0]
    full = lambda shape: pl.BlockSpec(shape, lambda j: (0,) * len(shape))
    block = lambda rows: pl.BlockSpec((rows, BLOCK), lambda j: (0, j))
    return pl.pallas_call(
        mix_kernel,
        grid=(inner // BLOCK,),
        in_specs=[
            block(tokens),
            block(tokens),
            block(STATE),
            full((tokens, LANES)),
            full((tokens, 2 * STATE)),
            block(1),
            block(width),
        ],
        out_shape=[
            jax.ShapeDtypeStruct((tokens, inner), f32),
            jax.ShapeDtypeStruct((tokens, inner), bf16),
            jax.ShapeDtypeStruct((tokens, width), f32),
            jax.ShapeDtypeStruct((tokens, LANES), f32),
        ],
        out_specs=[block(tokens), block(tokens), full((tokens, width)), full((tokens, LANES))],
        name="mix",
    )(yloc, gate, state_in, run, bc, gain, wout)


def gate_kernel(
    gm_ref, wout_ref, y_ref, gate_ref, gain_ref, coef_ref, run_ref, bc_ref,
    ggate_ref, dy_ref, term_ref, own_ref, ct,
):
    j = pl.program_id(0)
    tokens = y_ref.shape[0]
    chunks = tokens // CHUNK
    offsets = offsets_of(run_ref, chunks)

    @pl.when(j == 0)
    def _():
        for c in range(chunks):
            rows = slice(c * CHUNK, (c + 1) * CHUNK)
            ct[:, rows] = bc_ref[rows, STATE:].astype(f32).T.astype(bf16)

    own = jnp.zeros((STATE, BLOCK), f32)
    term = jnp.zeros((1, BLOCK), f32)
    for c in range(chunks):
        rows = slice(c * CHUNK, (c + 1) * CHUNK)
        ggw = mm(gm_ref[rows, :], wout_ref[...])
        y = y_ref[rows, :]
        gate = gate_ref[rows, :]
        sig = 1.0 / (1.0 + jnp.exp(-gate))
        act = gate * sig
        out = y * act
        term = term + jnp.sum(ggw * out, axis=0, keepdims=True)
        coef = jnp.concatenate([coef_ref[rows, :]] * (BLOCK // LANES), axis=1)
        gg = ggw * gain_ref[...] - coef * out
        dy = gg * act
        dy_ref[rows, :] = dy
        ggate_ref[0, rows, :] = (gg * y * (sig * (1.0 + gate * (1.0 - sig)))).astype(bf16)
        grow = rolled(jnp.exp(run_ref[rows, :] + offsets[c]), j)[:, :BLOCK_HEADS]
        own = own + mm_right(ct[:, rows], dy * widen(grow))
    own_ref[...] = own
    term_ref[...] = term


def gate_call(gm, wout, y, gate, gain, coef, run, bc):
    tokens, inner = y.shape
    width = wout.shape[0]
    full = lambda shape: pl.BlockSpec(shape, lambda j: (0,) * len(shape))
    block = lambda rows: pl.BlockSpec((rows, BLOCK), lambda j: (0, j))
    return pl.pallas_call(
        gate_kernel,
        grid=(inner // BLOCK,),
        in_specs=[
            full((tokens, width)),
            block(width),
            block(tokens),
            block(tokens),
            block(1),
            full((tokens, LANES)),
            full((tokens, LANES)),
            full((tokens, 2 * STATE)),
        ],
        out_shape=[
            jax.ShapeDtypeStruct((inner // BLOCK, tokens, BLOCK), bf16),
            jax.ShapeDtypeStruct((tokens, inner), f32),
            jax.ShapeDtypeStruct((1, inner), f32),
            jax.ShapeDtypeStruct((STATE, inner), f32),
        ],
        out_specs=[
            pl.BlockSpec((1, tokens, BLOCK), lambda j: (j, 0, 0)),
            block(tokens),
            block(1),
            block(STATE),
        ],
        scratch_shapes=[pltpu.VMEM((STATE, tokens), bf16)],
        name="gate_back",
    )(gm, wout, y, gate, gain, coef, run, bc)


def order_bits(part, bits):
    order = list(range(bits))
    if part == 1 and bits > 1:
        order[0], order[1] = 1, 0
    return order


def slot_of(owner, part, bits):
    slot = 0
    for bit in order_bits(part, bits):
        slot = slot * 2 + ((owner >> bit) & 1)
    return slot


class Reduction:
    def __init__(self, held, landing, out, part, bits, index, send_sems, recv_sems, cols):
        self.held, self.landing, self.out = held, landing, out
        self.part, self.bits, self.index = part, bits, index
        self.send_sems, self.recv_sems, self.cols = send_sems, recv_sems, cols

    def place(self, stage):
        base = 0
        size = 1 << self.bits
        for s, bit in enumerate(order_bits(self.part, self.bits)[: stage + 1]):
            mine = (self.index // (1 << bit)) % 2
            half = size >> (s + 1)
            keep, give = base + mine * half, base + (1 - mine) * half
            base = keep
        return keep, give, half, order_bits(self.part, self.bits)[stage]

    def copy(self, stage):
        _, give, half, bit = self.place(stage)
        mine = (self.index // (1 << bit)) % 2
        partner = self.index + (1 - 2 * mine) * (1 << bit)
        return pltpu.make_async_remote_copy(
            src_ref=self.held.at[pl.ds(give, half)],
            dst_ref=self.landing[stage],
            send_sem=self.send_sems.at[stage],
            recv_sem=self.recv_sems.at[stage],
            device_id={"seq": partner},
            device_id_type=pl.DeviceIdType.MESH,
        )

    def start(self, stage):
        self.copy(stage).start()

    def finish(self, stage):
        self.copy(stage).wait()
        keep, _, half, _ = self.place(stage)
        if stage == self.bits - 1:
            self.out[:, self.cols] = self.held[keep].astype(f32) + self.landing[stage][0].astype(f32)
        else:

            @pl.loop(0, half)
            def _(i):
                total = self.held[keep + i].astype(f32) + self.landing[stage][i].astype(f32)
                self.held[keep + i] = total.astype(bf16)

    def advance(self, stage):
        self.finish(stage)
        if stage + 1 < self.bits:
            self.start(stage + 1)


def exchange_sum(acc, landing, bit, index, send_sem, recv_sem):
    mine = (index // (1 << bit)) % 2
    partner = index + (1 - 2 * mine) * (1 << bit)
    copy = pltpu.make_async_remote_copy(
        src_ref=acc.at[bit],
        dst_ref=landing.at[bit],
        send_sem=send_sem.at[bit],
        recv_sem=recv_sem.at[bit],
        device_id={"seq": partner},
        device_id_type=pl.DeviceIdType.MESH,
    )
    copy.start()
    copy.wait()
    acc[bit + 1] = acc[bit] + landing[bit]


def back_kernel(
    bits,
    gmt_ref, normedt_ref, ggate_ref, run_ref, step_ref, slope_ref, bc_ref, sext_ref, skip_ref,
    decay_ref, cs_ref, wsmall_ref, gain_ref, tgate_ref,
    gw_ref, vext_ref, dy_ref, after_ref, in_ref, dstate_ref, cv_ref, runt_ref, stept_ref,
    wi_ref,
    hid_ref, cot_ref, scale_ref,
    gout_ref, ggw_ref, gvw_ref, gsmall_ref, ghid_ref, sums_ref, heads_ref,
    w_out, w_gate, w_values, w_small,
    land_out, land_gate, land_values, land_small,
    rs_send, rs_recv,
    gv, acc, acc_send, acc_land, acc_sems,
    edge_own, edge_tail, edge_land, edge_sems,
    dbc, dbc_land, dbc_sems, small, sedge_own, sedge_land, sedge_sems,
    vec, vec_land, vec_sems, norm_vec, norm_land, norm_sems, hvec, hvec_land, hvec_sems,
    scores, scorest, ct, dscores, end_w, ends, dcols, xdu, dyc, xdus, vwide, gext,
):
    step_id = pl.program_id(0)
    index = lax.axis_index("seq")
    core = lax.axis_index("head")
    size = 1 << bits
    tokens = dy_ref.shape[0]
    chunks = tokens // CHUNK
    nb = w_out.shape[0] * w_out.shape[3] // BLOCK
    half_nb = nb // 2
    width = normedt_ref.shape[0]
    rows_own = width // size
    part_cols = w_out.shape[3]
    t_out, t_gate, t_scan, t_values, t_grad, t_final = 0, nb, 2 * nb, 3 * nb, 4 * nb, 5 * nb
    after_id = lax.rem(index + 1, size)
    before_id = lax.rem(index + size - 1, size)

    def reduction(g, part):
        held, landing, out = (
            (w_out, land_out, gout_ref), (w_gate, land_gate, ggw_ref), (w_values, land_values, gvw_ref),
        )[g]
        land = [ref.at[part] for ref in landing]
        slot = 2 * g + part
        return Reduction(
            held.at[part], land, out, part, bits, index, rs_send.at[slot], rs_recv.at[slot],
            pl.ds(part * part_cols, part_cols),
        )

    rs = [[reduction(g, part) for part in range(2)] for g in range(3)]
    rs_small = Reduction(
        w_small, list(land_small), gsmall_ref, 1, bits, index, rs_send.at[6], rs_recv.at[6],
        pl.ds(0, w_small.shape[2]),
    )

    def when_after(step):
        return pl.when(step_id == step)

    def send_to(src, dst, send_sem, recv_sem, **where):
        return pltpu.make_async_remote_copy(
            src_ref=src, dst_ref=dst, send_sem=send_sem, recv_sem=recv_sem, device_id=where,
            device_id_type=pl.DeviceIdType.MESH,
        )

    @pl.when(step_id == 0)
    def _():
        barrier = pltpu.get_barrier_semaphore()
        for bit in range(bits):
            mine = (index // (1 << bit)) % 2
            pl.semaphore_signal(
                barrier, inc=1, device_id={"seq": index + (1 - 2 * mine) * (1 << bit)},
                device_id_type=pl.DeviceIdType.MESH,
            )
        for other in (after_id, before_id):
            pl.semaphore_signal(
                barrier, inc=1, device_id={"seq": other}, device_id_type=pl.DeviceIdType.MESH
            )
        pl.semaphore_signal(
            barrier, inc=1, device_id={"head": 1 - core}, device_id_type=pl.DeviceIdType.MESH
        )
        pl.semaphore_wait(barrier, bits + 3)

    def put_block(held, left, right, j):
        part = j // half_nb
        cols = pl.ds(pl.multiple_of((j % half_nb) * BLOCK, BLOCK), BLOCK)
        group = width // 4
        for q in range(4):
            piece = mm(left[q * group : (q + 1) * group, :], right).astype(bf16)
            for b in range(size // 4):
                owner = q * (size // 4) + b
                slots = [slot_of(owner, p, bits) for p in range(2)]
                slot = slots[0] + part * (slots[1] - slots[0])
                held[part, slot, :, cols] = piece[b * rows_own : (b + 1) * rows_own, :]

    @pl.when(step_id < t_gate)
    def _():
        put_block(w_out, gmt_ref, gw_ref[...], step_id)

    @pl.when((step_id >= t_gate) & (step_id < t_scan))
    def _():
        j = step_id - t_gate
        put_block(w_gate, normedt_ref, ggate_ref[j], j)

    @when_after(half_nb - 1)
    def _():
        rs[0][0].start(0)

    @when_after(t_gate - 1)
    def _():
        rs[0][1].start(0)

    @when_after(t_gate + half_nb - 1)
    def _():
        rs[1][0].start(0)

    @when_after(t_scan - 1)
    def _():
        rs[1][1].start(0)

    mask = causal()
    rows_i = lax.broadcasted_iota(jnp.int32, (CHUNK, CHUNK), 0)
    cols_i = lax.broadcasted_iota(jnp.int32, (CHUNK, CHUNK), 1)
    mask_t = rows_i <= cols_i

    @pl.when(step_id == t_scan)
    def _():
        dbc[...] = jnp.zeros_like(dbc)
        dscores[...] = jnp.zeros_like(dscores)
        dcols[...] = jnp.zeros_like(dcols)
        xdu[...] = jnp.zeros_like(xdu)
        dyc[...] = jnp.zeros_like(dyc)
        xdus[...] = jnp.zeros_like(xdus)
        ends[...] = jnp.zeros_like(ends)
        vec[...] = jnp.zeros_like(vec)
        for c in range(chunks):
            rows = slice(c * CHUNK, (c + 1) * CHUNK)
            b_rows = bc_ref[rows, :STATE]
            c_rows = bc_ref[rows, STATE:]
            scores[c] = mm(c_rows, b_rows, NT)
            scorest[c] = mm(b_rows, c_rows, NT)
            ct[:, rows] = c_rows.astype(f32).T.astype(bf16)
            run = run_ref[rows, :]
            end_w[rows, :] = jnp.exp(run[CHUNK - 1 :, :] - run)

    @pl.when((step_id >= t_scan) & (step_id < t_values))
    def _():
        j = step_id - t_scan
        offsets = offsets_of(run_ref, chunks)
        vwide[...] = vext_ref[...].astype(f32)
        conv = conv_rows(vwide, cv_ref[...], HALO - CONV + 1, tokens)
        sig_all = 1.0 / (1.0 + jnp.exp(-conv))
        act = (conv * sig_all).astype(bf16)
        slope = sig_all * (1.0 + conv * (1.0 - sig_all))
        run_cols = rolled(run_ref[...], j)
        step_cols = rolled(step_ref[...], j)
        end_cols = rolled(end_w[...], j)
        skip = widen(rolled(skip_ref[...], j)[:, :BLOCK_HEADS])
        channel = lax.broadcasted_iota(jnp.int32, (BLOCK, LANES), 0) // HEAD_DIM
        lane = lax.broadcasted_iota(jnp.int32, (BLOCK, LANES), 1)
        pick = (lane == BLOCK_HEADS * j + channel).astype(bf16)
        lane_row = lax.broadcasted_iota(jnp.int32, (CHUNK, LANES), 1)
        dstate = dstate_ref[...]
        dskip = jnp.zeros((1, BLOCK), f32)
        gext[tokens : tokens + 8, :] = jnp.zeros((8, BLOCK), f32)
        for c in reversed(range(chunks)):
            rows = slice(c * CHUNK, (c + 1) * CHUNK)
            cols = run_cols[rows, :BLOCK_HEADS]
            x = act[rows, :]
            wide_x = x.astype(f32)
            dy = dy_ref[rows, :]
            b_rows = bc_ref[rows, :STATE]
            c_rows = bc_ref[rows, STATE:]
            grow = widen(jnp.exp(cols))
            tail = widen(end_cols[rows, :BLOCK_HEADS])
            step_w = widen(step_cols[rows, :BLOCK_HEADS])
            last = grow[CHUNK - 1 :, :]
            base = rolled(jnp.exp(offsets[c]), j)[:, :BLOCK_HEADS]
            enter = widen(base) * in_ref[...]
            if c:
                enter = enter + after_ref[c - 1]
            du_state = tail * mm_right(b_rows, dstate)
            carried = grow * mm_right(c_rows, enter)
            weighted = wide_x * (tail * step_w)
            grown = dy * grow
            dbc[0, rows, :] += mm_both(weighted, dstate, NT)
            dbc[1, rows, :] += mm_both(grown, enter, NT)
            hold = last * jnp.sum(dstate * enter, axis=0, keepdims=True)
            ends[c : c + 1, :] += mm_exact(
                jnp.broadcast_to(hold, (8, BLOCK)), pick.astype(f32)
            )[:1, :]
            dstate = last * dstate + mm_right(ct[:, rows], grown)
            du_pairs = []
            col_sum = jnp.zeros((CHUNK, LANES), f32)
            for pair in range(BLOCK // LANES):
                lanes = slice(pair * LANES, (pair + 1) * LANES)
                low, high = stack_pair(dy[:, lanes])
                both = jnp.concatenate([low, high], axis=0)
                dmat = mm_left(both, x[:, lanes], NT)
                mats = []
                for k in range(2):
                    head = 2 * pair + k
                    col = cols[:, head : head + 1]
                    row = runt_ref[0, head : head + 1, rows]
                    keep = jnp.exp(jnp.where(mask, col - row, -1e30))
                    piece = dmat[k * CHUNK : (k + 1) * CHUNK, :] * keep
                    piece = piece * stept_ref[0, head : head + 1, rows]
                    dscores[c] += piece
                    full = piece * scores[c]
                    col_sum = jnp.where(
                        lane_row == BLOCK_HEADS * j + head,
                        jnp.sum(full, axis=1, keepdims=True),
                        col_sum,
                    )
                    dcols[j, head : head + 1, rows] = jnp.sum(full, axis=0, keepdims=True)
                    keep_t = jnp.exp(jnp.where(mask_t, row - col, -1e30))
                    mats.append(scorest[c] * keep_t)
                du_pairs.append(mm_both(jnp.concatenate(mats, axis=1), both))
            dyc[rows, :] += col_sum
            du = jnp.concatenate(du_pairs, axis=1) + du_state
            xdu[rows, :] += mm_left(wide_x * du, pick)
            dyc[rows, :] += mm_left(dy * carried, pick)
            xdus[rows, :] += mm_left(wide_x * du_state, pick)
            dskip = dskip + jnp.sum(dy * wide_x, axis=0, keepdims=True)
            gext[rows, :] = (step_w * du + skip * dy) * slope[rows, :]
        gconv = gext[0:tokens, :]
        for k in range(CONV):
            first = HALO - CONV + 1 + k
            vec[0, j, k : k + 1, :] = jnp.sum(
                vwide[first : first + tokens, :] * gconv, axis=0, keepdims=True
            )
        vec[0, j, CONV : CONV + 1, :] = jnp.sum(gconv, axis=0, keepdims=True)
        vec[0, j, CONV + 1 : CONV + 2, :] = tgate_ref[...]
        vec[0, j, CONV + 2 : CONV + 3, :] = dskip
        total = cv_ref[CONV - 1 : CONV, :] * gconv
        for k in range(CONV - 1):
            total = total + cv_ref[k : k + 1, :] * gext[CONV - 1 - k : CONV - 1 - k + tokens, :]
        gv[j] = total.astype(bf16)
        lacking = jnp.zeros((8, BLOCK), f32)
        edge_tail[j] = total[tokens - 8 :, :] + lacking
        edge_own[j] = gconv[0:8, :]
        send_to(
            edge_own.at[j], edge_land.at[j], edge_sems.at[0, j], edge_sems.at[1, j], seq=before_id
        ).start()

    @when_after(t_scan + half_nb)
    def _():
        rs[0][0].advance(0)
        rs[0][1].advance(0)

    @when_after(t_values - 1)
    def _():
        tri = mask.astype(f32)
        tri_t = mask_t.astype(f32)
        strict = (rows_i > cols_i).astype(f32)
        decay = jnp.exp(decay_ref[...])
        bias_sum = jnp.zeros((1, LANES), f32)
        decay_sum = jnp.zeros((1, LANES), f32)
        for c in range(chunks):
            rows = slice(c * CHUNK, (c + 1) * CHUNK)
            step = step_ref[rows, :]
            col_rows = [dcols[b, 0:BLOCK_HEADS, rows] for b in range(nb)]
            rest = LANES - BLOCK_HEADS * nb
            col_rows.append(jnp.zeros((rest, CHUNK), f32))
            dlog = dyc[rows, :] - jnp.concatenate(col_rows, axis=0).T
            drate = (
                mm_exact(tri_t, dlog)
                + mm_exact(strict, xdus[rows, :] * step)
                + ends[c : c + 1, :]
            )
            dstep = xdu[rows, :] - decay * drate
            draw = dstep * slope_ref[rows, :]
            small[rows, LANES:] = draw.astype(bf16)
            bias_sum = bias_sum + jnp.sum(draw, axis=0, keepdims=True)
            decay_sum = decay_sum - jnp.sum(drate * step, axis=0, keepdims=True) * decay
            b_rows = bc_ref[rows, :STATE]
            c_rows = bc_ref[rows, STATE:]
            high, low = parts(dscores[c])
            dbc[1, rows, :] += mm(high, b_rows) + mm(low, b_rows)
            dbc[0, rows, :] += mm(high, c_rows, TN) + mm(low, c_rows, TN)
        hvec[0] = jnp.zeros_like(hvec[0])
        hvec[0, 0:1, :] = bias_sum
        hvec[0, 1:2, :] = decay_sum
        send_to(
            dbc.at[1 - core], dbc_land, dbc_sems.at[0], dbc_sems.at[1], head=1 - core
        ).start()

    @pl.when((step_id >= t_values) & (step_id < t_grad))
    def _():
        j = step_id - t_values
        send_to(
            edge_own.at[j], edge_land.at[j], edge_sems.at[0, j], edge_sems.at[1, j], seq=before_id
        ).wait()
        cv = cv_ref[...]
        nxt = jnp.where(index == size - 1, 0.0, 1.0) * edge_land[j]
        row8 = lax.broadcasted_iota(jnp.int32, (8, BLOCK), 0)
        fix = edge_tail[j]
        for k in range(CONV - 1):
            ahead = CONV - 1 - k
            moved = pltpu.roll(nxt, 8 - ahead, 0)
            fix = fix + jnp.where(row8 >= 8 - ahead, cv[k : k + 1, :] * moved, 0.0)
        both_rows = jnp.concatenate([gv[j, tokens - 16 : tokens - 8, :].astype(f32), fix], axis=0)
        gv[j, tokens - 16 :, :] = both_rows.astype(bf16)
        put_block(w_values, normedt_ref, gv[j], j)

    @when_after(t_values + half_nb - 1)
    def _():
        rs[2][0].start(0)

    @when_after(t_values)
    def _():
        send_to(
            dbc.at[1 - core], dbc_land, dbc_sems.at[0], dbc_sems.at[1], head=1 - core
        ).wait()
        sext = sext_ref[core].astype(f32)
        taps = cs_ref[core]
        conv = conv_rows(sext, taps, HALO - CONV + 1, tokens)
        gs = (dbc[core] + dbc_land[...]) * silu_grad(conv)
        for k in range(CONV):
            first = HALO - CONV + 1 + k
            hvec[0, 2 + k : 3 + k, :] = jnp.sum(
                sext[first : first + tokens, :] * gs, axis=0, keepdims=True
            )
        hvec[0, 2 + CONV : 3 + CONV, :] = jnp.sum(gs, axis=0, keepdims=True)
        dbc[core] = gs
        sedge_own[...] = gs[0:8, :]
        send_to(
            sedge_own, sedge_land, sedge_sems.at[0], sedge_sems.at[1], seq=before_id
        ).start()

    @when_after(t_grad - 1)
    def _():
        rs[2][1].start(0)
        send_to(
            sedge_own, sedge_land, sedge_sems.at[0], sedge_sems.at[1], seq=before_id
        ).wait()
        taps = cs_ref[core]
        nxt = jnp.where(index == size - 1, 0.0, 1.0) * sedge_land[...]
        gs = jnp.concatenate([dbc[core], nxt], axis=0)
        total = taps[CONV - 1 : CONV, :] * gs[0:tokens, :]
        for k in range(CONV - 1):
            total = total + taps[k : k + 1, :] * gs[CONV - 1 - k : CONV - 1 - k + tokens, :]
        small[:, 0:LANES] = total.astype(bf16)
        group = width // 4
        for q in range(4):
            piece = mm(normedt_ref[q * group : (q + 1) * group, :], small[...]).astype(bf16)
            for b in range(size // 4):
                slot = slot_of(q * (size // 4) + b, 1, bits)
                w_small[slot] = piece[b * rows_own : (b + 1) * rows_own, :]
        rs_small.start(0)

    @pl.when((step_id >= t_grad) & (step_id < t_final))
    def _():
        j = step_id - t_grad
        part = mm(ggate_ref[j], wi_ref[0], NT) + mm(gv[j], wi_ref[1], NT)

        @pl.when(j == 0)
        def _():
            acc[...] = part + mm(small[...], wsmall_ref[...], NT)

        @pl.when(j > 0)
        def _():
            acc[...] += part

    @when_after(t_grad + half_nb)
    def _():
        rs[1][0].advance(0)
        rs[1][1].advance(0)

    @when_after(t_final - 1)
    def _():
        for c in range(chunks):
            rows = slice(c * CHUNK, (c + 1) * CHUNK)
            acc_send[c] = acc[rows, :].astype(bf16)
            send_to(
                acc_send.at[c], acc_land.at[c], acc_sems.at[0, c], acc_sems.at[1, c], head=1 - core
            ).start()

    @pl.when(step_id >= t_final)
    def _():
        c = step_id - t_final
        send_to(
            acc_send.at[c], acc_land.at[c], acc_sems.at[0, c], acc_sems.at[1, c], head=1 - core
        ).wait()
        total = acc[pl.ds(pl.multiple_of(c * CHUNK, CHUNK), CHUNK), :] + acc_land[c].astype(f32)
        scale = scale_ref[:, 0:1]
        hat = hid_ref[...].astype(f32) * scale
        term = jnp.sum(total * hat, axis=0, keepdims=True)

        @pl.when(c == 0)
        def _():
            norm_vec[0] = jnp.broadcast_to(term, norm_vec.shape[1:])

        @pl.when(c > 0)
        def _():
            norm_vec[0] += jnp.broadcast_to(term, norm_vec.shape[1:])

        ghat = total * gain_ref[...]
        mean = jnp.mean(ghat * hat, axis=1, keepdims=True)
        ghid_ref[...] = cot_ref[...].astype(f32) + scale * (ghat - hat * mean)

    @when_after(t_final + chunks - 1)
    def _():
        for bit in range(bits):
            exchange_sum(norm_vec, norm_land, bit, index, norm_sems.at[0], norm_sems.at[1])
            exchange_sum(vec, vec_land, bit, index, vec_sems.at[0], vec_sems.at[1])
            exchange_sum(hvec, hvec_land, bit, index, hvec_sems.at[0], hvec_sems.at[1])
        heads_ref[...] = hvec[bits]
        for b in range(nb):
            sums_ref[0:8, b * BLOCK : (b + 1) * BLOCK] = vec[bits, b]
        sums_ref[8:16, :] = norm_vec[bits]
        for stage in range(1, bits):
            for g in range(2):
                for part in range(2):
                    rs[g][part].advance(stage)
            for part in range(2):
                rs[2][part].advance(stage - 1)
            rs_small.advance(stage - 1)
        for part in range(2):
            rs[2][part].advance(bits - 1)
        rs_small.advance(bits - 1)


def back_call(
    gm_t, normed_t, ggate, run, step, slope, bc, sext, skip, decay, conv_shared, wsmall, gain,
    tgate, gated_w, vext, dy, after, state_in, dstate, conv_values, runt, stept, both, hidden,
    cotangent, scale,
):
    width, tokens = normed_t.shape
    inner = dy.shape[1]
    chunks = tokens // CHUNK
    nb = inner // BLOCK
    size = lax.axis_size("seq")
    bits = size.bit_length() - 1
    rows_own = width // size
    t_scan, t_values, t_grad, t_final = 2 * nb, 3 * nb, 4 * nb, 5 * nb

    def column(start):
        return lambda s: jnp.clip(s - start, 0, nb - 1)

    def full(shape):
        return pl.BlockSpec(shape, lambda s: (0,) * len(shape), pipeline_mode=pl.Buffered(1))

    def cols(rows, start):
        at = column(start)
        return pl.BlockSpec((rows, BLOCK), lambda s: (0, at(s)))

    def scan_or_values(s):
        return jnp.where(s < t_values, column(t_scan)(s), column(t_values)(s))

    row_block = lambda w: pl.BlockSpec((CHUNK, w), lambda s: (jnp.clip(s - t_final, 0, chunks - 1), 0))
    part_cols = inner // 2
    held = lambda: pltpu.VMEM((2, size, rows_own, part_cols), bf16)
    landing = lambda: tuple(
        pltpu.VMEM((2, size >> (s + 1), rows_own, part_cols), bf16) for s in range(bits)
    )
    sem = pltpu.SemaphoreType.DMA
    return pl.pallas_call(
        functools.partial(back_kernel, bits),
        grid=(5 * nb + chunks,),
        in_specs=[
            full((width, tokens)),
            full((width, tokens)),
            full((nb, tokens, BLOCK)),
            full((tokens, LANES)),
            full((tokens, LANES)),
            full((tokens, LANES)),
            full((tokens, 2 * STATE)),
            full((2, HALO + tokens, LANES)),
            full((1, LANES)),
            full((1, LANES)),
            full((2, CONV + 1, LANES)),
            full((width, 2 * LANES)),
            full((1, width)),
            cols(1, t_scan),
            cols(tokens, 0),
            cols(HALO + tokens, t_scan),
            cols(tokens, t_scan),
            pl.BlockSpec((chunks, STATE, BLOCK), lambda s: (0, 0, column(t_scan)(s))),
            cols(STATE, t_scan),
            cols(STATE, t_scan),
            pl.BlockSpec((CONV + 1, BLOCK), lambda s: (0, scan_or_values(s))),
            pl.BlockSpec((1, 8, tokens), lambda s: (column(t_scan)(s), 0, 0)),
            pl.BlockSpec((1, 8, tokens), lambda s: (column(t_scan)(s), 0, 0)),
            pl.BlockSpec((2, width, BLOCK), lambda s: (0, 0, column(t_grad)(s))),
            row_block(width),
            row_block(width),
            row_block(LANES),
        ],
        out_shape=[
            jax.ShapeDtypeStruct((rows_own, inner), f32),
            jax.ShapeDtypeStruct((rows_own, inner), f32),
            jax.ShapeDtypeStruct((rows_own, inner), f32),
            jax.ShapeDtypeStruct((rows_own, 2 * LANES), f32),
            jax.ShapeDtypeStruct((tokens, width), f32),
            jax.ShapeDtypeStruct((16, inner), f32),
            jax.ShapeDtypeStruct((8, LANES), f32),
        ],
        out_specs=[
            pl.BlockSpec((rows_own, inner), lambda s: (0, 0)),
            pl.BlockSpec((rows_own, inner), lambda s: (0, 0)),
            pl.BlockSpec((rows_own, inner), lambda s: (0, 0)),
            pl.BlockSpec((rows_own, 2 * LANES), lambda s: (0, 0)),
            row_block(width),
            pl.BlockSpec((16, inner), lambda s: (0, 0)),
            pl.BlockSpec((8, LANES), lambda s: (0, 0)),
        ],
        scratch_shapes=[
            held(), held(), held(),
            pltpu.VMEM((size, rows_own, 2 * LANES), bf16),
            landing(), landing(), landing(),
            tuple(pltpu.VMEM((size >> (s + 1), rows_own, 2 * LANES), bf16) for s in range(bits)),
            sem((7, bits)), sem((7, bits)),
            pltpu.VMEM((nb, tokens, BLOCK), bf16),
            pltpu.VMEM((tokens, width), f32),
            pltpu.VMEM((chunks, CHUNK, width), bf16),
            pltpu.VMEM((chunks, CHUNK, width), bf16),
            sem((2, chunks)),
            pltpu.VMEM((nb, 8, BLOCK), f32),
            pltpu.VMEM((nb, 8, BLOCK), f32),
            pltpu.VMEM((nb, 8, BLOCK), f32),
            sem((2, nb)),
            pltpu.VMEM((2, tokens, LANES), f32),
            pltpu.VMEM((tokens, LANES), f32),
            sem((2,)),
            pltpu.VMEM((tokens, 2 * LANES), bf16),
            pltpu.VMEM((8, LANES), f32),
            pltpu.VMEM((8, LANES), f32),
            sem((2,)),
            pltpu.VMEM((bits + 1, nb, 8, BLOCK), f32),
            pltpu.VMEM((bits, nb, 8, BLOCK), f32),
            sem((2, bits)),
            pltpu.VMEM((bits + 1, 8, width), f32),
            pltpu.VMEM((bits, 8, width), f32),
            sem((2, bits)),
            pltpu.VMEM((bits + 1, 8, LANES), f32),
            pltpu.VMEM((bits, 8, LANES), f32),
            sem((2, bits)),
            pltpu.VMEM((chunks, CHUNK, CHUNK), f32),
            pltpu.VMEM((chunks, CHUNK, CHUNK), f32),
            pltpu.VMEM((STATE, tokens), bf16),
            pltpu.VMEM((chunks, CHUNK, CHUNK), f32),
            pltpu.VMEM((tokens, LANES), f32),
            pltpu.VMEM((8, LANES), f32),
            pltpu.VMEM((nb, 8, tokens), f32),
            pltpu.VMEM((tokens, LANES), f32),
            pltpu.VMEM((tokens, LANES), f32),
            pltpu.VMEM((tokens, LANES), f32),
            pltpu.VMEM((HALO + tokens, BLOCK), f32),
            pltpu.VMEM((tokens + 8, BLOCK), f32),
        ],
        compiler_params=pltpu.CompilerParams(
            collective_id=3, has_side_effects=True, vmem_limit_bytes=66000000
        ),
        name="back",
    )(
        gm_t, normed_t, ggate, run, step, slope, bc, sext, skip, decay, conv_shared, wsmall, gain,
        tgate, gated_w, vext, dy, after, state_in, dstate, conv_values, runt, stept, both, hidden,
        cotangent, scale,
    )


def to_owners(states, kind):
    size = lax.axis_size("seq")
    pieces = states.astype(kind).reshape(size, states.shape[0] // size, states.shape[1])
    return lax.all_to_all(pieces, "seq", split_axis=0, concat_axis=0, tiled=True).astype(f32)


def from_owners(pieces, kind):
    back = lax.all_to_all(
        pieces.astype(kind), "seq", split_axis=0, concat_axis=0, tiled=True
    ).astype(f32)
    return back.reshape(-1, back.shape[2])


def carried_in(pieces, gains, reverse):
    size = pieces.shape[0]
    order = range(size - 1, -1, -1) if reverse else range(size)
    held = jnp.zeros_like(pieces[0])
    out = [None] * size
    for i in order:
        out[i] = held
        held = gains[i][None, :] * held + pieces[i]
    return jnp.stack(out)


def body(
    hidden, cotangent, norm_gain, proj_inner, proj_step, proj_shared, conv_values, conv_shared,
    step_bias, decay_log, skip_gain, gate_gain, proj_out,
):
    tokens = hidden.shape[0]
    inner = proj_inner.shape[2]
    heads = proj_step.shape[1]
    width = hidden.shape[1]
    size = lax.axis_size("seq")
    shared_here = conv_shared.shape[1] // lax.axis_size("head")
    shared_start = lax.axis_index("head") * shared_here
    halo = from_behind(hidden[-HALO:], 1)
    both = jnp.transpose(proj_inner, (1, 0, 2))
    lanes = lambda v: jnp.pad(v, (0, LANES - heads))[None, :]
    wstep = jnp.pad(proj_step, ((0, 0), (0, LANES - heads)))
    bias, decay, skip = lanes(step_bias), lanes(decay_log), lanes(skip_gain)
    (
        normed, norm_scale, gate_in, vext, yloc, after, step, slope, run, runt, stept, sext, bc,
    ) = front_call(
        hidden, halo, norm_gain[None, :], both, wstep, proj_shared, conv_values, conv_shared,
        bias, decay, skip,
    )
    total = jnp.sum(run[CHUNK - 1 :: CHUNK], axis=0)
    totals = lax.all_to_all(
        jnp.broadcast_to(total[None, None], (size, 1, LANES)), "seq", 0, 0, tiled=True
    )[:, 0, :heads]
    gains = jnp.repeat(jnp.exp(totals), HEAD_DIM, axis=1)
    state_in = from_owners(carried_in(to_owners(after[-1], f32), gains, False), f32)
    y, gated_w, partial_mix, squares = mix_call(
        yloc, gate_in, state_in, run, bc, gate_gain[None, :], proj_out
    )
    mixed_sum = partial_mix + swap(partial_mix)
    squares = squares[:, 0] + swap(squares[:, 0])
    inverse = lax.rsqrt(squares / INNER + norm_eps)[:, None]
    wide_hidden = hidden.astype(f32)
    wide_cot = cotangent.astype(f32)
    block_out = wide_hidden + mixed_sum * inverse
    grad_mixed = (wide_cot * inverse).astype(bf16)
    grad_inverse = jnp.sum(wide_cot * mixed_sum, axis=1, keepdims=True)
    coef = jnp.broadcast_to(grad_inverse * inverse**3 / INNER, (tokens, LANES))
    ggate, dy, term_gate, own_term = gate_call(
        grad_mixed, proj_out, y, gate_in, gate_gain[None, :], coef, run, bc
    )
    dstate = from_owners(carried_in(to_owners(own_term, bf16), gains, True), bf16)
    wshared_own = lax.dynamic_slice_in_dim(proj_shared, shared_start, shared_here, 1)
    (gout, ggw, gvw, gsmall, grad_hidden, sums, head_sums) = back_call(
        grad_mixed.T, normed.T, ggate, run, step, slope, bc, sext, skip, decay,
        conv_shared.reshape(CONV + 1, -1, LANES).transpose(1, 0, 2),
        jnp.concatenate([wshared_own, wstep], axis=1), norm_gain[None, :], term_gate, gated_w, vext,
        dy, after, state_in, dstate, conv_values, runt, stept, both, hidden, cotangent, norm_scale,
    )
    return (
        block_out,
        grad_hidden,
        sums[8],
        jnp.stack([ggw, gvw], axis=1),
        gsmall[:, shared_here : shared_here + heads],
        gsmall[:, :shared_here],
        sums[: CONV + 1],
        head_sums[2 : 3 + CONV],
        head_sums[0, :heads],
        head_sums[1, :heads],
        jnp.sum(sums[CONV + 2].reshape(heads, HEAD_DIM), axis=1),
        sums[CONV + 1],
        gout,
    )


def solution(mesh):
    return jax.shard_map(
        body,
        mesh=mesh,
        in_specs=(
            P("seq", None),
            P("seq", None),
            P(),
            P(None, None, "head"),
            P(None, "head"),
            P(),
            P(None, "head"),
            P(),
            P("head"),
            P("head"),
            P("head"),
            P("head"),
            P(None, "head"),
        ),
        out_specs=(
            P("seq", None),
            P("seq", None),
            P(),
            P("seq", None, "head"),
            P("seq", "head"),
            P("seq", "head"),
            P(None, "head"),
            P(None, "head"),
            P("head"),
            P("head"),
            P("head"),
            P("head"),
            P("seq", "head"),
        ),
        check_vma=False,
    )
```

time: 1040 us -> 432 us (0.42)
  waiting for transfers between devices: 508 us -> 55.4 us
  Pallas kernels: 0 us -> 256 us
  matrix products: 165 us -> 0 us
  blocking collectives: 85.9 us -> 0 us
  local copies, waits for them, and re-layouts: 132 us -> 54.5 us
  other arithmetic: 83.6 us -> 34.2 us
  starting transfers between devices: 44.4 us -> 29.3 us
  between operations: 15.9 us -> 1.18 us
    reduce_scatter x3 -> x0, waiting for transfers between devices: 376 us -> none  [the longest x1 202 us: body(): lax.psum_scatter(term_inner, 'seq', scatter_dimension=0, tiled=True)]
    pallas_call x0 -> x4, Pallas kernels: none -> 256 us  [the longest x1 209 us: back_call(): pl.pallas_call(functools.partial(back_kernel, bits), grid=(5 * nb + chunk...]
    dot_general x32 -> x0, matrix products: 163 us -> none  [the longest x3 48 us: ssd_parts(): jnp.einsum('cijh,cjhp->cihp', scores[:, :, :, None] * decay_mat, weighted...]
    psum x2 -> x0, blocking collectives: 85.9 us -> none  [the longest x1 83.5 us: body(): lax.psum((term_conv_values, term_conv_shared, head_terms, term_gate, term...]
    unnamed x7 -> x0, waiting for transfers between devices: 85.3 us -> none
    all_to_all x5, waiting for transfers between devices: 16.5 us -> 55.4 us  [the longest x2 27.7 us: to_owners(): lax.all_to_all(pieces, 'seq', split_axis=0, concat_axis=0, tiled=True)]
    reduce_sum x15 -> x3, other arithmetic: 42.2 us -> 3.82 us  [the longest x1 3.17 us: body(): grad_inverse = jnp.sum(wide_cot * mixed_sum, axis=1, keepdims=True)]
    psum x2 -> x0, waiting for transfers between devices: 26.2 us -> none  [the longest x1 22 us: body(): grad_normed = lax.psum(partial_normed, 'head')]
  transfers between devices with their start and end apart: 15 -> 8, of which waited for: 8 -> 5; matrix products, arithmetic and copies ran while one was open for 22% -> 8% of each run, Pallas kernels for 0% -> 0%
where the time goes in v1:
time: 432 us; the launch traced here: 431 us
  Pallas kernels  256 us (59%)
  waiting for transfers between devices  55.4 us (13%)
  local copies, waits for them, and re-layouts  54.5 us (13%)
  other arithmetic  34.2 us (8%)
  starting transfers between devices  29.3 us (7%)
    pallas_call x1, Pallas kernels, back_call(): pl.pallas_call(functools.partial(back_kernel, bits), grid=(5 * nb + chunk...  209 us
    all_to_all x2, waiting for transfers between devices, to_owners(): lax.all_to_all(pieces, 'seq', split_axis=0, concat_axis=0, tiled=True)  27.7 us
    unnamed x83, local copies, waits for them, and re-layouts  24.6 us
    all_to_all x2, waiting for transfers between devices, from_owners(): lax.all_to_all(pieces.astype(kind), 'seq', split_axis=0, concat_axis=0, t...  22.6 us
    pallas_call x1, Pallas kernels, front_call(): pl.pallas_call(front_kernel, grid=(inner // BLOCK,), in_specs=[full((toke...  21.9 us
    unnamed x28, other arithmetic  17.6 us
    pallas_call x1, Pallas kernels, mix_call(): pl.pallas_call(mix_kernel, grid=(inner // BLOCK,), in_specs=[block(tokens...  13.4 us
    pallas_call x1, Pallas kernels, gate_call(): pl.pallas_call(gate_kernel, grid=(inner // BLOCK,), in_specs=[full((token...  12.3 us
  transfers between devices with their start and end apart: 8, of which 5 were waited for; matrix products, arithmetic and copies ran while one was open for 8% of the time, Pallas kernels for 0%

profile of v1, /device:TPU:0, one launch (start us, length us, event | category | flops | bytes accessed | tf_op | source)
XLA Modules:
  0.0 430.9 jit_solution(9881521282248592848)
XLA Ops:
  0.6 0.8 slice.271
  1.4 4.9 %collective-permute-start = (bf16[16,1536]{1,0:T(8,128)(2,1)S(1)}, bf16[16,1536]{1,0:T(8,128)(2,1)S(1)}, u32[]{:S(2)}, u32[]{:S(2)}) collective-permute-start(bf16[16,1536]{1,0:T(8,128)(2,1)S(1)} %slice.271), channel_id=1, source_target_pairs={{0,2},{2,4},{4,6},{6,8},{8,10},{10,12},{12,14},{14,16},{16,18},{18... | collective-permute-start | bytes 147464 | tf_op jit(solution)/shard_map/ppermute | solution.py:41
  6.3 1.2 pad_bitcast_fusion
  7.5 1.2 pad_bitcast_fusion.2.bias_ref
  8.7 1.3 broadcast_in_dim.91.gain_ref
  10.0 8.8 %copy.49 = bf16[1536,2,1536]{2,0,1:T(8,128)(2,1)} copy(bf16[1536,2,1536]{2,1,0:T(2,128)(2,1)} %param.16) | data formatting | bytes 18874368 | tf_op args[3]
  19.0 0.8 pad.14.wstep_ref
  20.5 21.9 %front.1 = (bf16[512,1536]{1,0:T(8,128)(2,1)}, f32[512,128]{1,0:T(8,128)}, f32[512,1536]{1,0:T(8,128)}, bf16[528,1536]{1,0:T(8,128)(2,1)}, f32[512,1536]{1,0:T(8...) custom-call(bf16[512,1536]{1,0:T(8,128)(2,1)} %hid_ref.3, ...), custom_call_target="tpu_custom_call" | custom-call | tf_op jit(solution)/shard_map/front/pallas_call | solution.py:258
  42.4 0.9 slice.272
  44.0 5.9 %all-to-all-start = ((f32[16,1,128]{2,1,0:T(1,128)}), f32[16,1,128]{2,1,0:T(1,128)S(1)}, u32[]{:S(2)}, u32[]{:S(2)}) async-start(f32[16,1,128]{2,1,0:T(1,128)} %broadcast_in_dim.95), calls=%async_computation | async-start | bytes 16384 | tf_op jit(solution)/shard_map/all_to_all | solution.py:1107
  49.9 2.1 slice_bitcast_fusion
  52.0 5.1 %all-to-all-done = f32[16,1,128]{2,1,0:T(1,128)S(1)} async-done(((f32[16,1,128]{2,1,0:T(1,128)}), f32[16,1,128]{2,1,0:T(1,128)S(1)}, u32[]{:S(2)}, u32[]{:S(2)}) %all-to-all-start) | async-done | bytes 8224 | tf_op jit(solution)/shard_map/all_to_all | solution.py:1107
  57.1 3.6 all-to-all-start.1
  64.1 15.1 %all-to-all-done.1 = f32[16,8,1536]{2,1,0:T(8,128)S(1)} async-done(((f32[16,8,1536]{2,1,0:T(8,128)}), f32[16,8,1536]{2,1,0:T(8,128)S(1)}, u32[]{:S(2)}, u32[]{:S(2)}) %all-to-all-start.1) | async-done | bytes 786464 | tf_op jit(solution)/shard_map/all_to_all | solution.py:1063
  88.7 4.7 %all-to-all-start.2 = ((f32[16,8,1536]{2,1,0:T(8,128)}), f32[16,8,1536]{2,1,0:T(8,128)S(1)}, u32[]{:S(2)}, u32[]{:S(2)}) async-start(f32[16,8,1536]{2,1,0:T(8,128)} %constant_dynamic-update-slice_fusion), calls=%async_computation.2 | async-start | bytes 1572864 | tf_op jit(solution)/shard_map/all_to_all | solution.py:1067
  94.0 17.9 %all-to-all-done.2 = f32[16,8,1536]{2,1,0:T(8,128)S(1)} async-done(((f32[16,8,1536]{2,1,0:T(8,128)}), f32[16,8,1536]{2,1,0:T(8,128)S(1)}, u32[]{:S(2)}, u32[]{:S(2)}) %all-to-all-start.2) | async-done | bytes 786464 | tf_op jit(solution)/shard_map/all_to_all | solution.py:1067
  112.0 0.9 copy-done.2
  112.8 13.4 %mix.1 = (f32[512,1536]{1,0:T(8,128)}, bf16[512,1536]{1,0:T(8,128)(2,1)}, f32[512,1536]{1,0:T(8,128)}, f32[512,128]{1,0:T(8,128)}) custom-call(f32[512,1536]{1,0:T(8,128)} %get-tuple-element.41.yloc_ref, f32[512,1536]{1,0:T(8,128)} %get-tuple-element.42.gate_ref, f32[128,1536]{1,0:T(8,128)} %bitcast.64, f32[512,128]{1,0:T(8,128)} %get-tuple-element.43.run_ref, ...), custom_call_target="tpu_custom_call" | custom-call | tf_op jit(solution)/shard_map/mix/pallas_call | solution.py:330
  126.4 2.4 copy.41
  128.9 2.7 copy.37
  131.5 2.6 copy.42
  134.8 3.2 fusion.1
  138.1 5.3 %fusion = (bf16[512,1536]{0,1:T(8,128)(2,1)}, f32[512,1536]{0,1:T(8,128)}) fusion(bf16[512,1536]{0,1:T(8,128)(2,1)S(1)} %copy-done, f32[512]{0:T(512)S(1)} %get-tuple-element.107, f32[512,1536]{0,1:T(8,128)S(1)} %copy.41, f32[512,1536]{0,1:T(8,128)} %collective-permute-done.1, bf16[512,1536]{0,1:T(8,128)(2,1)S(1)} %copy-done.3), kind=kLoop, calls=%fused_computation.3 | loop fusion | flops 5505024 | bytes 14157824 | tf_op jit(solution)/shard_map/convert_element_type | solution.py:1121
  143.4 2.6 copy.44.gm_ref
  146.0 0.8 broadcast_in_dim.126.coef_ref
  146.8 12.3 %gate_back.1 = (bf16[6,512,256]{2,1,0:T(8,128)(2,1)}, f32[512,1536]{1,0:T(8,128)}, f32[1,1536]{1,0:T(1,128)}, f32[128,1536]{1,0:T(8,128)}) custom-call(bf16[512,1536]{1,0:T(8,128)(2,1)} %copy.44.gm_ref, bf16[1536,1536]{1,0:T(8,128)(2,1)} %wout_ref.3, f32[512,1536]{1,0:T(8,128)} %get-tuple-element.49.y_ref, f32[512,1536]{1,0:T(8,128)} %get-tuple-element.42.gate_ref, ...), custom_call_target="tpu_custom_call" | custom-call | tf_op jit(solution)/shard_map/gate_back/pallas_call | solution.py:395
  159.3 2.0 convert_bitcast_fusion
  161.3 5.1 %all-to-all-start.3 = ((bf16[16,8,1536]{2,1,0:T(8,128)(2,1)}), bf16[16,8,1536]{2,1,0:T(8,128)(2,1)S(1)}, u32[]{:S(2)}, u32[]{:S(2)}) async-start(bf16[16,8,1536]{2,1,0:T(8,128)(2,1)} %convert_bitcast_fusion), calls=%async_computation.3 | async-start | bytes 786432 | tf_op jit(solution)/shard_map/all_to_all | solution.py:1063
  166.5 12.6 %all-to-all-done.3 = bf16[16,8,1536]{2,1,0:T(8,128)(2,1)S(1)} async-done(((bf16[16,8,1536]{2,1,0:T(8,128)(2,1)}), bf16[16,8,1536]{2,1,0:T(8,128)(2,1)S(1)}, u32[]{:S(2)}, u32[]{:S(2)}) %all-to-all-start.3) | async-done | bytes 393248 | tf_op jit(solution)/shard_map/all_to_all | solution.py:1063
  179.3 0.7 constant_dynamic-update-slice_fusion.31
  189.2 4.5 %all-to-all-start.4 = ((bf16[16,8,1536]{2,1,0:T(8,128)(2,1)}), bf16[16,8,1536]{2,1,0:T(8,128)(2,1)}, u32[]{:S(2)}, u32[]{:S(2)}) async-start(bf16[16,8,1536]{2,1,0:T(8,128)(2,1)} %constant_dynamic-update-slice_fusion.16), calls=%async_computation.4 | async-start | bytes 786432 | tf_op jit(solution)/shard_map/all_to_all | solution.py:1067
  193.7 1.0 constant_dynamic-slice_fusion
  194.8 1.0 pad_maximum_fusion.1.wsmall_ref
  195.7 2.6 copy.43
  198.3 2.4 copy.45
  200.7 4.6 %all-to-all-done.4 = bf16[16,8,1536]{2,1,0:T(8,128)(2,1)} async-done(((bf16[16,8,1536]{2,1,0:T(8,128)(2,1)}), bf16[16,8,1536]{2,1,0:T(8,128)(2,1)}, u32[]{:S(2)}, u32[]{:S(2)}) %all-to-all-start.4) | async-done | bytes 393248 | tf_op jit(solution)/shard_map/all_to_all | solution.py:1067
  205.3 2.0 bitcast_convert_fusion.dstate_ref
  207.2 208.6 %back.1 = (f32[96,1536]{1,0:T(8,128)}, f32[96,1536]{1,0:T(8,128)}, f32[96,1536]{1,0:T(8,128)}, f32[96,256]{1,0:T(8,128)}, f32[512,1536]{1,0:T(8,128)}, /*index=5*/f32[16,1536]{1,0:T(8,128)}, f32[8,128]{1,0:T(8,128)}) custom-call(bf16[1536,512]{1,0:T(8,128)(2,1)} %bitcast.63, bf16[1536,512]{1,0:T(8,128)(2,1)} %bitcast.66, ...), custom_call_target="tpu_custom_call" | custom-call | tf_op jit(solution)/shard_map/back/pallas_call | solution.py:955
  415.9 1.0 slice.337
  416.8 1.4 slice.338
  418.3 1.5 slice_reduce_fusion.1
  419.8 1.4 slice.339
  421.2 1.3 slice.340
  422.5 1.3 slice_bitcast_fusion.15
  423.8 1.3 pad_maximum_fusion
  425.1 1.9 copy.46
  428.4 1.7 copy.82
  430.0 0.8 copy.83
  (151 shorter events, 26.6 us)
Async XLA Ops:
  1.4 18.4 %collective-permute-start = (bf16[16,1536]{1,0:T(8,128)(2,1)S(1)}, bf16[16,1536]{1,0:T(8,128)(2,1)S(1)}, u32[]{:S(2)}, u32[]{:S(2)}) collective-permute-start(bf16[16,1536]{1,0:T(8,128)(2,1)S(1)} %slice.271), channel_id=1, source_target_pairs={{0,2},{2,4},{4,6},{6,8},{8,10},{10,12},{12,14},{14,16},{16,18},{18... | collective-permute-start | bytes 147464 | tf_op jit(solution)/shard_map/ppermute | solution.py:41
  10.0 8.8 %copy-start.32 = (bf16[1536,24]{0,1:T(8,128)(2,1)S(1)}, bf16[1536,24]{0,1:T(8,128)(2,1)}, u32[]{:S(2)}) copy-start(bf16[1536,24]{0,1:T(8,128)(2,1)} %param.17) | copy-start | bytes 221188
  19.9 0.6 copy-start.33
  44.0 13.2 %all-to-all-start = ((f32[16,1,128]{2,1,0:T(1,128)}), f32[16,1,128]{2,1,0:T(1,128)S(1)}, u32[]{:S(2)}, u32[]{:S(2)}) async-start(f32[16,1,128]{2,1,0:T(1,128)} %broadcast_in_dim.95), calls=%async_computation | async-start | bytes 16384 | tf_op jit(solution)/shard_map/all_to_all | solution.py:1107
  52.0 41.4 %copy-start.34 = (f32[1536]{0:T(1024)S(1)}, f32[1536]{0:T(1024)}, u32[]{:S(2)}) copy-start(f32[1536]{0:T(1024)} %param.24) | copy-start | bytes 18436
  57.1 22.0 %all-to-all-start.1 = ((f32[16,8,1536]{2,1,0:T(8,128)}), f32[16,8,1536]{2,1,0:T(8,128)S(1)}, u32[]{:S(2)}, u32[]{:S(2)}) async-start(f32[16,8,1536]{2,1,0:T(8,128)} %slice_bitcast_fusion), calls=%async_computation.1 | async-start | bytes 1572864 | tf_op jit(solution)/shard_map/all_to_all | solution.py:1063
  62.2 64.1 %copy-start.30 = (f32[1536]{0:T(1024)}, f32[1536]{0:T(1024)S(1)}, u32[]{:S(2)}) copy-start(f32[1536]{0:T(1024)S(1)} %broadcast_in_dim.98) | copy-start | bytes 18436
  62.4 63.9 %copy-start.12 = (f32[1536]{0:T(1024)}, f32[1536]{0:T(1024)S(1)}, u32[]{:S(2)}) copy-start(f32[1536]{0:T(1024)S(1)} %broadcast_in_dim.100) | copy-start | bytes 18436
  62.7 63.7 %copy-start.18 = (f32[1536]{0:T(1024)}, f32[1536]{0:T(1024)S(1)}, u32[]{:S(2)}) copy-start(f32[1536]{0:T(1024)S(1)} %broadcast_in_dim.104) | copy-start | bytes 18436
  62.9 63.4 %copy-start.20 = (f32[1536]{0:T(1024)}, f32[1536]{0:T(1024)S(1)}, u32[]{:S(2)}) copy-start(f32[1536]{0:T(1024)S(1)} %broadcast_in_dim.108) | copy-start | bytes 18436
  63.1 63.2 %copy-start.8 = (f32[1536]{0:T(1024)}, f32[1536]{0:T(1024)S(1)}, u32[]{:S(2)}) copy-start(f32[1536]{0:T(1024)S(1)} %broadcast_in_dim.110) | copy-start | bytes 18436
  63.2 63.1 %copy-start.22 = (f32[1536]{0:T(1024)}, f32[1536]{0:T(1024)S(1)}, u32[]{:S(2)}) copy-start(f32[1536]{0:T(1024)S(1)} %broadcast_in_dim.112) | copy-start | bytes 18436
  63.4 63.0 %copy-start.10 = (f32[1536]{0:T(1024)}, f32[1536]{0:T(1024)S(1)}, u32[]{:S(2)}) copy-start(f32[1536]{0:T(1024)S(1)} %broadcast_in_dim.114) | copy-start | bytes 18436
  63.5 62.8 %copy-start.24 = (f32[1536]{0:T(1024)}, f32[1536]{0:T(1024)S(1)}, u32[]{:S(2)}) copy-start(f32[1536]{0:T(1024)S(1)} %broadcast_in_dim.116) | copy-start | bytes 18436
  63.7 62.7 %copy-start.14 = (f32[1536]{0:T(1024)}, f32[1536]{0:T(1024)S(1)}, u32[]{:S(2)}) copy-start(f32[1536]{0:T(1024)S(1)} %broadcast_in_dim.118) | copy-start | bytes 18436
  63.8 62.6 %copy-start.26 = (f32[1536]{0:T(1024)}, f32[1536]{0:T(1024)S(1)}, u32[]{:S(2)}) copy-start(f32[1536]{0:T(1024)S(1)} %broadcast_in_dim.120) | copy-start | bytes 18436
  64.0 62.4 %copy-start.16 = (f32[1536]{0:T(1024)}, f32[1536]{0:T(1024)S(1)}, u32[]{:S(2)}) copy-start(f32[1536]{0:T(1024)S(1)} %broadcast_in_dim.122) | copy-start | bytes 18436
  64.1 62.3 %copy-start.28 = (f32[1536]{0:T(1024)}, f32[1536]{0:T(1024)S(1)}, u32[]{:S(2)}) copy-start(f32[1536]{0:T(1024)S(1)} %broadcast_in_dim.124) | copy-start | bytes 18436
  88.7 23.3 %all-to-all-start.2 = ((f32[16,8,1536]{2,1,0:T(8,128)}), f32[16,8,1536]{2,1,0:T(8,128)S(1)}, u32[]{:S(2)}, u32[]{:S(2)}) async-start(f32[16,8,1536]{2,1,0:T(8,128)} %constant_dynamic-update-slice_fusion), calls=%async_computation.2 | async-start | bytes 1572864 | tf_op jit(solution)/shard_map/all_to_all | solution.py:1067
  112.0 0.9 copy-start.2
  128.8 5.3 %copy-start.7 = (f32[512,128]{1,0:T(8,128)S(1)}, f32[512,128]{1,0:T(8,128)}, u32[]{:S(2)}) copy-start(f32[512,128]{1,0:T(8,128)} %get-tuple-element.47) | copy-start | bytes 786436
  128.8 6.0 %collective-permute-start.1 = (f32[512,1536]{0,1:T(8,128)S(1)}, f32[512,1536]{0,1:T(8,128)}, u32[]{:S(2)}, u32[]{:S(2)}) collective-permute-start(f32[512,1536]{0,1:T(8,128)S(1)} %copy.41), channel_id=1, source_target_pairs={{0,1},{1,0},{2,3},{3,2},{4,5},{5,4},{6,7},{7,6},{8,9},{9,8},{10,11... | collective-permute-start | bytes 9437192 | tf_op jit(solution)/shard_map/ppermute | solution.py:35
  134.3 3.8 copy-start
  134.3 3.8 copy-start.3
  134.3 3.7 collective-permute-start.2
  146.8 19.6 %copy-start.35 = (f32[24]{0:T(128)S(1)}, f32[24]{0:T(128)}, u32[]{:S(2)}) copy-start(f32[24]{0:T(128)} %get-tuple-element.122) | copy-start | bytes 292
  159.2 20.1 %copy-start.9 = (f32[1536]{0:T(1024)S(1)}, f32[1536]{0:T(1024)}, u32[]{:S(2)}) copy-start(f32[1536]{0:T(1024)} %copy-done.8) | copy-start | bytes 18436
  159.2 20.1 %copy-start.11 = (f32[1536]{0:T(1024)S(1)}, f32[1536]{0:T(1024)}, u32[]{:S(2)}) copy-start(f32[1536]{0:T(1024)} %copy-done.10) | copy-start | bytes 18436
  159.2 20.1 %copy-start.13 = (f32[1536]{0:T(1024)S(1)}, f32[1536]{0:T(1024)}, u32[]{:S(2)}) copy-start(f32[1536]{0:T(1024)} %copy-done.12) | copy-start | bytes 18436
  159.2 20.1 %copy-start.15 = (f32[1536]{0:T(1024)S(1)}, f32[1536]{0:T(1024)}, u32[]{:S(2)}) copy-start(f32[1536]{0:T(1024)} %copy-done.14) | copy-start | bytes 18436
  159.2 20.1 %copy-start.17 = (f32[1536]{0:T(1024)S(1)}, f32[1536]{0:T(1024)}, u32[]{:S(2)}) copy-start(f32[1536]{0:T(1024)} %copy-done.16) | copy-start | bytes 18436
  159.2 20.1 %copy-start.19 = (f32[1536]{0:T(1024)S(1)}, f32[1536]{0:T(1024)}, u32[]{:S(2)}) copy-start(f32[1536]{0:T(1024)} %copy-done.18) | copy-start | bytes 18436
  159.2 20.1 %copy-start.21 = (f32[1536]{0:T(1024)S(1)}, f32[1536]{0:T(1024)}, u32[]{:S(2)}) copy-start(f32[1536]{0:T(1024)} %copy-done.20) | copy-start | bytes 18436
  159.2 20.0 %copy-start.23 = (f32[1536]{0:T(1024)S(1)}, f32[1536]{0:T(1024)}, u32[]{:S(2)}) copy-start(f32[1536]{0:T(1024)} %copy-done.22) | copy-start | bytes 18436
  159.3 20.0 %copy-start.25 = (f32[1536]{0:T(1024)S(1)}, f32[1536]{0:T(1024)}, u32[]{:S(2)}) copy-start(f32[1536]{0:T(1024)} %copy-done.24) | copy-start | bytes 18436
  159.3 20.0 %copy-start.27 = (f32[1536]{0:T(1024)S(1)}, f32[1536]{0:T(1024)}, u32[]{:S(2)}) copy-start(f32[1536]{0:T(1024)} %copy-done.26) | copy-start | bytes 18436
  159.3 20.0 %copy-start.29 = (f32[1536]{0:T(1024)S(1)}, f32[1536]{0:T(1024)}, u32[]{:S(2)}) copy-start(f32[1536]{0:T(1024)} %copy-done.28) | copy-start | bytes 18436
  159.3 20.0 %copy-start.31 = (f32[1536]{0:T(1024)S(1)}, f32[1536]{0:T(1024)}, u32[]{:S(2)}) copy-start(f32[1536]{0:T(1024)} %copy-done.30) | copy-start | bytes 18436
  161.3 33.5 %copy-start.4 = (bf16[1536,128]{1,0:T(8,128)(2,1)S(1)}, bf16[1536,128]{1,0:T(8,128)(2,1)}, u32[]{:S(2)}) copy-start(bf16[1536,128]{1,0:T(8,128)(2,1)} %pad.14.wstep_ref) | copy-start | bytes 1179652
  161.3 17.9 %all-to-all-start.3 = ((bf16[16,8,1536]{2,1,0:T(8,128)(2,1)}), bf16[16,8,1536]{2,1,0:T(8,128)(2,1)S(1)}, u32[]{:S(2)}, u32[]{:S(2)}) async-start(bf16[16,8,1536]{2,1,0:T(8,128)(2,1)} %convert_bitcast_fusion), calls=%async_computation.3 | async-start | bytes 786432 | tf_op jit(solution)/shard_map/all_to_all | solution.py:1063
  189.2 9.1 %copy-start.1 = (f32[512,1536]{0,1:T(8,128)S(1)}, f32[512,1536]{0,1:T(8,128)}, u32[]{:S(2)}) copy-start(f32[512,1536]{0,1:T(8,128)} %get-tuple-element.141) | copy-start | bytes 9437188
  189.2 16.0 %all-to-all-start.4 = ((bf16[16,8,1536]{2,1,0:T(8,128)(2,1)}), bf16[16,8,1536]{2,1,0:T(8,128)(2,1)}, u32[]{:S(2)}, u32[]{:S(2)}) async-start(bf16[16,8,1536]{2,1,0:T(8,128)(2,1)} %constant_dynamic-update-slice_fusion.16), calls=%async_computation.4 | async-start | bytes 786432 | tf_op jit(solution)/shard_map/all_to_all | solution.py:1067
  415.9 12.5 %copy-start.5 = (f32[512,1536]{1,0:T(8,128)S(1)}, f32[512,1536]{1,0:T(8,128)}, u32[]{:S(2)}) copy-start(f32[512,1536]{1,0:T(8,128)} %get-tuple-element.166) | copy-start | bytes 9437188
  428.4 1.7 copy-start.6

commit v2 on v1

v2 whole, which is shorter than its diff:
```python
import functools

import jax
import jax.numpy as jnp
from jax import lax
from jax.experimental import pallas as pl
from jax.experimental.pallas import tpu as pltpu
from jax.sharding import PartitionSpec as P

HEAD_DIM = 64
STATE = 128
CONV = 4
INNER = 3072
CHUNK = 128
LANES = 128
BLOCK = 256
HALO = 16
BLOCK_HEADS = BLOCK // HEAD_DIM

norm_eps = 1e-05
highest = lax.Precision.HIGHEST
f32 = jnp.float32
bf16 = jnp.bfloat16
NN = (((1,), (0,)), ((), ()))
NT = (((1,), (1,)), ((), ()))
TN = (((0,), (0,)), ((), ()))


def flip(shard, bit):
    size = lax.axis_size("seq")
    return lax.ppermute(shard, "seq", [(i, i ^ (1 << bit)) for i in range(size)])


def swap(shard):
    return lax.ppermute(shard, "head", [(0, 1), (1, 0)])


def from_behind(shard, by):
    size = lax.axis_size("seq")
    pairs = [(i, i + by) for i in range(size) if 0 <= i + by < size]
    return lax.ppermute(shard, "seq", pairs)


def silu_grad(values):
    sigmoid = 1.0 / (1.0 + jnp.exp(-values))
    return sigmoid * (1.0 + values * (1.0 - sigmoid))


def silu(values):
    return values / (1.0 + jnp.exp(-values))


def mm(a, b, dims=NN):
    return lax.dot_general(a, b, dims, preferred_element_type=f32)


def parts(a):
    high = a.astype(bf16)
    return high, (a - high.astype(f32)).astype(bf16)


def mm_left(a, b, dims=NN):
    high, low = parts(a)
    return mm(high, b, dims) + mm(low, b, dims)


def mm_right(a, b, dims=NN):
    high, low = parts(b)
    return mm(a, high, dims) + mm(a, low, dims)


def mm_both(a, b, dims=NN):
    a_high, a_low = parts(a)
    b_high, b_low = parts(b)
    return mm(a_high, b_high, dims) + mm(a_low, b_high, dims) + mm(a_high, b_low, dims)


def mm_exact(a, b, dims=NN):
    return lax.dot_general(a, b, dims, precision=highest, preferred_element_type=f32)


def widen(cols):
    rows = cols.shape[0]
    lane = lax.broadcasted_iota(jnp.int32, (rows, LANES), 1)
    pieces = []
    for pair in range(BLOCK // LANES):
        first = jnp.broadcast_to(cols[:, 2 * pair : 2 * pair + 1], (rows, LANES))
        second = jnp.broadcast_to(cols[:, 2 * pair + 1 : 2 * pair + 2], (rows, LANES))
        pieces.append(jnp.where(lane < HEAD_DIM, first, second))
    return jnp.concatenate(pieces, axis=1)


def rolled(full, step):
    shift = lax.rem(LANES - BLOCK_HEADS * step, LANES)
    return pltpu.roll(full, shift, 1)


def causal():
    rows = lax.broadcasted_iota(jnp.int32, (CHUNK, CHUNK), 0)
    cols = lax.broadcasted_iota(jnp.int32, (CHUNK, CHUNK), 1)
    return rows >= cols


def conv_rows(ext, taps, first, rows):
    out = taps[CONV : CONV + 1, :]
    for k in range(CONV):
        out = out + taps[k : k + 1, :] * ext[first + k : first + k + rows, :]
    return out


def stack_pair(block):
    lane = lax.broadcasted_iota(jnp.int32, block.shape, 1)
    low = jnp.where(lane < HEAD_DIM, block, jnp.zeros_like(block))
    return low, block - low


class StateExchange:
    def __init__(self, index, size, reverse, own, landing, mixed, result, sems, gains):
        self.index, self.size, self.reverse = index, size, reverse
        self.own, self.landing, self.mixed, self.result = own, landing, mixed, result
        self.sems, self.gains = sems, gains

    def other(self, distance):
        return lax.rem(self.index + distance, self.size)

    def slot(self, source):
        return lax.rem(source - self.index - 1 + 2 * self.size, self.size)

    def send(self, j, value):
        share = value.shape[0] // self.size
        kind = self.own.dtype
        pieces = value.reshape(self.size, share, value.shape[1])
        self.own[j] = pieces.astype(kind)
        for d in range(1, self.size):
            pltpu.make_async_remote_copy(
                src_ref=self.own.at[j, self.other(d)],
                dst_ref=self.landing.at[j, self.size - d - 1],
                send_sem=self.sems.at[0, j],
                recv_sem=self.sems.at[1, j],
                device_id={"seq": self.other(d)},
                device_id_type=pl.DeviceIdType.MESH,
            ).start()

    def all_of(self, buffer, j, send, recv):
        return pltpu.make_async_remote_copy(
            src_ref=buffer.at[j, pl.ds(0, self.size - 1)],
            dst_ref=buffer.at[j, pl.ds(0, self.size - 1)],
            send_sem=self.sems.at[send, j],
            recv_sem=self.sems.at[recv, j],
            device_id={"seq": self.other(1)},
            device_id_type=pl.DeviceIdType.MESH,
        )

    def turn(self, j):
        self.all_of(self.landing, j, 0, 1).wait()
        kind = self.own.dtype
        self.landing[j, self.size - 1] = self.own[j, self.index]
        held = jnp.zeros(self.own.shape[2:], f32)
        order = range(self.size - 1, -1, -1) if self.reverse else range(self.size)
        for source in order:
            self.mixed[j, source] = held.astype(kind)
            gain = widen(rolled(self.gains[source : source + 1, :], j)[:, :BLOCK_HEADS])
            held = gain * held + self.landing[j, self.slot(source)].astype(f32)
        for d in range(1, self.size):
            pltpu.make_async_remote_copy(
                src_ref=self.mixed.at[j, self.other(d)],
                dst_ref=self.result.at[j, self.index],
                send_sem=self.sems.at[2, j],
                recv_sem=self.sems.at[3, j],
                device_id={"seq": self.other(d)},
                device_id_type=pl.DeviceIdType.MESH,
            ).start()

    def take(self, j):
        self.all_of(self.result, j, 2, 3).wait()
        self.result[j, self.index] = self.mixed[j, self.index]
        whole = self.result[j].astype(f32)
        return whole.reshape(whole.shape[0] * whole.shape[1], whole.shape[2])


def exchange_scratch(nb, size, kind):
    share = STATE // size
    return [pltpu.VMEM((nb, size, share, BLOCK), kind) for _ in range(4)] + [
        pltpu.SemaphoreType.DMA((4, nb))
    ]


def greet(index, core, size):
    barrier = pltpu.get_barrier_semaphore()
    for d in range(1, size):
        pl.semaphore_signal(
            barrier, inc=1, device_id={"seq": lax.rem(index + d, size)},
            device_id_type=pl.DeviceIdType.MESH,
        )
    pl.semaphore_signal(
        barrier, inc=1, device_id={"head": 1 - core}, device_id_type=pl.DeviceIdType.MESH
    )
    pl.semaphore_wait(barrier, size)


def send_to(src, dst, send_sem, recv_sem, **where):
    return pltpu.make_async_remote_copy(
        src_ref=src, dst_ref=dst, send_sem=send_sem, recv_sem=recv_sem, device_id=where,
        device_id_type=pl.DeviceIdType.MESH,
    )


def transposed(block):
    return block.astype(f32).T.astype(bf16)


def forward_kernel(
    size,
    hid_ref, gain_ref, wi_ref, wstep_ref, wshared_ref, cv_ref, cs_ref, bias_ref, decay_ref,
    skip_ref, ggain_ref, wout_ref, hrow_ref, crow_ref,
    normedt_ref, scale_ref, gate_ref, vext_ref, after_ref, y_ref, gw_ref, in_ref, step_ref,
    slope_ref, run_ref, runt_ref, stept_ref, sext_ref, bc_ref, gains_ref, out_ref, gmt_ref,
    coef_ref,
    nx, halo, halo_sems, scores, bt, end_w, vwide, act_all, gates, ys, states, acc, acc_send,
    acc_land, acc_sems, squares, sq_land, sq_sems, totals, totals_land, totals_sems,
    ex_own, ex_landing, ex_mixed, ex_result, ex_sems,
):
    step_id = pl.program_id(0)
    index = lax.axis_index("seq")
    core = lax.axis_index("head")
    tokens = hid_ref.shape[0]
    width = hid_ref.shape[1]
    chunks = tokens // CHUNK
    nb = act_all.shape[0]
    t_gate, t_mix, t_last = nb, 2 * nb, 3 * nb
    exchange = StateExchange(
        index, size, False, ex_own, ex_landing, ex_mixed, ex_result, ex_sems, gains_ref
    )

    def norm_rows(rows):
        wide = rows.astype(f32)
        scale = lax.rsqrt(jnp.mean(wide * wide, axis=1, keepdims=True) + norm_eps)
        return (wide * scale * gain_ref[...]).astype(bf16), scale

    def totals_copy(d):
        return send_to(
            totals, totals_land.at[size - d - 1], totals_sems.at[0], totals_sems.at[1],
            seq=lax.rem(index + d, size),
        )

    @pl.when(step_id == 0)
    def _():
        @pl.loop(0, chunks)
        def _(i):
            start = pl.multiple_of(i * CHUNK, CHUNK)
            for part in range(2):
                at = pl.multiple_of(start + part * 64, 64)
                rows, scale = norm_rows(hid_ref[pl.ds(at, 64), :])
                nx[pl.ds(pl.multiple_of(HALO + at, HALO), 64), :] = rows
                scale_ref[pl.ds(at, 64), :] = jnp.broadcast_to(scale, (64, LANES))

        greet(index, core, size)
        after_id = lax.rem(index + 1, size)
        halo_copy = send_to(
            hid_ref.at[pl.ds(tokens - HALO, HALO)], halo, halo_sems.at[0], halo_sems.at[1],
            seq=after_id,
        )
        halo_copy.start()
        for c in range(chunks):
            for b in range(width // LANES):
                normedt_ref[b * LANES : (b + 1) * LANES, c * CHUNK : (c + 1) * CHUNK] = transposed(
                    nx[HALO + c * CHUNK : HALO + (c + 1) * CHUNK, b * LANES : (b + 1) * LANES]
                )
        raw = mm(nx[HALO:, :], wstep_ref[...]) + bias_ref[...]
        small = jnp.exp(-jnp.abs(raw))
        step = jnp.maximum(raw, 0.0) + jnp.log1p(small)
        step_ref[...] = step
        slope_ref[...] = 1.0 / (1.0 + jnp.exp(-raw))
        rate = -step * jnp.exp(decay_ref[...])
        tri = causal().astype(f32)
        total = jnp.zeros((1, LANES), f32)
        for c in range(chunks):
            rows = slice(c * CHUNK, (c + 1) * CHUNK)
            run = mm_exact(tri, rate[rows, :])
            run_ref[rows, :] = run
            total = total + run[CHUNK - 1 :, :]
            run_t = run.T
            step_t = step[rows, :].T
            for b in range(nb):
                heads = slice(BLOCK_HEADS * b, BLOCK_HEADS * (b + 1))
                runt_ref[b, 0:BLOCK_HEADS, rows] = run_t[heads, :]
                stept_ref[b, 0:BLOCK_HEADS, rows] = step_t[heads, :]
                runt_ref[b, BLOCK_HEADS:, rows] = jnp.zeros((8 - BLOCK_HEADS, CHUNK), f32)
                stept_ref[b, BLOCK_HEADS:, rows] = jnp.zeros((8 - BLOCK_HEADS, CHUNK), f32)
            end_w[rows, :] = step[rows, :] * jnp.exp(run[CHUNK - 1 :, :] - run)
        totals[...] = jnp.broadcast_to(jnp.exp(total), totals.shape)
        for d in range(1, size):
            totals_copy(d).start()
        halo_copy.wait()
        keep = jnp.where(index == 0, 0.0, 1.0)
        nx[0:HALO, :] = (norm_rows(halo[...])[0].astype(f32) * keep).astype(bf16)
        shared = mm(nx[...], wshared_ref[...]).astype(bf16)
        sext_ref[0] = shared[:, :STATE]
        sext_ref[1] = shared[:, STATE:]
        conv = conv_rows(shared.astype(f32), cs_ref[...], HALO - CONV + 1, tokens)
        act = silu(conv).astype(bf16)
        bc_ref[...] = act
        for c in range(chunks):
            rows = slice(c * CHUNK, (c + 1) * CHUNK)
            b_rows = act[rows, :STATE]
            c_rows = act[rows, STATE:]
            scores[c] = mm(c_rows, b_rows, NT)
            bt[:, rows] = transposed(b_rows)

    @pl.when(step_id < t_gate)
    def _():
        j = step_id
        values = mm(nx[...], wi_ref[0]).astype(bf16)
        vext_ref[...] = values
        vwide[...] = values.astype(f32)
        conv = conv_rows(vwide, cv_ref[...], HALO - CONV + 1, tokens)
        act = silu(conv).astype(bf16)
        act_all[j] = act
        run_cols = rolled(run_ref[...], j)
        end_cols = rolled(end_w[...], j)
        state = jnp.zeros((STATE, BLOCK), f32)
        for c in range(chunks):
            rows = slice(c * CHUNK, (c + 1) * CHUNK)
            weighted = act[rows, :].astype(f32) * widen(end_cols[rows, :BLOCK_HEADS])
            last = widen(jnp.exp(run_cols[(c + 1) * CHUNK - 1 : (c + 1) * CHUNK, :BLOCK_HEADS]))
            state = last * state + mm_right(bt[:, rows], weighted)
            after_ref[c] = state
            states[j, c] = state
        exchange.send(j, state)

    @pl.when((step_id >= t_gate) & (step_id < t_mix))
    def _():
        j = step_id - t_gate
        gate = mm(nx[HALO:, :], wi_ref[0])
        gate_ref[...] = gate
        gates[j] = gate

        @pl.when(j == 0)
        def _():
            pltpu.make_async_remote_copy(
                src_ref=totals_land.at[pl.ds(0, size - 1)],
                dst_ref=totals_land.at[pl.ds(0, size - 1)],
                send_sem=totals_sems.at[0], recv_sem=totals_sems.at[1],
                device_id={"seq": lax.rem(index + 1, size)},
                device_id_type=pl.DeviceIdType.MESH,
            ).wait()
            totals_land[size - 1] = totals[...]
            for source in range(size):
                gains_ref[source : source + 1, :] = totals_land[exchange.slot(source), 0:1, :]

        run_cols = rolled(run_ref[...], j)
        mask = causal()
        skip = widen(rolled(skip_ref[...], j)[:, :BLOCK_HEADS])
        for c in range(chunks):
            rows = slice(c * CHUNK, (c + 1) * CHUNK)
            cols = run_cols[rows, :BLOCK_HEADS]
            x = act_all[j, rows, :]
            y_pairs = []
            for pair in range(BLOCK // LANES):
                mats = []
                for k in range(2):
                    head = 2 * pair + k
                    gap = cols[:, head : head + 1] - runt_ref[j, head : head + 1, rows]
                    decayed = jnp.exp(jnp.where(mask, gap, -1e30))
                    mats.append(scores[c] * decayed * stept_ref[j, head : head + 1, rows])
                low, high = stack_pair(x[:, pair * LANES : (pair + 1) * LANES])
                y_pairs.append(
                    mm_left(jnp.concatenate(mats, axis=1), jnp.concatenate([low, high], axis=0))
                )
            ys[j, rows, :] = jnp.concatenate(y_pairs, axis=1) + skip * x.astype(f32)
        exchange.turn(j)

    @pl.when((step_id >= t_mix) & (step_id < t_last))
    def _():
        j = step_id - t_mix
        entering = exchange.take(j)
        in_ref[...] = entering
        offsets = offsets_of(run_ref, chunks)
        gated = []
        for c in range(chunks):
            rows = slice(c * CHUNK, (c + 1) * CHUNK)
            grow = rolled(jnp.exp(run_ref[rows, :]), j)[:, :BLOCK_HEADS]
            base = rolled(jnp.exp(offsets[c]), j)[:, :BLOCK_HEADS]
            enter = widen(base) * entering
            if c:
                enter = enter + states[j, c - 1]
            y = ys[j, rows, :] + widen(grow) * mm_right(bc_ref[rows, STATE:], enter)
            y_ref[rows, :] = y
            out = y * silu(gates[j, rows, :])
            gw_ref[rows, :] = (out * ggain_ref[...]).astype(bf16)
            gated.append(
                jnp.broadcast_to(jnp.sum(out * out, axis=1, keepdims=True), (CHUNK, LANES))
            )
        part = mm(gw_ref[...], wout_ref[...], NT)
        block_squares = jnp.concatenate(gated, axis=0)

        @pl.when(j == 0)
        def _():
            acc[...] = part
            squares[...] = block_squares

        @pl.when(j > 0)
        def _():
            acc[...] += part
            squares[...] += block_squares

        @pl.when(j == nb - 1)
        def _():
            send_to(squares, sq_land, sq_sems.at[0], sq_sems.at[1], head=1 - core).start()
            for c in range(chunks):
                acc_send[c] = acc[c * CHUNK : (c + 1) * CHUNK, :].astype(bf16)
                send_to(
                    acc_send.at[c], acc_land.at[c], acc_sems.at[0, c], acc_sems.at[1, c],
                    head=1 - core,
                ).start()

    @pl.when(step_id >= t_last)
    def _():
        c = step_id - t_last

        @pl.when(c == 0)
        def _():
            send_to(squares, sq_land, sq_sems.at[0], sq_sems.at[1], head=1 - core).wait()

        send_to(
            acc_send.at[c], acc_land.at[c], acc_sems.at[0, c], acc_sems.at[1, c], head=1 - core
        ).wait()
        rows = pl.ds(pl.multiple_of(c * CHUNK, CHUNK), CHUNK)
        mixed = acc[rows, :] + acc_land[c].astype(f32)
        inverse = lax.rsqrt((squares[rows, 0:1] + sq_land[rows, 0:1]) / INNER + norm_eps)
        out_ref[...] = hrow_ref[...].astype(f32) + mixed * inverse
        cot = crow_ref[...].astype(f32)
        scaled = (cot * inverse).astype(bf16)
        for b in range(width // LANES):
            gmt_ref[b * LANES : (b + 1) * LANES, :] = transposed(
                scaled[:, b * LANES : (b + 1) * LANES]
            )
        grad_inverse = jnp.sum(cot * mixed, axis=1, keepdims=True)
        coef_ref[:, 0:LANES] = jnp.broadcast_to(
            grad_inverse * inverse * inverse * inverse / INNER, (CHUNK, LANES)
        )
        coef_ref[:, LANES:] = jnp.broadcast_to(inverse, (CHUNK, LANES))


def offsets_of(run_ref, chunks):
    rows = [jnp.zeros((1, LANES), f32)]
    for c in range(chunks):
        rows.append(rows[-1] + run_ref[(c + 1) * CHUNK - 1 : (c + 1) * CHUNK, :])
    return rows


def forward_call(
    hidden, cotangent, gain, both, wstep, wshared, conv_values, conv_shared, bias, decay, skip,
    gate_gain, wout,
):
    tokens, width = hidden.shape
    inner = both.shape[2]
    chunks = tokens // CHUNK
    nb = inner // BLOCK
    size = lax.axis_size("seq")
    t_gate, t_mix, t_last = nb, 2 * nb, 3 * nb

    def at(start):
        return lambda s: jnp.clip(s - start, 0, nb - 1)

    def full(shape):
        return pl.BlockSpec(shape, lambda s: (0,) * len(shape), pipeline_mode=pl.Buffered(1))

    def cols(rows, start):
        return pl.BlockSpec((rows, BLOCK), lambda s: (0, at(start)(s)))

    row_of = lambda s: jnp.clip(s - t_last, 0, chunks - 1)
    row_block = lambda w: pl.BlockSpec((CHUNK, w), lambda s: (row_of(s), 0))
    outs = [
        ((width, tokens), bf16, full((width, tokens))),
        ((tokens, LANES), f32, full((tokens, LANES))),
        ((tokens, inner), f32, cols(tokens, t_gate)),
        ((HALO + tokens, inner), bf16, cols(HALO + tokens, 0)),
        (
            (chunks, STATE, inner), f32,
            pl.BlockSpec((chunks, STATE, BLOCK), lambda s: (0, 0, at(0)(s))),
        ),
        ((tokens, inner), f32, cols(tokens, t_mix)),
        ((tokens, inner), bf16, cols(tokens, t_mix)),
        ((STATE, inner), f32, cols(STATE, t_mix)),
        ((tokens, LANES), f32, full((tokens, LANES))),
        ((tokens, LANES), f32, full((tokens, LANES))),
        ((tokens, LANES), f32, full((tokens, LANES))),
        ((nb, 8, tokens), f32, full((nb, 8, tokens))),
        ((nb, 8, tokens), f32, full((nb, 8, tokens))),
        ((2, HALO + tokens, STATE), bf16, full((2, HALO + tokens, STATE))),
        ((tokens, 2 * STATE), bf16, full((tokens, 2 * STATE))),
        ((size, LANES), f32, full((size, LANES))),
        ((tokens, width), f32, row_block(width)),
        ((width, tokens), bf16, pl.BlockSpec((width, CHUNK), lambda s: (0, row_of(s)))),
        ((tokens, 2 * LANES), f32, row_block(2 * LANES)),
    ]
    sem = pltpu.SemaphoreType.DMA
    return pl.pallas_call(
        functools.partial(forward_kernel, size),
        grid=(3 * nb + chunks,),
        in_specs=[
            full((tokens, width)),
            full((1, width)),
            pl.BlockSpec(
                (1, width, BLOCK),
                lambda s: (jnp.where(s < t_gate, 1, 0), 0, jnp.where(s < t_gate, at(0)(s), at(t_gate)(s))),
            ),
            full((width, LANES)),
            full((width, 2 * STATE)),
            cols(CONV + 1, 0),
            full((CONV + 1, 2 * STATE)),
            full((1, LANES)),
            full((1, LANES)),
            full((1, LANES)),
            cols(1, t_mix),
            cols(width, t_mix),
            row_block(width),
            row_block(width),
        ],
        out_shape=[jax.ShapeDtypeStruct(shape, kind) for shape, kind, _ in outs],
        out_specs=[spec for _, _, spec in outs],
        scratch_shapes=[
            pltpu.VMEM((HALO + tokens, width), bf16),
            pltpu.VMEM((HALO, width), bf16),
            sem((2,)),
            pltpu.VMEM((chunks, CHUNK, CHUNK), f32),
            pltpu.VMEM((STATE, tokens), bf16),
            pltpu.VMEM((tokens, LANES), f32),
            pltpu.VMEM((HALO + tokens, BLOCK), f32),
            pltpu.VMEM((nb, tokens, BLOCK), bf16),
            pltpu.VMEM((nb, tokens, BLOCK), f32),
            pltpu.VMEM((nb, tokens, BLOCK), f32),
            pltpu.VMEM((nb, chunks, STATE, BLOCK), f32),
            pltpu.VMEM((tokens, width), f32),
            pltpu.VMEM((chunks, CHUNK, width), bf16),
            pltpu.VMEM((chunks, CHUNK, width), bf16),
            sem((2, chunks)),
            pltpu.VMEM((tokens, LANES), f32),
            pltpu.VMEM((tokens, LANES), f32),
            sem((2,)),
            pltpu.VMEM((8, LANES), f32),
            pltpu.VMEM((size, 8, LANES), f32),
            sem((2,)),
        ] + exchange_scratch(nb, size, f32),
        compiler_params=pltpu.CompilerParams(
            collective_id=1, has_side_effects=True, vmem_limit_bytes=67043328
        ),
        name="forward",
    )(
        hidden, gain, both, wstep, wshared, conv_values, conv_shared, bias, decay, skip, gate_gain,
        wout, hidden, cotangent,
    )


def order_bits(part, bits):
    order = list(range(bits))
    if part == 1 and bits > 1:
        order[0], order[1] = 1, 0
    return order


def slot_of(owner, part, bits):
    slot = 0
    for bit in order_bits(part, bits):
        slot = slot * 2 + ((owner >> bit) & 1)
    return slot


class Reduction:
    def __init__(self, held, landing, out, part, bits, index, send_sems, recv_sems, cols):
        self.held, self.landing, self.out = held, landing, out
        self.part, self.bits, self.index = part, bits, index
        self.send_sems, self.recv_sems, self.cols = send_sems, recv_sems, cols

    def place(self, stage):
        base = 0
        size = 1 << self.bits
        for s, bit in enumerate(order_bits(self.part, self.bits)[: stage + 1]):
            mine = (self.index // (1 << bit)) % 2
            half = size >> (s + 1)
            keep, give = base + mine * half, base + (1 - mine) * half
            base = keep
        return keep, give, half, order_bits(self.part, self.bits)[stage]

    def copy(self, stage):
        _, give, half, bit = self.place(stage)
        mine = (self.index // (1 << bit)) % 2
        partner = self.index + (1 - 2 * mine) * (1 << bit)
        return pltpu.make_async_remote_copy(
            src_ref=self.held.at[pl.ds(give, half)],
            dst_ref=self.landing[stage],
            send_sem=self.send_sems.at[stage],
            recv_sem=self.recv_sems.at[stage],
            device_id={"seq": partner},
            device_id_type=pl.DeviceIdType.MESH,
        )

    def start(self, stage):
        self.copy(stage).start()

    def finish(self, stage):
        self.copy(stage).wait()
        keep, _, half, _ = self.place(stage)
        if stage == self.bits - 1:
            self.out[:, self.cols] = self.held[keep].astype(f32) + self.landing[stage][0].astype(f32)
        else:

            @pl.loop(0, half)
            def _(i):
                total = self.held[keep + i].astype(f32) + self.landing[stage][i].astype(f32)
                self.held[keep + i] = total.astype(bf16)

    def advance(self, stage):
        self.finish(stage)
        if stage + 1 < self.bits:
            self.start(stage + 1)


def sum_copy(acc, landing, bit, index, sems):
    mine = (index // (1 << bit)) % 2
    return pltpu.make_async_remote_copy(
        src_ref=acc.at[bit],
        dst_ref=landing.at[bit],
        send_sem=sems.at[0, bit],
        recv_sem=sems.at[1, bit],
        device_id={"seq": index + (1 - 2 * mine) * (1 << bit)},
        device_id_type=pl.DeviceIdType.MESH,
    )


def back_kernel(
    bits,
    gmt_ref, normedt_ref, coef_ref, gains_ref, run_ref, step_ref, slope_ref, bc_ref, sext_ref, skip_ref,
    decay_ref, cs_ref, wsmall_ref, gain_ref,
    wout_ref, y_ref, gate_ref, ggain_ref, gw_ref, vext_ref, after_ref, in_ref, cv_ref, runt_ref,
    stept_ref, wi_ref,
    hid_ref, cot_ref, scale_ref,
    gout_ref, ggw_ref, gvw_ref, gsmall_ref, ghid_ref, sums_ref, heads_ref,
    w_out, w_gate, w_values, w_small,
    land_out, land_gate, land_values, land_small,
    rs_send, rs_recv,
    gv, acc_send, acc_land, acc_sems,
    edge_own, edge_tail, edge_land, edge_sems,
    dbc, dbc_land, dbc_sems, small, sedge_own, sedge_land, sedge_sems,
    vec, vec_land, vec_sems,
    scores, scorest, ct, dscores, end_w, ends, dcols, xdu, dyc, xdus, vwide, gext,
    dys, ggates, term_gate, ex_own, ex_landing, ex_mixed, ex_result, ex_sems,
):
    step_id = pl.program_id(0)
    index = lax.axis_index("seq")
    core = lax.axis_index("head")
    size = 1 << bits
    tokens = y_ref.shape[0]
    chunks = tokens // CHUNK
    nb = w_out.shape[0] * w_out.shape[3] // BLOCK
    half_nb = nb // 2
    width = normedt_ref.shape[0]
    rows_own = width // size
    part_cols = w_out.shape[3]
    t_out, t_gate, t_scan, t_values, t_grad, t_final = (nb * i for i in range(1, 7))
    after_id = lax.rem(index + 1, size)
    before_id = lax.rem(index + size - 1, size)

    def reduction(g, part):
        held, landing, out = (
            (w_out, land_out, gout_ref), (w_gate, land_gate, ggw_ref), (w_values, land_values, gvw_ref),
        )[g]
        land = [ref.at[part] for ref in landing]
        slot = 2 * g + part
        return Reduction(
            held.at[part], land, out, part, bits, index, rs_send.at[slot], rs_recv.at[slot],
            pl.ds(part * part_cols, part_cols),
        )

    rs = [[reduction(g, part) for part in range(2)] for g in range(3)]
    rs_small = Reduction(
        w_small, list(land_small), gsmall_ref, 1, bits, index, rs_send.at[6], rs_recv.at[6],
        pl.ds(0, w_small.shape[2]),
    )

    def when_after(step):
        return pl.when(step_id == step)

    exchange = StateExchange(
        index, size, True, ex_own, ex_landing, ex_mixed, ex_result, ex_sems, gains_ref
    )

    @pl.when(step_id == 0)
    def _():
        greet(index, core, size)
        for c in range(chunks):
            rows = slice(c * CHUNK, (c + 1) * CHUNK)
            ct[:, rows] = transposed(bc_ref[rows, STATE:])
            for b in range(width // LANES):
                acc_send[c, :, b * LANES : (b + 1) * LANES] = transposed(
                    gmt_ref[b * LANES : (b + 1) * LANES, rows]
                )

    @pl.when(step_id < t_out)
    def _():
        j = step_id
        offsets = offsets_of(run_ref, chunks)
        own = jnp.zeros((STATE, BLOCK), f32)
        term = jnp.zeros((1, BLOCK), f32)
        for c in range(chunks):
            rows = slice(c * CHUNK, (c + 1) * CHUNK)
            ggw = mm(acc_send[c], wout_ref[...])
            y = y_ref[rows, :]
            gate = gate_ref[rows, :]
            sig = 1.0 / (1.0 + jnp.exp(-gate))
            act = gate * sig
            out = y * act
            term = term + jnp.sum(ggw * out, axis=0, keepdims=True)
            coef = jnp.concatenate([coef_ref[rows, 0:LANES]] * (BLOCK // LANES), axis=1)
            gg = ggw * ggain_ref[...] - coef * out
            dy = gg * act
            dys[j, rows, :] = dy
            ggates[j, rows, :] = (gg * y * (sig * (1.0 + gate * (1.0 - sig)))).astype(bf16)
            grow = rolled(jnp.exp(run_ref[rows, :] + offsets[c]), j)[:, :BLOCK_HEADS]
            own = own + mm_right(ct[:, rows], dy * widen(grow))
        term_gate[j, 0:1, :] = term
        exchange.send(j, own)

    def put_block(held, left, right, j):
        part = j // half_nb
        cols = pl.ds(pl.multiple_of((j % half_nb) * BLOCK, BLOCK), BLOCK)
        group = width // 4
        for q in range(4):
            piece = mm(left[q * group : (q + 1) * group, :], right).astype(bf16)
            for b in range(size // 4):
                owner = q * (size // 4) + b
                slots = [slot_of(owner, p, bits) for p in range(2)]
                slot = slots[0] + part * (slots[1] - slots[0])
                held[part, slot, :, cols] = piece[b * rows_own : (b + 1) * rows_own, :]

    @pl.when((step_id >= t_out) & (step_id < t_gate))
    def _():
        j = step_id - t_out
        put_block(w_out, gmt_ref, gw_ref[...], j)
        exchange.turn(j)

    @pl.when((step_id >= t_gate) & (step_id < t_scan))
    def _():
        j = step_id - t_gate
        put_block(w_gate, normedt_ref, ggates[j], j)

    @when_after(t_out + half_nb - 1)
    def _():
        rs[0][0].start(0)

    @when_after(t_gate - 1)
    def _():
        rs[0][1].start(0)

    @when_after(t_gate + half_nb - 1)
    def _():
        rs[1][0].start(0)

    @when_after(t_scan - 1)
    def _():
        rs[1][1].start(0)

    mask = causal()
    rows_i = lax.broadcasted_iota(jnp.int32, (CHUNK, CHUNK), 0)
    cols_i = lax.broadcasted_iota(jnp.int32, (CHUNK, CHUNK), 1)
    mask_t = rows_i <= cols_i

    @pl.when(step_id == t_scan)
    def _():
        dbc[...] = jnp.zeros_like(dbc)
        dscores[...] = jnp.zeros_like(dscores)
        dcols[...] = jnp.zeros_like(dcols)
        xdu[...] = jnp.zeros_like(xdu)
        dyc[...] = jnp.zeros_like(dyc)
        xdus[...] = jnp.zeros_like(xdus)
        ends[...] = jnp.zeros_like(ends)
        vec[...] = jnp.zeros_like(vec)
        for c in range(chunks):
            rows = slice(c * CHUNK, (c + 1) * CHUNK)
            b_rows = bc_ref[rows, :STATE]
            c_rows = bc_ref[rows, STATE:]
            scores[c] = mm(c_rows, b_rows, NT)
            scorest[c] = mm(b_rows, c_rows, NT)
            run = run_ref[rows, :]
            end_w[rows, :] = jnp.exp(run[CHUNK - 1 :, :] - run)

    @pl.when((step_id >= t_scan) & (step_id < t_values))
    def _():
        j = step_id - t_scan
        offsets = offsets_of(run_ref, chunks)
        vwide[...] = vext_ref[...].astype(f32)
        conv = conv_rows(vwide, cv_ref[...], HALO - CONV + 1, tokens)
        sig_all = 1.0 / (1.0 + jnp.exp(-conv))
        act = (conv * sig_all).astype(bf16)
        slope = sig_all * (1.0 + conv * (1.0 - sig_all))
        run_cols = rolled(run_ref[...], j)
        step_cols = rolled(step_ref[...], j)
        end_cols = rolled(end_w[...], j)
        skip = widen(rolled(skip_ref[...], j)[:, :BLOCK_HEADS])
        channel = lax.broadcasted_iota(jnp.int32, (BLOCK, LANES), 0) // HEAD_DIM
        lane = lax.broadcasted_iota(jnp.int32, (BLOCK, LANES), 1)
        pick = (lane == BLOCK_HEADS * j + channel).astype(bf16)
        lane_row = lax.broadcasted_iota(jnp.int32, (CHUNK, LANES), 1)
        dstate = exchange.take(j)
        dskip = jnp.zeros((1, BLOCK), f32)
        gext[tokens : tokens + 8, :] = jnp.zeros((8, BLOCK), f32)
        for c in reversed(range(chunks)):
            rows = slice(c * CHUNK, (c + 1) * CHUNK)
            cols = run_cols[rows, :BLOCK_HEADS]
            x = act[rows, :]
            wide_x = x.astype(f32)
            dy = dys[j, rows, :]
            b_rows = bc_ref[rows, :STATE]
            c_rows = bc_ref[rows, STATE:]
            grow = widen(jnp.exp(cols))
            tail = widen(end_cols[rows, :BLOCK_HEADS])
            step_w = widen(step_cols[rows, :BLOCK_HEADS])
            last = grow[CHUNK - 1 :, :]
            base = rolled(jnp.exp(offsets[c]), j)[:, :BLOCK_HEADS]
            enter = widen(base) * in_ref[...]
            if c:
                enter = enter + after_ref[c - 1]
            du_state = tail * mm_right(b_rows, dstate)
            carried = grow * mm_right(c_rows, enter)
            weighted = wide_x * (tail * step_w)
            grown = dy * grow
            dbc[0, rows, :] += mm_both(weighted, dstate, NT)
            dbc[1, rows, :] += mm_both(grown, enter, NT)
            hold = last * jnp.sum(dstate * enter, axis=0, keepdims=True)
            ends[c : c + 1, :] += mm_exact(
                jnp.broadcast_to(hold, (8, BLOCK)), pick.astype(f32)
            )[:1, :]
            dstate = last * dstate + mm_right(ct[:, rows], grown)
            du_pairs = []
            col_sum = jnp.zeros((CHUNK, LANES), f32)
            for pair in range(BLOCK // LANES):
                lanes = slice(pair * LANES, (pair + 1) * LANES)
                low, high = stack_pair(dy[:, lanes])
                both = jnp.concatenate([low, high], axis=0)
                dmat = mm_left(both, x[:, lanes], NT)
                mats = []
                for k in range(2):
                    head = 2 * pair + k
                    col = cols[:, head : head + 1]
                    row = runt_ref[0, head : head + 1, rows]
                    keep = jnp.exp(jnp.where(mask, col - row, -1e30))
                    piece = dmat[k * CHUNK : (k + 1) * CHUNK, :] * keep
                    piece = piece * stept_ref[0, head : head + 1, rows]
                    dscores[c] += piece
                    full = piece * scores[c]
                    col_sum = jnp.where(
                        lane_row == BLOCK_HEADS * j + head,
                        jnp.sum(full, axis=1, keepdims=True),
                        col_sum,
                    )
                    dcols[j, head : head + 1, rows] = jnp.sum(full, axis=0, keepdims=True)
                    keep_t = jnp.exp(jnp.where(mask_t, row - col, -1e30))
                    mats.append(scorest[c] * keep_t)
                du_pairs.append(mm_both(jnp.concatenate(mats, axis=1), both))
            dyc[rows, :] += col_sum
            du = jnp.concatenate(du_pairs, axis=1) + du_state
            xdu[rows, :] += mm_left(wide_x * du, pick)
            dyc[rows, :] += mm_left(dy * carried, pick)
            xdus[rows, :] += mm_left(wide_x * du_state, pick)
            dskip = dskip + jnp.sum(dy * wide_x, axis=0, keepdims=True)
            gext[rows, :] = (step_w * du + skip * dy) * slope[rows, :]
        gconv = gext[0:tokens, :]
        for k in range(CONV):
            first = HALO - CONV + 1 + k
            vec[0, j, k : k + 1, :] = jnp.sum(
                vwide[first : first + tokens, :] * gconv, axis=0, keepdims=True
            )
        vec[0, j, CONV : CONV + 1, :] = jnp.sum(gconv, axis=0, keepdims=True)
        vec[0, j, CONV + 1 : CONV + 2, :] = term_gate[j, 0:1, :]
        vec[0, j, CONV + 2 : CONV + 3, :] = dskip
        total = cv_ref[CONV - 1 : CONV, :] * gconv
        for k in range(CONV - 1):
            total = total + cv_ref[k : k + 1, :] * gext[CONV - 1 - k : CONV - 1 - k + tokens, :]
        gv[j] = total.astype(bf16)
        lacking = jnp.zeros((8, BLOCK), f32)
        edge_tail[j] = total[tokens - 8 :, :] + lacking
        edge_own[j] = gconv[0:8, :]
        send_to(
            edge_own.at[j], edge_land.at[j], edge_sems.at[0, j], edge_sems.at[1, j], seq=before_id
        ).start()

    @when_after(t_scan + half_nb)
    def _():
        rs[0][0].advance(0)
        rs[0][1].advance(0)

    @when_after(t_values - 1)
    def _():
        tri = mask.astype(f32)
        tri_t = mask_t.astype(f32)
        strict = (rows_i > cols_i).astype(f32)
        decay = jnp.exp(decay_ref[...])
        bias_sum = jnp.zeros((1, LANES), f32)
        decay_sum = jnp.zeros((1, LANES), f32)
        for c in range(chunks):
            rows = slice(c * CHUNK, (c + 1) * CHUNK)
            step = step_ref[rows, :]
            col_rows = [dcols[b, 0:BLOCK_HEADS, rows] for b in range(nb)]
            rest = LANES - BLOCK_HEADS * nb
            col_rows.append(jnp.zeros((rest, CHUNK), f32))
            dlog = dyc[rows, :] - jnp.concatenate(col_rows, axis=0).T
            drate = (
                mm_exact(tri_t, dlog)
                + mm_exact(strict, xdus[rows, :] * step)
                + ends[c : c + 1, :]
            )
            dstep = xdu[rows, :] - decay * drate
            draw = dstep * slope_ref[rows, :]
            small[rows, LANES:] = draw.astype(bf16)
            bias_sum = bias_sum + jnp.sum(draw, axis=0, keepdims=True)
            decay_sum = decay_sum - jnp.sum(drate * step, axis=0, keepdims=True) * decay
            b_rows = bc_ref[rows, :STATE]
            c_rows = bc_ref[rows, STATE:]
            high, low = parts(dscores[c])
            dbc[1, rows, :] += mm(high, b_rows) + mm(low, b_rows)
            dbc[0, rows, :] += mm(high, c_rows, TN) + mm(low, c_rows, TN)
        vec[0, nb, 0:1, 0:LANES] = bias_sum
        vec[0, nb, 1:2, 0:LANES] = decay_sum
        send_to(
            dbc.at[1 - core], dbc_land, dbc_sems.at[0], dbc_sems.at[1], head=1 - core
        ).start()

    @pl.when((step_id >= t_values) & (step_id < t_grad))
    def _():
        j = step_id - t_values
        send_to(
            edge_own.at[j], edge_land.at[j], edge_sems.at[0, j], edge_sems.at[1, j], seq=before_id
        ).wait()
        cv = cv_ref[...]
        nxt = jnp.where(index == size - 1, 0.0, 1.0) * edge_land[j]
        row8 = lax.broadcasted_iota(jnp.int32, (8, BLOCK), 0)
        fix = edge_tail[j]
        for k in range(CONV - 1):
            ahead = CONV - 1 - k
            moved = pltpu.roll(nxt, 8 - ahead, 0)
            fix = fix + jnp.where(row8 >= 8 - ahead, cv[k : k + 1, :] * moved, 0.0)
        both_rows = jnp.concatenate([gv[j, tokens - 16 : tokens - 8, :].astype(f32), fix], axis=0)
        gv[j, tokens - 16 :, :] = both_rows.astype(bf16)
        put_block(w_values, normedt_ref, gv[j], j)

    @when_after(t_values + half_nb - 1)
    def _():
        rs[2][0].start(0)

    @when_after(t_values)
    def _():
        send_to(
            dbc.at[1 - core], dbc_land, dbc_sems.at[0], dbc_sems.at[1], head=1 - core
        ).wait()
        sext = sext_ref[core].astype(f32)
        taps = cs_ref[core]
        conv = conv_rows(sext, taps, HALO - CONV + 1, tokens)
        gs = (dbc[core] + dbc_land[...]) * silu_grad(conv)
        for k in range(CONV):
            first = HALO - CONV + 1 + k
            vec[0, nb, 2 + k : 3 + k, 0:LANES] = jnp.sum(
                sext[first : first + tokens, :] * gs, axis=0, keepdims=True
            )
        vec[0, nb, 2 + CONV : 3 + CONV, 0:LANES] = jnp.sum(gs, axis=0, keepdims=True)
        dbc[core] = gs
        sedge_own[...] = gs[0:8, :]
        send_to(
            sedge_own, sedge_land, sedge_sems.at[0], sedge_sems.at[1], seq=before_id
        ).start()

    @when_after(t_grad - 1)
    def _():
        rs[2][1].start(0)
        send_to(
            sedge_own, sedge_land, sedge_sems.at[0], sedge_sems.at[1], seq=before_id
        ).wait()
        taps = cs_ref[core]
        nxt = jnp.where(index == size - 1, 0.0, 1.0) * sedge_land[...]
        gs = jnp.concatenate([dbc[core], nxt], axis=0)
        total = taps[CONV - 1 : CONV, :] * gs[0:tokens, :]
        for k in range(CONV - 1):
            total = total + taps[k : k + 1, :] * gs[CONV - 1 - k : CONV - 1 - k + tokens, :]
        small[:, 0:LANES] = total.astype(bf16)
        group = width // 4
        for q in range(4):
            piece = mm(normedt_ref[q * group : (q + 1) * group, :], small[...]).astype(bf16)
            for b in range(size // 4):
                slot = slot_of(q * (size // 4) + b, 1, bits)
                w_small[slot] = piece[b * rows_own : (b + 1) * rows_own, :]
        rs_small.start(0)

    @pl.when((step_id >= t_grad) & (step_id < t_final))
    def _():
        j = step_id - t_grad
        part = mm(ggates[j], wi_ref[0], NT) + mm(gv[j], wi_ref[1], NT)

        @pl.when(j == 0)
        def _():
            first = part + mm(small[...], wsmall_ref[...], NT)
            for b in range(width // BLOCK):
                dys[b] = first[:, b * BLOCK : (b + 1) * BLOCK]

        @pl.when(j > 0)
        def _():
            for b in range(width // BLOCK):
                dys[b] += part[:, b * BLOCK : (b + 1) * BLOCK]

    @when_after(t_grad + half_nb)
    def _():
        rs[1][0].advance(0)
        rs[1][1].advance(0)

    @when_after(t_final - 1)
    def _():
        for c in range(chunks):
            rows = slice(c * CHUNK, (c + 1) * CHUNK)
            for b in range(width // BLOCK):
                acc_send[c, :, b * BLOCK : (b + 1) * BLOCK] = dys[b, rows, :].astype(bf16)
            send_to(
                acc_send.at[c], acc_land.at[c], acc_sems.at[0, c], acc_sems.at[1, c], head=1 - core
            ).start()

    @pl.when(step_id >= t_final)
    def _():
        c = step_id - t_final
        send_to(
            acc_send.at[c], acc_land.at[c], acc_sems.at[0, c], acc_sems.at[1, c], head=1 - core
        ).wait()
        here = pl.ds(pl.multiple_of(c * CHUNK, CHUNK), CHUNK)
        own_total = jnp.concatenate([dys[b, here, :] for b in range(width // BLOCK)], axis=1)
        total = own_total + acc_land[c].astype(f32)
        scale = scale_ref[:, 0:1]
        hat = hid_ref[...].astype(f32) * scale
        term = jnp.sum(total * hat, axis=0, keepdims=True)

        for b in range(width // BLOCK):
            piece = term[:, b * BLOCK : (b + 1) * BLOCK]
            vec[0, b, 7:8, :] = vec[0, b, 7:8, :] + piece

        ghat = total * gain_ref[...]
        mean = jnp.mean(ghat * hat, axis=1, keepdims=True)
        ghid_ref[...] = cot_ref[...].astype(f32) + scale * (ghat - hat * mean)

    @when_after(t_final + chunks - 1)
    def _():
        def add(bit):
            sum_copy(vec, vec_land, bit, index, vec_sems).wait()
            vec[bit + 1] = vec[bit] + vec_land[bit]

        for stage in range(1, bits):
            sum_copy(vec, vec_land, stage - 1, index, vec_sems).start()
            for g in range(2):
                for part in range(2):
                    rs[g][part].advance(stage)
            for part in range(2):
                rs[2][part].advance(stage - 1)
            rs_small.advance(stage - 1)
            add(stage - 1)
        sum_copy(vec, vec_land, bits - 1, index, vec_sems).start()
        for part in range(2):
            rs[2][part].advance(bits - 1)
        rs_small.advance(bits - 1)
        add(bits - 1)
        heads_ref[...] = vec[bits, nb, :, 0:LANES]
        for b in range(nb):
            sums_ref[:, b * BLOCK : (b + 1) * BLOCK] = vec[bits, b]


def back_call(
    gm_t, normed_t, coef, gains, run, step, slope, bc, sext, skip, decay, conv_shared, wsmall, gain,
    wout, y, gate, gate_gain, gated_w, vext, after, state_in, conv_values, runt, stept, both,
    hidden, cotangent, scale,
):
    width, tokens = normed_t.shape
    inner = y.shape[1]
    chunks = tokens // CHUNK
    nb = inner // BLOCK
    size = lax.axis_size("seq")
    bits = size.bit_length() - 1
    rows_own = width // size
    t_out, t_gate, t_scan, t_values, t_grad, t_final = (nb * i for i in range(1, 7))

    def column(start):
        return lambda s: jnp.clip(s - start, 0, nb - 1)

    def full(shape):
        return pl.BlockSpec(shape, lambda s: (0,) * len(shape), pipeline_mode=pl.Buffered(1))

    def cols(rows, start):
        at = column(start)
        return pl.BlockSpec((rows, BLOCK), lambda s: (0, at(s)))

    def scan_or_values(s):
        return jnp.where(s < t_values, column(t_scan)(s), column(t_values)(s))

    row_block = lambda w: pl.BlockSpec((CHUNK, w), lambda s: (jnp.clip(s - t_final, 0, chunks - 1), 0))
    row_single = lambda w: pl.BlockSpec(
        (CHUNK, w),
        lambda s: (jnp.clip(s - t_final, 0, chunks - 1), 0),
        pipeline_mode=pl.Buffered(1),
    )
    part_cols = inner // 2
    held = lambda: pltpu.VMEM((2, size, rows_own, part_cols), bf16)
    landing = lambda: tuple(
        pltpu.VMEM((2, size >> (s + 1), rows_own, part_cols), bf16) for s in range(bits)
    )
    sem = pltpu.SemaphoreType.DMA
    return pl.pallas_call(
        functools.partial(back_kernel, bits),
        grid=(6 * nb + chunks,),
        in_specs=[
            full((width, tokens)),
            full((width, tokens)),
            full((tokens, LANES)),
            full((size, LANES)),
            full((tokens, LANES)),
            full((tokens, LANES)),
            full((tokens, LANES)),
            full((tokens, 2 * STATE)),
            full((2, HALO + tokens, LANES)),
            full((1, LANES)),
            full((1, LANES)),
            full((2, CONV + 1, LANES)),
            full((width, 2 * LANES)),
            full((1, width)),
            cols(width, 0),
            cols(tokens, 0),
            cols(tokens, 0),
            cols(1, 0),
            cols(tokens, t_out),
            pl.BlockSpec(
                (HALO + tokens, BLOCK), lambda s: (0, column(t_scan)(s)), pipeline_mode=pl.Buffered(1)
            ),
            pl.BlockSpec((chunks, STATE, BLOCK), lambda s: (0, 0, column(t_scan)(s))),
            cols(STATE, t_scan),
            pl.BlockSpec((CONV + 1, BLOCK), lambda s: (0, scan_or_values(s))),
            pl.BlockSpec((1, 8, tokens), lambda s: (column(t_scan)(s), 0, 0)),
            pl.BlockSpec((1, 8, tokens), lambda s: (column(t_scan)(s), 0, 0)),
            pl.BlockSpec(
                (2, width, BLOCK), lambda s: (0, 0, column(t_grad)(s)), pipeline_mode=pl.Buffered(1)
            ),
            row_single(width),
            row_single(width),
            row_block(LANES),
        ],
        out_shape=[
            jax.ShapeDtypeStruct((rows_own, inner), f32),
            jax.ShapeDtypeStruct((rows_own, inner), f32),
            jax.ShapeDtypeStruct((rows_own, inner), f32),
            jax.ShapeDtypeStruct((rows_own, 2 * LANES), f32),
            jax.ShapeDtypeStruct((tokens, width), f32),
            jax.ShapeDtypeStruct((8, inner), f32),
            jax.ShapeDtypeStruct((8, LANES), f32),
        ],
        out_specs=[
            full((rows_own, inner)),
            full((rows_own, inner)),
            full((rows_own, inner)),
            full((rows_own, 2 * LANES)),
            row_block(width),
            pl.BlockSpec((8, inner), lambda s: (0, 0)),
            pl.BlockSpec((8, LANES), lambda s: (0, 0)),
        ],
        scratch_shapes=[
            held(), held(), held(),
            pltpu.VMEM((size, rows_own, 2 * LANES), bf16),
            landing(), landing(), landing(),
            tuple(pltpu.VMEM((size >> (s + 1), rows_own, 2 * LANES), bf16) for s in range(bits)),
            sem((7, bits)), sem((7, bits)),
            pltpu.VMEM((nb, tokens, BLOCK), bf16),
            pltpu.VMEM((chunks, CHUNK, width), bf16),
            pltpu.VMEM((chunks, CHUNK, width), bf16),
            sem((2, chunks)),
            pltpu.VMEM((nb, 8, BLOCK), f32),
            pltpu.VMEM((nb, 8, BLOCK), f32),
            pltpu.VMEM((nb, 8, BLOCK), f32),
            sem((2, nb)),
            pltpu.VMEM((2, tokens, LANES), f32),
            pltpu.VMEM((tokens, LANES), f32),
            sem((2,)),
            pltpu.VMEM((tokens, 2 * LANES), bf16),
            pltpu.VMEM((8, LANES), f32),
            pltpu.VMEM((8, LANES), f32),
            sem((2,)),
            pltpu.VMEM((bits + 1, nb + 1, 8, BLOCK), f32),
            pltpu.VMEM((bits, nb + 1, 8, BLOCK), f32),
            sem((2, bits)),
            pltpu.VMEM((chunks, CHUNK, CHUNK), f32),
            pltpu.VMEM((chunks, CHUNK, CHUNK), f32),
            pltpu.VMEM((STATE, tokens), bf16),
            pltpu.VMEM((chunks, CHUNK, CHUNK), f32),
            pltpu.VMEM((tokens, LANES), f32),
            pltpu.VMEM((8, LANES), f32),
            pltpu.VMEM((nb, 8, tokens), f32),
            pltpu.VMEM((tokens, LANES), f32),
            pltpu.VMEM((tokens, LANES), f32),
            pltpu.VMEM((tokens, LANES), f32),
            pltpu.VMEM((HALO + tokens, BLOCK), f32),
            pltpu.VMEM((tokens + 8, BLOCK), f32),
            pltpu.VMEM((nb, tokens, BLOCK), f32),
            pltpu.VMEM((nb, tokens, BLOCK), bf16),
            pltpu.VMEM((nb, 8, BLOCK), f32),
        ] + exchange_scratch(nb, size, bf16),
        compiler_params=pltpu.CompilerParams(
            collective_id=3, has_side_effects=True, vmem_limit_bytes=67043328
        ),
        name="back",
    )(
        gm_t, normed_t, coef, gains, run, step, slope, bc, sext, skip, decay, conv_shared, wsmall,
        gain, wout, y, gate, gate_gain, gated_w, vext, after, state_in, conv_values, runt, stept,
        both, hidden, cotangent, scale,
    )


def body(
    hidden, cotangent, norm_gain, proj_inner, proj_step, proj_shared, conv_values, conv_shared,
    step_bias, decay_log, skip_gain, gate_gain, proj_out,
):
    tokens = hidden.shape[0]
    inner = proj_inner.shape[2]
    heads = proj_step.shape[1]
    width = hidden.shape[1]
    size = lax.axis_size("seq")
    shared_here = conv_shared.shape[1] // lax.axis_size("head")
    shared_start = lax.axis_index("head") * shared_here
    both = jnp.transpose(proj_inner, (1, 0, 2))
    lanes = lambda v: jnp.pad(v, (0, LANES - heads))[None, :]
    wstep = jnp.pad(proj_step, ((0, 0), (0, LANES - heads)))
    bias, decay, skip = lanes(step_bias), lanes(decay_log), lanes(skip_gain)
    wshared_own = lax.dynamic_slice_in_dim(proj_shared, shared_start, shared_here, 1)
    (
        normed_t, norm_scale, gate_in, vext, after, y, gated_w, state_in, step, slope, run, runt,
        stept, sext, bc, gains, block_out, gm_t, coef,
    ) = forward_call(
        hidden, cotangent, norm_gain[None, :], both, wstep, proj_shared, conv_values, conv_shared,
        bias, decay, skip, gate_gain[None, :], proj_out,
    )
    (gout, ggw, gvw, gsmall, grad_hidden, sums, head_sums) = back_call(
        gm_t, normed_t, coef, gains, run, step, slope, bc, sext, skip, decay,
        conv_shared.reshape(CONV + 1, -1, LANES).transpose(1, 0, 2),
        jnp.concatenate([wshared_own, wstep], axis=1), norm_gain[None, :], proj_out, y, gate_in,
        gate_gain[None, :], gated_w, vext, after, state_in, conv_values, runt, stept, both, hidden,
        cotangent, norm_scale,
    )
    return (
        block_out,
        grad_hidden,
        sums[7],
        jnp.stack([ggw, gvw], axis=1),
        gsmall[:, shared_here : shared_here + heads],
        gsmall[:, :shared_here],
        sums[: CONV + 1],
        head_sums[2 : 3 + CONV],
        head_sums[0, :heads],
        head_sums[1, :heads],
        jnp.sum(sums[CONV + 2].reshape(heads, HEAD_DIM), axis=1),
        sums[CONV + 1],
        gout,
    )


def solution(mesh):
    return jax.shard_map(
        body,
        mesh=mesh,
        in_specs=(
            P("seq", None),
            P("seq", None),
            P(),
            P(None, None, "head"),
            P(None, "head"),
            P(),
            P(None, "head"),
            P(),
            P("head"),
            P("head"),
            P("head"),
            P("head"),
            P(None, "head"),
        ),
        out_specs=(
            P("seq", None),
            P("seq", None),
            P(),
            P("seq", None, "head"),
            P("seq", "head"),
            P("seq", "head"),
            P(None, "head"),
            P(None, "head"),
            P("head"),
            P("head"),
            P("head"),
            P("head"),
            P("seq", "head"),
        ),
        check_vma=False,
    )
```

time: 432 us -> 293 us (0.68)
  waiting for transfers between devices: 55.4 us -> 0 us
  other arithmetic: 34.2 us -> 4.06 us
  starting transfers between devices: 29.3 us -> 0 us
  local copies, waits for them, and re-layouts: 54.5 us -> 26 us
  Pallas kernels: 256 us -> 262 us
    all_to_all x5 -> x0, waiting for transfers between devices: 55.4 us -> none  [the longest x2 27.7 us: to_owners(): lax.all_to_all(pieces, 'seq', split_axis=0, concat_axis=0, tiled=True)]
    all_to_all x5 -> x0, starting transfers between devices: 23.8 us -> none  [the longest x2 9.18 us: from_owners(): lax.all_to_all(pieces.astype(kind), 'seq', split_axis=0, concat_axis=0, t...]
    unnamed x28 -> x0, other arithmetic: 17.6 us -> none
    unnamed x83 -> x30, local copies, waits for them, and re-layouts: 24.6 us -> 17.8 us
    pallas_call x4 -> x2, Pallas kernels: 256 us -> 262 us  [the longest x1 200 us: back_call(): pl.pallas_call(functools.partial(back_kernel, bits), grid=(6 * nb + chunk...]
    ppermute x3 -> x0, starting transfers between devices: 5.49 us -> none  [the longest x1 4.86 us: from_behind(): return lax.ppermute(shard, 'seq', pairs)]
    convert_element_type x2 -> x0, other arithmetic: 5.41 us -> none  [the longest x1 5.34 us: body(): grad_mixed = (wide_cot * inverse).astype(bf16)]
    pallas_call x2 -> x0, local copies, waits for them, and re-layouts: 4.96 us -> none  [the longest x1 2.58 us: front_call(): pl.pallas_call(front_kernel, grid=(inner // BLOCK,), in_specs=[full((toke...]
  transfers between devices with their start and end apart: 8 -> 0, of which waited for: 5 -> 0; matrix products, arithmetic and copies ran while one was open for 8% -> 0% of each run, Pallas kernels for 0% -> 0%
where the time goes in v2:
time: 293 us
  Pallas kernels  262 us (89%)
  local copies, waits for them, and re-layouts  26 us (9%)
  other arithmetic  4.06 us (1%)
    pallas_call x1, Pallas kernels, back_call(): pl.pallas_call(functools.partial(back_kernel, bits), grid=(6 * nb + chunk...  200 us
    pallas_call x1, Pallas kernels, forward_call(): pl.pallas_call(functools.partial(forward_kernel, size), grid=(3 * nb + ch...  62.1 us
    unnamed x30, local copies, waits for them, and re-layouts  17.8 us

profile of v2, /device:TPU:0, one launch (start us, length us, event | category | flops | bytes accessed | tf_op | source)
XLA Modules:
  0.0 292.6 jit_solution(17742636604943213018)
XLA Ops:
  0.6 1.3 broadcast_in_dim.17.gain_ref
  1.9 0.0 copy-start.5
  1.9 0.0 copy-start.10
  1.9 0.0 copy-start.8
  1.9 0.0 copy-start.9
  2.0 0.0 copy-start.6
  2.0 8.9 %copy.31 = bf16[1536,2,1536]{2,0,1:T(8,128)(2,1)} copy(bf16[1536,2,1536]{2,1,0:T(2,128)(2,1)} %param.16) | data formatting | bytes 18874368 | tf_op args[3]
  10.8 0.0 copy-done.5
  10.8 0.2 copy.27
  11.1 0.8 pad.14.wstep_ref
  11.9 0.0 copy-done.10
  11.9 0.5 pad_bitcast_fusion.2.bias_ref
  12.4 0.0 copy-done.8
  12.4 0.0 copy-done.9
  12.4 0.5 pad_bitcast_fusion
  12.9 0.0 copy-done.6
  12.9 0.6 broadcast_in_dim.21.ggain_ref
  13.5 62.1 %forward.1 = (bf16[1536,512]{1,0:T(8,128)(2,1)}, f32[512,128]{1,0:T(8,128)}, f32[512,1536]{1,0:T(8,128)}, bf16[528,1536]{1,0:T(8,128)(2,1)}, f32[4,128,1536]{2,1...) custom-call(bf16[512,1536]{1,0:T(8,128)(2,1)} %hid_ref.3, ...), custom_call_target="tpu_custom_call" | custom-call | tf_op jit(solution)/shard_map/forward/pallas_call | solution.py:499
  75.6 1.0 constant_dynamic-slice_fusion
  76.7 2.0 pad_maximum_fusion.1.wsmall_ref
  78.6 199.7 %back.1 = (f32[96,1536]{1,0:T(8,128)}, f32[96,1536]{1,0:T(8,128)}, f32[96,1536]{1,0:T(8,128)}, f32[96,256]{1,0:T(8,128)}, f32[512,1536]{1,0:T(8,128)}, /*index=5*/f32[8,1536]{1,0:T(8,128)}, f32[8,128]{1,0:T(8,128)}) custom-call(bf16[1536,512]{1,0:T(8,128)(2,1)} %get-tuple-element.40.gmt_ref, bf16[1536,512]{1,0:T(8,128)(2,1)} %get-tuple-element.41.normedt_ref, ...), custom_call_target="tpu_custom_call" | custom-call | tf_op jit(solution)/shard_map/back/pallas_call | solution.py:1109
  278.4 1.6 slice_reduce_fusion
  279.9 0.0 copy-start
  280.0 1.5 pad_maximum_fusion
  281.4 0.0 copy-start.3
  281.4 0.0 copy-start.7
  281.4 1.9 copy.28
  283.4 0.0 copy-done.3
  283.4 0.7 copy.29
  284.0 0.6 slice.29
  284.7 0.0 copy-done.7
  284.7 0.6 slice.31
  285.3 0.5 slice_bitcast_fusion
  285.8 0.1 reshape_squeeze.3
  285.9 0.6 reduce_sum.9
  286.5 0.0 copy-done
  286.5 0.0 copy-start.1
  286.5 1.7 copy.36
  288.2 1.4 copy-done.1
  289.5 0.0 copy-start.4
  289.5 0.0 copy-start.2
  289.5 1.7 copy.37
  291.2 0.0 copy-done.4
  291.2 0.6 copy.38
  291.8 0.0 copy-done.2
  291.8 0.8 copy.39
  (1 shorter events, 0.0 us)
Async XLA Ops:
  1.9 8.9 %copy-start.5 = (bf16[1536,24]{0,1:T(8,128)(2,1)S(1)}, bf16[1536,24]{0,1:T(8,128)(2,1)}, u32[]{:S(2)}) copy-start(bf16[1536,24]{0,1:T(8,128)(2,1)} %param.17) | copy-start | bytes 221188
  1.9 9.9 %copy-start.10 = (f32[24]{0:T(128)S(1)}, f32[24]{0:T(128)}, u32[]{:S(2)}) copy-start(f32[24]{0:T(128)} %param.21) | copy-start | bytes 292
  1.9 10.5 %copy-start.8 = (f32[24]{0:T(128)S(1)}, f32[24]{0:T(128)}, u32[]{:S(2)}) copy-start(f32[24]{0:T(128)} %param.23) | copy-start | bytes 292
  1.9 10.5 %copy-start.9 = (f32[24]{0:T(128)S(1)}, f32[24]{0:T(128)}, u32[]{:S(2)}) copy-start(f32[24]{0:T(128)} %param.22) | copy-start | bytes 292
  2.0 11.0 %copy-start.6 = (f32[1536]{0:T(1024)S(1)}, f32[1536]{0:T(1024)}, u32[]{:S(2)}) copy-start(f32[1536]{0:T(1024)} %param.24) | copy-start | bytes 18436
  279.9 6.5 %copy-start = (f32[512,1536]{1,0:T(8,128)S(1)}, f32[512,1536]{1,0:T(8,128)}, u32[]{:S(2)}) copy-start(f32[512,1536]{1,0:T(8,128)} %get-tuple-element.98) | copy-start | bytes 9437188
  281.4 1.9 copy-start.3
  281.4 3.2 %copy-start.7 = (f32[8,128]{1,0:T(8,128)S(1)}, f32[8,128]{1,0:T(8,128)}, u32[]{:S(2)}) copy-start(f32[8,128]{1,0:T(8,128)} %get-tuple-element.63) | copy-start | bytes 12292
  286.5 3.0 %copy-start.1 = (f32[512,1536]{1,0:T(8,128)S(1)}, f32[512,1536]{1,0:T(8,128)}, u32[]{:S(2)}) copy-start(f32[512,1536]{1,0:T(8,128)} %get-tuple-element.99) | copy-start | bytes 9437188
  289.5 1.7 copy-start.4
  289.5 2.3 copy-start.2

commit v3 on v2

--- a/solution.py
+++ b/solution.py
@@ -215,10 +215,10 @@
     skip_ref, ggain_ref, wout_ref, hrow_ref, crow_ref,
     normedt_ref, scale_ref, gate_ref, vext_ref, after_ref, y_ref, gw_ref, in_ref, step_ref,
     slope_ref, run_ref, runt_ref, stept_ref, sext_ref, bc_ref, gains_ref, out_ref, gmt_ref,
-    coef_ref,
-    nx, halo, halo_sems, scores, bt, end_w, vwide, act_all, gates, ys, states, acc, acc_send,
+    coef_ref, near_ref,
+    nx, halo, halo_sems, scores, bt, end_w, vwide, gates, ys, states, acc, acc_send,
     acc_land, acc_sems, squares, sq_land, sq_sems, totals, totals_land, totals_sems,
-    ex_own, ex_landing, ex_mixed, ex_result, ex_sems,
+    near_land, near_sems, ex_own, ex_landing, ex_mixed, ex_result, ex_sems,
 ):
     step_id = pl.program_id(0)
     index = lax.axis_index("seq")
@@ -226,8 +226,9 @@
     tokens = hid_ref.shape[0]
     width = hid_ref.shape[1]
     chunks = tokens // CHUNK
-    nb = act_all.shape[0]
-    t_gate, t_mix, t_last = nb, 2 * nb, 3 * nb
+    nb = gates.shape[0]
+    t_mix, t_last = nb, 2 * nb
+    half_width = width // 2
     exchange = StateExchange(
         index, size, False, ex_own, ex_landing, ex_mixed, ex_result, ex_sems, gains_ref
     )
@@ -307,15 +308,14 @@
             scores[c] = mm(c_rows, b_rows, NT)
             bt[:, rows] = transposed(b_rows)
 
-    @pl.when(step_id < t_gate)
+    @pl.when(step_id < t_mix)
     def _():
         j = step_id
-        values = mm(nx[...], wi_ref[0]).astype(bf16)
+        values = mm(nx[...], wi_ref[1]).astype(bf16)
         vext_ref[...] = values
         vwide[...] = values.astype(f32)
         conv = conv_rows(vwide, cv_ref[...], HALO - CONV + 1, tokens)
         act = silu(conv).astype(bf16)
-        act_all[j] = act
         run_cols = rolled(run_ref[...], j)
         end_cols = rolled(end_w[...], j)
         state = jnp.zeros((STATE, BLOCK), f32)
@@ -327,34 +327,15 @@
             after_ref[c] = state
             states[j, c] = state
         exchange.send(j, state)
-
-    @pl.when((step_id >= t_gate) & (step_id < t_mix))
-    def _():
-        j = step_id - t_gate
         gate = mm(nx[HALO:, :], wi_ref[0])
         gate_ref[...] = gate
         gates[j] = gate
-
-        @pl.when(j == 0)
-        def _():
-            pltpu.make_async_remote_copy(
-                src_ref=totals_land.at[pl.ds(0, size - 1)],
-                dst_ref=totals_land.at[pl.ds(0, size - 1)],
-                send_sem=totals_sems.at[0], recv_sem=totals_sems.at[1],
-                device_id={"seq": lax.rem(index + 1, size)},
-                device_id_type=pl.DeviceIdType.MESH,
-            ).wait()
-            totals_land[size - 1] = totals[...]
-            for source in range(size):
-                gains_ref[source : source + 1, :] = totals_land[exchange.slot(source), 0:1, :]
-
-        run_cols = rolled(run_ref[...], j)
         mask = causal()
         skip = widen(rolled(skip_ref[...], j)[:, :BLOCK_HEADS])
         for c in range(chunks):
             rows = slice(c * CHUNK, (c + 1) * CHUNK)
             cols = run_cols[rows, :BLOCK_HEADS]
-            x = act_all[j, rows, :]
+            x = act[rows, :]
             y_pairs = []
             for pair in range(BLOCK // LANES):
                 mats = []
@@ -368,7 +349,36 @@
                     mm_left(jnp.concatenate(mats, axis=1), jnp.concatenate([low, high], axis=0))
                 )
             ys[j, rows, :] = jnp.concatenate(y_pairs, axis=1) + skip * x.astype(f32)
-        exchange.turn(j)
+
+    @pl.when(step_id == 1)
+    def _():
+        pltpu.make_async_remote_copy(
+            src_ref=totals_land.at[pl.ds(0, size - 1)],
+            dst_ref=totals_land.at[pl.ds(0, size - 1)],
+            send_sem=totals_sems.at[0], recv_sem=totals_sems.at[1],
+            device_id={"seq": lax.rem(index + 1, size)},
+            device_id_type=pl.DeviceIdType.MESH,
+        ).wait()
+        totals_land[size - 1] = totals[...]
+        for source in range(size):
+            gains_ref[source : source + 1, :] = totals_land[exchange.slot(source), 0:1, :]
+
+    @pl.when((step_id >= 2) & (step_id < nb + 2))
+    def _():
+        exchange.turn(step_id - 2)
+
+    def neighbour_copy(bit):
+        mine = (index // (1 << bit)) % 2
+        return send_to(
+            normedt_ref.at[pl.ds(pl.multiple_of(core * half_width, half_width), half_width)],
+            near_land.at[bit], near_sems.at[0, bit], near_sems.at[1, bit],
+            seq=index + (1 - 2 * mine) * (1 << bit),
+        )
+
+    @pl.when(step_id == nb + 1)
+    def _():
+        for bit in range(2):
+            neighbour_copy(bit).start()
 
     @pl.when((step_id >= t_mix) & (step_id < t_last))
     def _():
@@ -436,10 +446,15 @@
                 scaled[:, b * LANES : (b + 1) * LANES]
             )
         grad_inverse = jnp.sum(cot * mixed, axis=1, keepdims=True)
-        coef_ref[:, 0:LANES] = jnp.broadcast_to(
+        coef_ref[...] = jnp.broadcast_to(
             grad_inverse * inverse * inverse * inverse / INNER, (CHUNK, LANES)
         )
-        coef_ref[:, LANES:] = jnp.broadcast_to(inverse, (CHUNK, LANES))
+
+        @pl.when(c == chunks - 1)
+        def _():
+            for bit in range(2):
+                neighbour_copy(bit).wait()
+                near_ref[bit] = near_land[bit]
 
 
 def offsets_of(run_ref, chunks):
@@ -458,7 +473,7 @@
     chunks = tokens // CHUNK
     nb = inner // BLOCK
     size = lax.axis_size("seq")
-    t_gate, t_mix, t_last = nb, 2 * nb, 3 * nb
+    t_mix, t_last = nb, 2 * nb
 
     def at(start):
         return lambda s: jnp.clip(s - start, 0, nb - 1)
@@ -474,7 +489,7 @@
     outs = [
         ((width, tokens), bf16, full((width, tokens))),
         ((tokens, LANES), f32, full((tokens, LANES))),
-        ((tokens, inner), f32, cols(tokens, t_gate)),
+        ((tokens, inner), f32, cols(tokens, 0)),
         ((HALO + tokens, inner), bf16, cols(HALO + tokens, 0)),
         (
             (chunks, STATE, inner), f32,
@@ -493,19 +508,17 @@
         ((size, LANES), f32, full((size, LANES))),
         ((tokens, width), f32, row_block(width)),
         ((width, tokens), bf16, pl.BlockSpec((width, CHUNK), lambda s: (0, row_of(s)))),
-        ((tokens, 2 * LANES), f32, row_block(2 * LANES)),
+        ((tokens, LANES), f32, row_block(LANES)),
+        ((2, width // 2, tokens), bf16, full((2, width // 2, tokens))),
     ]
     sem = pltpu.SemaphoreType.DMA
     return pl.pallas_call(
         functools.partial(forward_kernel, size),
-        grid=(3 * nb + chunks,),
+        grid=(2 * nb + chunks,),
         in_specs=[
             full((tokens, width)),
             full((1, width)),
-            pl.BlockSpec(
-                (1, width, BLOCK),
-                lambda s: (jnp.where(s < t_gate, 1, 0), 0, jnp.where(s < t_gate, at(0)(s), at(t_gate)(s))),
-            ),
+            pl.BlockSpec((2, width, BLOCK), lambda s: (0, 0, at(0)(s))),
             full((width, LANES)),
             full((width, 2 * STATE)),
             cols(CONV + 1, 0),
@@ -528,7 +541,6 @@
             pltpu.VMEM((STATE, tokens), bf16),
             pltpu.VMEM((tokens, LANES), f32),
             pltpu.VMEM((HALO + tokens, BLOCK), f32),
-            pltpu.VMEM((nb, tokens, BLOCK), bf16),
             pltpu.VMEM((nb, tokens, BLOCK), f32),
             pltpu.VMEM((nb, tokens, BLOCK), f32),
             pltpu.VMEM((nb, chunks, STATE, BLOCK), f32),
@@ -542,6 +554,8 @@
             pltpu.VMEM((8, LANES), f32),
             pltpu.VMEM((size, 8, LANES), f32),
             sem((2,)),
+            pltpu.VMEM((2, width // 2, tokens), bf16),
+            sem((2, 2)),
         ] + exchange_scratch(nb, size, f32),
         compiler_params=pltpu.CompilerParams(
             collective_id=1, has_side_effects=True, vmem_limit_bytes=67043328
@@ -553,68 +567,69 @@
     )
 
 
-def order_bits(part, bits):
+def order_rows(part, bits):
     order = list(range(bits))
     if part == 1 and bits > 1:
         order[0], order[1] = 1, 0
     return order
 
 
-def slot_of(owner, part, bits):
+def order_columns(part, bits):
+    return [bit for bit in range(bits) if bit != part] + [part]
+
+
+def slot_of(owner, order):
     slot = 0
-    for bit in order_bits(part, bits):
+    for bit in order:
         slot = slot * 2 + ((owner >> bit) & 1)
     return slot
 
 
 class Reduction:
-    def __init__(self, held, landing, out, part, bits, index, send_sems, recv_sems, cols):
-        self.held, self.landing, self.out = held, landing, out
-        self.part, self.bits, self.index = part, bits, index
-        self.send_sems, self.recv_sems, self.cols = send_sems, recv_sems, cols
+    def __init__(self, held, landing, order, index, sems, put, put_other=None):
+        self.held, self.landing, self.order = held, landing, order
+        self.index, self.sems, self.put, self.put_other = index, sems, put, put_other
+        self.stages = len(order)
 
     def place(self, stage):
         base = 0
-        size = 1 << self.bits
-        for s, bit in enumerate(order_bits(self.part, self.bits)[: stage + 1]):
+        size = 1 << self.stages
+        for s, bit in enumerate(self.order[: stage + 1]):
             mine = (self.index // (1 << bit)) % 2
             half = size >> (s + 1)
             keep, give = base + mine * half, base + (1 - mine) * half
             base = keep
-        return keep, give, half, order_bits(self.part, self.bits)[stage]
+        return keep, give, half
 
     def copy(self, stage):
-        _, give, half, bit = self.place(stage)
+        _, give, half = self.place(stage)
+        bit = self.order[stage]
         mine = (self.index // (1 << bit)) % 2
-        partner = self.index + (1 - 2 * mine) * (1 << bit)
-        return pltpu.make_async_remote_copy(
-            src_ref=self.held.at[pl.ds(give, half)],
-            dst_ref=self.landing[stage],
-            send_sem=self.send_sems.at[stage],
-            recv_sem=self.recv_sems.at[stage],
-            device_id={"seq": partner},
-            device_id_type=pl.DeviceIdType.MESH,
+        return send_to(
+            self.held.at[pl.ds(give, half)], self.landing[stage],
+            self.sems.at[0, stage], self.sems.at[1, stage],
+            seq=self.index + (1 - 2 * mine) * (1 << bit),
         )
 
     def start(self, stage):
         self.copy(stage).start()
 
-    def finish(self, stage):
+    def advance(self, stage):
         self.copy(stage).wait()
-        keep, _, half, _ = self.place(stage)
-        if stage == self.bits - 1:
-            self.out[:, self.cols] = self.held[keep].astype(f32) + self.landing[stage][0].astype(f32)
-        else:
+        keep, _, half = self.place(stage)
+        if stage < self.stages - 1:
 
             @pl.loop(0, half)
             def _(i):
                 total = self.held[keep + i].astype(f32) + self.landing[stage][i].astype(f32)
                 self.held[keep + i] = total.astype(bf16)
 
-    def advance(self, stage):
-        self.finish(stage)
-        if stage + 1 < self.bits:
             self.start(stage + 1)
+        elif self.put_other is None:
+            self.put(self.held[keep].astype(f32) + self.landing[stage][0].astype(f32))
+        else:
+            self.put(self.held[keep].astype(f32))
+            self.put_other(self.landing[stage][0].astype(f32))
 
 
 def sum_copy(acc, landing, bit, index, sems):
@@ -631,15 +646,16 @@
 
 def back_kernel(
     bits,
-    gmt_ref, normedt_ref, coef_ref, gains_ref, run_ref, step_ref, slope_ref, bc_ref, sext_ref, skip_ref,
-    decay_ref, cs_ref, wsmall_ref, gain_ref,
-    wout_ref, y_ref, gate_ref, ggain_ref, gw_ref, vext_ref, after_ref, in_ref, cv_ref, runt_ref,
+    gmt_ref, normedt_ref, near_ref, gw_ref, coef_ref, gains_ref, run_ref, step_ref, slope_ref,
+    bc_ref, sext_ref, skip_ref, decay_ref, cs_ref, wsmall_ref, gain_ref,
+    wout_ref, y_ref, gate_ref, ggain_ref, vext_ref, after_ref, in_ref, cv_ref, runt_ref,
     stept_ref, wi_ref,
     hid_ref, cot_ref, scale_ref,
     gout_ref, ggw_ref, gvw_ref, gsmall_ref, ghid_ref, sums_ref, heads_ref,
     w_out, w_gate, w_values, w_small,
     land_out, land_gate, land_values, land_small,
-    rs_send, rs_recv,
+    rs_sems, near, near_sems,
+    own_cols, other_cols, land_cols, cols_sems,
     gv, acc_send, acc_land, acc_sems,
     edge_own, edge_tail, edge_land, edge_sems,
     dbc, dbc_land, dbc_sems, small, sedge_own, sedge_land, sedge_sems,
@@ -653,30 +669,51 @@
     size = 1 << bits
     tokens = y_ref.shape[0]
     chunks = tokens // CHUNK
-    nb = w_out.shape[0] * w_out.shape[3] // BLOCK
+    nb = ggates.shape[0]
     half_nb = nb // 2
     width = normedt_ref.shape[0]
+    half_width = width // 2
     rows_own = width // size
-    part_cols = w_out.shape[3]
-    t_out, t_gate, t_scan, t_values, t_grad, t_final = (nb * i for i in range(1, 7))
+    t_scan, t_grad, t_final = nb, 2 * nb, 3 * nb
     after_id = lax.rem(index + 1, size)
     before_id = lax.rem(index + size - 1, size)
-
-    def reduction(g, part):
-        held, landing, out = (
-            (w_out, land_out, gout_ref), (w_gate, land_gate, ggw_ref), (w_values, land_values, gvw_ref),
-        )[g]
-        land = [ref.at[part] for ref in landing]
-        slot = 2 * g + part
+    bit_of = lambda bit: (index // (1 << bit)) % 2
+    flip_of = lambda bit: index + (1 - 2 * bit_of(bit)) * (1 << bit)
+
+    def out_reduction(part):
+        cols = w_out.shape[3]
+
+        def put(value):
+            gout_ref[:, part * cols : (part + 1) * cols] = value
+
         return Reduction(
-            held.at[part], land, out, part, bits, index, rs_send.at[slot], rs_recv.at[slot],
-            pl.ds(part * part_cols, part_cols),
+            w_out.at[part], [ref.at[part] for ref in land_out], order_rows(part, bits), index,
+            rs_sems.at[part], put,
         )
 
-    rs = [[reduction(g, part) for part in range(2)] for g in range(3)]
+    def columns_reduction(g, part):
+        held, landing, out = ((w_gate, land_gate, ggw_ref), (w_values, land_values, gvw_ref))[g]
+
+        def put_half(half):
+            def put(value):
+                for b in range(half_nb):
+                    out[part * half_nb + b, half] = value[:, b * LANES : (b + 1) * LANES]
+
+            return put
+
+        return Reduction(
+            held.at[part], [ref.at[part] for ref in landing], order_columns(part, bits), index,
+            rs_sems.at[2 + 2 * g + part], put_half(bit_of(part)), put_half(1 - bit_of(part)),
+        )
+
+    def put_small(value):
+        gsmall_ref[...] = value
+
+    rs_out = [out_reduction(part) for part in range(2)]
+    rs_gate = [columns_reduction(0, part) for part in range(2)]
+    rs_values = [columns_reduction(1, part) for part in range(2)]
     rs_small = Reduction(
-        w_small, list(land_small), gsmall_ref, 1, bits, index, rs_send.at[6], rs_recv.at[6],
-        pl.ds(0, w_small.shape[2]),
+        w_small, list(land_small), order_rows(1, bits), index, rs_sems.at[6], put_small
     )
 
     def when_after(step):
@@ -686,9 +723,22 @@
         index, size, True, ex_own, ex_landing, ex_mixed, ex_result, ex_sems, gains_ref
     )
 
+    def near_copies(bit):
+        half = pl.ds(pl.multiple_of(core * half_width, half_width), half_width)
+        return (
+            pltpu.make_async_copy(near_ref.at[bit], near.at[bit, half], near_sems.at[0, bit]),
+            send_to(
+                near_ref.at[bit], near.at[bit, half], near_sems.at[1, bit], near_sems.at[2, bit],
+                head=1 - core,
+            ),
+        )
+
     @pl.when(step_id == 0)
     def _():
         greet(index, core, size)
+        for bit in range(2):
+            for copy in near_copies(bit):
+                copy.start()
         for c in range(chunks):
             rows = slice(c * CHUNK, (c + 1) * CHUNK)
             ct[:, rows] = transposed(bc_ref[rows, STATE:])
@@ -697,7 +747,54 @@
                     gmt_ref[b * LANES : (b + 1) * LANES, rows]
                 )
 
-    @pl.when(step_id < t_out)
+    group = width // 4
+    owners = size // 4
+
+    def scatter(piece, q, order, store):
+        for b in range(owners):
+            store(slot_of(q * owners + b, order), piece[b * rows_own : (b + 1) * rows_own, :])
+
+    def put_out(part):
+        cols = w_out.shape[3]
+        for q in range(4):
+            left = gmt_ref[q * group : (q + 1) * group, :]
+            piece = mm(left, gw_ref[:, part * cols : (part + 1) * cols]).astype(bf16)
+
+            def store(slot, value):
+                w_out[part, slot] = value
+
+            scatter(piece, q, order_rows(part, bits), store)
+
+    def columns_copy(g, part):
+        return send_to(
+            other_cols.at[g, part], land_cols.at[g, part], cols_sems.at[0, g, part],
+            cols_sems.at[1, g, part], seq=flip_of(part),
+        )
+
+    def split_block(g, j, value):
+        part = j // half_nb
+        mine = jnp.where(part == 0, bit_of(0), bit_of(1))
+        place = pl.ds(pl.multiple_of((j % half_nb) * LANES, LANES), LANES)
+        first, second = value[:, :LANES], value[:, LANES:]
+        own_cols[g, part, :, place] = jnp.where(mine == 0, first, second)
+        other_cols[g, part, :, place] = jnp.where(mine == 0, second, first)
+
+    def put_columns(g, part):
+        columns_copy(g, part).wait()
+        held = (w_gate, w_values)[g]
+        for q in range(4):
+            rows = slice(q * group, (q + 1) * group)
+            piece = mm(normedt_ref[rows, :], own_cols[g, part]) + mm(
+                near[part, rows, :], land_cols[g, part]
+            )
+
+            def store(slot, value):
+                held[part, slot] = value
+
+            scatter(piece.astype(bf16), q, order_columns(part, bits), store)
+        (rs_gate, rs_values)[g][part].start(0)
+
+    @pl.when(step_id < t_scan)
     def _():
         j = step_id
         offsets = offsets_of(run_ref, chunks)
@@ -716,50 +813,35 @@
             gg = ggw * ggain_ref[...] - coef * out
             dy = gg * act
             dys[j, rows, :] = dy
-            ggates[j, rows, :] = (gg * y * (sig * (1.0 + gate * (1.0 - sig)))).astype(bf16)
+            ggate = (gg * y * (sig * (1.0 + gate * (1.0 - sig)))).astype(bf16)
+            ggates[j, rows, :] = ggate
             grow = rolled(jnp.exp(run_ref[rows, :] + offsets[c]), j)[:, :BLOCK_HEADS]
             own = own + mm_right(ct[:, rows], dy * widen(grow))
         term_gate[j, 0:1, :] = term
         exchange.send(j, own)
-
-    def put_block(held, left, right, j):
-        part = j // half_nb
-        cols = pl.ds(pl.multiple_of((j % half_nb) * BLOCK, BLOCK), BLOCK)
-        group = width // 4
-        for q in range(4):
-            piece = mm(left[q * group : (q + 1) * group, :], right).astype(bf16)
-            for b in range(size // 4):
-                owner = q * (size // 4) + b
-                slots = [slot_of(owner, p, bits) for p in range(2)]
-                slot = slots[0] + part * (slots[1] - slots[0])
-                held[part, slot, :, cols] = piece[b * rows_own : (b + 1) * rows_own, :]
-
-    @pl.when((step_id >= t_out) & (step_id < t_gate))
-    def _():
-        j = step_id - t_out
-        put_block(w_out, gmt_ref, gw_ref[...], j)
-        exchange.turn(j)
-
-    @pl.when((step_id >= t_gate) & (step_id < t_scan))
-    def _():
-        j = step_id - t_gate
-        put_block(w_gate, normedt_ref, ggates[j], j)
-
-    @when_after(t_out + half_nb - 1)
-    def _():
-        rs[0][0].start(0)
-
-    @when_after(t_gate - 1)
-    def _():
-        rs[0][1].start(0)
-
-    @when_after(t_gate + half_nb - 1)
-    def _():
-        rs[1][0].start(0)
-
-    @when_after(t_scan - 1)
-    def _():
-        rs[1][1].start(0)
+        split_block(0, j, ggates[j])
+
+    for part in range(2):
+
+        @when_after(part)
+        def _(part=part):
+            put_out(part)
+            rs_out[part].start(0)
+
+    @pl.when((step_id >= 2) & (step_id < nb + 2))
+    def _():
+        exchange.turn(step_id - 2)
+
+    @when_after(half_nb - 1)
+    def _():
+        columns_copy(0, 0).start()
+
+    @when_after(nb - 1)
+    def _():
+        columns_copy(0, 1).start()
+        for bit in range(2):
+            for copy in near_copies(bit):
+                copy.wait()
 
     mask = causal()
     rows_i = lax.broadcasted_iota(jnp.int32, (CHUNK, CHUNK), 0)
@@ -785,7 +867,7 @@
             run = run_ref[rows, :]
             end_w[rows, :] = jnp.exp(run[CHUNK - 1 :, :] - run)
 
-    @pl.when((step_id >= t_scan) & (step_id < t_values))
+    @pl.when((step_id >= t_scan) & (step_id < t_grad))
     def _():
         j = step_id - t_scan
         offsets = offsets_of(run_ref, chunks)
@@ -878,19 +960,59 @@
         for k in range(CONV - 1):
             total = total + cv_ref[k : k + 1, :] * gext[CONV - 1 - k : CONV - 1 - k + tokens, :]
         gv[j] = total.astype(bf16)
-        lacking = jnp.zeros((8, BLOCK), f32)
-        edge_tail[j] = total[tokens - 8 :, :] + lacking
+        edge_tail[j, 0:8, :] = total[tokens - 8 :, :]
+        edge_tail[j, 8 : 8 + CONV + 1, :] = cv_ref[...]
         edge_own[j] = gconv[0:8, :]
         send_to(
             edge_own.at[j], edge_land.at[j], edge_sems.at[0, j], edge_sems.at[1, j], seq=before_id
         ).start()
 
+    def finish_block(j):
+        send_to(
+            edge_own.at[j], edge_land.at[j], edge_sems.at[0, j], edge_sems.at[1, j], seq=before_id
+        ).wait()
+        nxt = jnp.where(index == size - 1, 0.0, 1.0) * edge_land[j]
+        row8 = lax.broadcasted_iota(jnp.int32, (8, BLOCK), 0)
+        fix = edge_tail[j, 0:8, :]
+        for k in range(CONV - 1):
+            ahead = CONV - 1 - k
+            moved = pltpu.roll(nxt, 8 - ahead, 0)
+            fix = fix + jnp.where(row8 >= 8 - ahead, edge_tail[j, 8 + k : 9 + k, :] * moved, 0.0)
+        both_rows = jnp.concatenate([gv[j, tokens - 16 : tokens - 8, :].astype(f32), fix], axis=0)
+        gv[j, tokens - 16 :, :] = both_rows.astype(bf16)
+        split_block(1, j, gv[j])
+
+    @pl.when((step_id > t_scan) & (step_id <= t_grad))
+    def _():
+        finish_block(step_id - t_scan - 1)
+
+    @when_after(t_scan)
+    def _():
+        rs_out[0].advance(0)
+
+    @when_after(t_scan + 1)
+    def _():
+        put_columns(0, 0)
+        rs_out[1].advance(0)
+
+    @when_after(t_scan + 2)
+    def _():
+        put_columns(0, 1)
+
     @when_after(t_scan + half_nb)
     def _():
-        rs[0][0].advance(0)
-        rs[0][1].advance(0)
-
-    @when_after(t_values - 1)
+        columns_copy(1, 0).start()
+        rs_out[0].advance(1)
+        rs_out[1].advance(1)
+
+    @when_after(t_grad - 1)
+    def _():
+        rs_gate[0].advance(0)
+        rs_gate[1].advance(0)
+        rs_out[0].advance(2)
+        rs_out[1].advance(2)
+
+    @when_after(t_grad - 1)
     def _():
         tri = mask.astype(f32)
         tri_t = mask_t.astype(f32)
@@ -926,29 +1048,11 @@
             dbc.at[1 - core], dbc_land, dbc_sems.at[0], dbc_sems.at[1], head=1 - core
         ).start()
 
-    @pl.when((step_id >= t_values) & (step_id < t_grad))
-    def _():
-        j = step_id - t_values
-        send_to(
-            edge_own.at[j], edge_land.at[j], edge_sems.at[0, j], edge_sems.at[1, j], seq=before_id
-        ).wait()
-        cv = cv_ref[...]
-        nxt = jnp.where(index == size - 1, 0.0, 1.0) * edge_land[j]
-        row8 = lax.broadcasted_iota(jnp.int32, (8, BLOCK), 0)
-        fix = edge_tail[j]
-        for k in range(CONV - 1):
-            ahead = CONV - 1 - k
-            moved = pltpu.roll(nxt, 8 - ahead, 0)
-            fix = fix + jnp.where(row8 >= 8 - ahead, cv[k : k + 1, :] * moved, 0.0)
-        both_rows = jnp.concatenate([gv[j, tokens - 16 : tokens - 8, :].astype(f32), fix], axis=0)
-        gv[j, tokens - 16 :, :] = both_rows.astype(bf16)
-        put_block(w_values, normedt_ref, gv[j], j)
-
-    @when_after(t_values + half_nb - 1)
-    def _():
-        rs[2][0].start(0)
-
-    @when_after(t_values)
+    @when_after(t_grad)
+    def _():
+        columns_copy(1, 1).start()
+
+    @when_after(t_grad)
     def _():
         send_to(
             dbc.at[1 - core], dbc_land, dbc_sems.at[0], dbc_sems.at[1], head=1 - core
@@ -969,9 +1073,8 @@
             sedge_own, sedge_land, sedge_sems.at[0], sedge_sems.at[1], seq=before_id
         ).start()
 
-    @when_after(t_grad - 1)
-    def _():
-        rs[2][1].start(0)
+    @when_after(t_grad + 1)
+    def _():
         send_to(
             sedge_own, sedge_land, sedge_sems.at[0], sedge_sems.at[1], seq=before_id
         ).wait()
@@ -982,12 +1085,13 @@
         for k in range(CONV - 1):
             total = total + taps[k : k + 1, :] * gs[CONV - 1 - k : CONV - 1 - k + tokens, :]
         small[:, 0:LANES] = total.astype(bf16)
-        group = width // 4
         for q in range(4):
             piece = mm(normedt_ref[q * group : (q + 1) * group, :], small[...]).astype(bf16)
-            for b in range(size // 4):
-                slot = slot_of(q * (size // 4) + b, 1, bits)
-                w_small[slot] = piece[b * rows_own : (b + 1) * rows_own, :]
+
+            def store(slot, value):
+                w_small[slot] = value
+
+            scatter(piece, q, order_rows(1, bits), store)
         rs_small.start(0)
 
     @pl.when((step_id >= t_grad) & (step_id < t_final))
@@ -997,19 +1101,26 @@
 
         @pl.when(j == 0)
         def _():
-            first = part + mm(small[...], wsmall_ref[...], NT)
             for b in range(width // BLOCK):
-                dys[b] = first[:, b * BLOCK : (b + 1) * BLOCK]
+                dys[b] = part[:, b * BLOCK : (b + 1) * BLOCK]
 
         @pl.when(j > 0)
         def _():
             for b in range(width // BLOCK):
                 dys[b] += part[:, b * BLOCK : (b + 1) * BLOCK]
 
-    @when_after(t_grad + half_nb)
-    def _():
-        rs[1][0].advance(0)
-        rs[1][1].advance(0)
+    @when_after(t_grad + 2)
+    def _():
+        put_columns(1, 0)
+        rs_gate[0].advance(1)
+        rs_gate[1].advance(1)
+
+    @when_after(t_grad + half_nb + 1)
+    def _():
+        put_columns(1, 1)
+        rest = mm(small[...], wsmall_ref[...], NT)
+        for b in range(width // BLOCK):
+            dys[b] += rest[:, b * BLOCK : (b + 1) * BLOCK]
 
     @when_after(t_final - 1)
     def _():
@@ -1048,28 +1159,28 @@
             sum_copy(vec, vec_land, bit, index, vec_sems).wait()
             vec[bit + 1] = vec[bit] + vec_land[bit]
 
-        for stage in range(1, bits):
-            sum_copy(vec, vec_land, stage - 1, index, vec_sems).start()
-            for g in range(2):
+        for part in range(2):
+            for stage in range(3, bits):
+                rs_out[part].advance(stage)
+        rs_small.advance(0)
+        for stage in range(bits):
+            sum_copy(vec, vec_land, stage, index, vec_sems).start()
+            if stage + 2 < bits:
                 for part in range(2):
-                    rs[g][part].advance(stage)
+                    rs_gate[part].advance(stage + 2)
             for part in range(2):
-                rs[2][part].advance(stage - 1)
-            rs_small.advance(stage - 1)
-            add(stage - 1)
-        sum_copy(vec, vec_land, bits - 1, index, vec_sems).start()
-        for part in range(2):
-            rs[2][part].advance(bits - 1)
-        rs_small.advance(bits - 1)
-        add(bits - 1)
+                rs_values[part].advance(stage)
+            if stage + 1 < bits:
+                rs_small.advance(stage + 1)
+            add(stage)
         heads_ref[...] = vec[bits, nb, :, 0:LANES]
         for b in range(nb):
             sums_ref[:, b * BLOCK : (b + 1) * BLOCK] = vec[bits, b]
 
 
 def back_call(
-    gm_t, normed_t, coef, gains, run, step, slope, bc, sext, skip, decay, conv_shared, wsmall, gain,
-    wout, y, gate, gate_gain, gated_w, vext, after, state_in, conv_values, runt, stept, both,
+    gm_t, normed_t, near, gated_w, coef, gains, run, step, slope, bc, sext, skip, decay,
+    conv_shared, wsmall, gain, wout, y, gate, gate_gain, vext, after, state_in, conv_values, runt, stept, both,
     hidden, cotangent, scale,
 ):
     width, tokens = normed_t.shape
@@ -1079,7 +1190,7 @@
     size = lax.axis_size("seq")
     bits = size.bit_length() - 1
     rows_own = width // size
-    t_out, t_gate, t_scan, t_values, t_grad, t_final = (nb * i for i in range(1, 7))
+    t_scan, t_grad, t_final = nb, 2 * nb, 3 * nb
 
     def column(start):
         return lambda s: jnp.clip(s - start, 0, nb - 1)
@@ -1090,9 +1201,6 @@
     def cols(rows, start):
         at = column(start)
         return pl.BlockSpec((rows, BLOCK), lambda s: (0, at(s)))
-
-    def scan_or_values(s):
-        return jnp.where(s < t_values, column(t_scan)(s), column(t_values)(s))
 
     row_block = lambda w: pl.BlockSpec((CHUNK, w), lambda s: (jnp.clip(s - t_final, 0, chunks - 1), 0))
     row_single = lambda w: pl.BlockSpec(
@@ -1100,18 +1208,20 @@
         lambda s: (jnp.clip(s - t_final, 0, chunks - 1), 0),
         pipeline_mode=pl.Buffered(1),
     )
-    part_cols = inner // 2
-    held = lambda: pltpu.VMEM((2, size, rows_own, part_cols), bf16)
-    landing = lambda: tuple(
-        pltpu.VMEM((2, size >> (s + 1), rows_own, part_cols), bf16) for s in range(bits)
+    held = lambda cols: pltpu.VMEM((2, size, rows_own, cols), bf16)
+    landing = lambda cols: tuple(
+        pltpu.VMEM((2, size >> (s + 1), rows_own, cols), bf16) for s in range(bits)
     )
+    columns = lambda: pltpu.VMEM((2, 2, tokens, inner // 4), bf16)
     sem = pltpu.SemaphoreType.DMA
     return pl.pallas_call(
         functools.partial(back_kernel, bits),
-        grid=(6 * nb + chunks,),
+        grid=(3 * nb + chunks,),
         in_specs=[
             full((width, tokens)),
             full((width, tokens)),
+            pl.BlockSpec(memory_space=pl.ANY),
+            full((tokens, inner)),
             full((tokens, LANES)),
             full((size, LANES)),
             full((tokens, LANES)),
@@ -1128,13 +1238,12 @@
             cols(tokens, 0),
             cols(tokens, 0),
             cols(1, 0),
-            cols(tokens, t_out),
             pl.BlockSpec(
                 (HALO + tokens, BLOCK), lambda s: (0, column(t_scan)(s)), pipeline_mode=pl.Buffered(1)
             ),
             pl.BlockSpec((chunks, STATE, BLOCK), lambda s: (0, 0, column(t_scan)(s))),
             cols(STATE, t_scan),
-            pl.BlockSpec((CONV + 1, BLOCK), lambda s: (0, scan_or_values(s))),
+            cols(CONV + 1, t_scan),
             pl.BlockSpec((1, 8, tokens), lambda s: (column(t_scan)(s), 0, 0)),
             pl.BlockSpec((1, 8, tokens), lambda s: (column(t_scan)(s), 0, 0)),
             pl.BlockSpec(
@@ -1146,8 +1255,8 @@
         ],
         out_shape=[
             jax.ShapeDtypeStruct((rows_own, inner), f32),
-            jax.ShapeDtypeStruct((rows_own, inner), f32),
-            jax.ShapeDtypeStruct((rows_own, inner), f32),
+            jax.ShapeDtypeStruct((nb, 2, rows_own, LANES), f32),
+            jax.ShapeDtypeStruct((nb, 2, rows_own, LANES), f32),
             jax.ShapeDtypeStruct((rows_own, 2 * LANES), f32),
             jax.ShapeDtypeStruct((tokens, width), f32),
             jax.ShapeDtypeStruct((8, inner), f32),
@@ -1155,25 +1264,27 @@
         ],
         out_specs=[
             full((rows_own, inner)),
-            full((rows_own, inner)),
-            full((rows_own, inner)),
+            full((nb, 2, rows_own, LANES)),
+            full((nb, 2, rows_own, LANES)),
             full((rows_own, 2 * LANES)),
             row_block(width),
             pl.BlockSpec((8, inner), lambda s: (0, 0)),
             pl.BlockSpec((8, LANES), lambda s: (0, 0)),
         ],
         scratch_shapes=[
-            held(), held(), held(),
+            held(inner // 2), held(inner // 4), held(inner // 4),
             pltpu.VMEM((size, rows_own, 2 * LANES), bf16),
-            landing(), landing(), landing(),
+            landing(inner // 2), landing(inner // 4), landing(inner // 4),
             tuple(pltpu.VMEM((size >> (s + 1), rows_own, 2 * LANES), bf16) for s in range(bits)),
-            sem((7, bits)), sem((7, bits)),
+            sem((7, 2, bits)),
+            pltpu.VMEM((2, width, tokens), bf16), sem((3, 2)),
+            columns(), columns(), columns(), sem((2, 2, 2)),
             pltpu.VMEM((nb, tokens, BLOCK), bf16),
             pltpu.VMEM((chunks, CHUNK, width), bf16),
             pltpu.VMEM((chunks, CHUNK, width), bf16),
             sem((2, chunks)),
             pltpu.VMEM((nb, 8, BLOCK), f32),
-            pltpu.VMEM((nb, 8, BLOCK), f32),
+            pltpu.VMEM((nb, 16, BLOCK), f32),
             pltpu.VMEM((nb, 8, BLOCK), f32),
             sem((2, nb)),
             pltpu.VMEM((2, tokens, LANES), f32),
@@ -1207,8 +1318,9 @@
         ),
         name="back",
     )(
-        gm_t, normed_t, coef, gains, run, step, slope, bc, sext, skip, decay, conv_shared, wsmall,
-        gain, wout, y, gate, gate_gain, gated_w, vext, after, state_in, conv_values, runt, stept,
+        gm_t, normed_t, near, gated_w, coef, gains, run, step, slope, bc, sext, skip, decay,
+        conv_shared, wsmall, gain, wout, y, gate, gate_gain, vext, after, state_in, conv_values,
+        runt, stept,
         both, hidden, cotangent, scale,
     )
 
@@ -1231,23 +1343,23 @@
     wshared_own = lax.dynamic_slice_in_dim(proj_shared, shared_start, shared_here, 1)
     (
         normed_t, norm_scale, gate_in, vext, after, y, gated_w, state_in, step, slope, run, runt,
-        stept, sext, bc, gains, block_out, gm_t, coef,
+        stept, sext, bc, gains, block_out, gm_t, coef, near,
     ) = forward_call(
         hidden, cotangent, norm_gain[None, :], both, wstep, proj_shared, conv_values, conv_shared,
         bias, decay, skip, gate_gain[None, :], proj_out,
     )
     (gout, ggw, gvw, gsmall, grad_hidden, sums, head_sums) = back_call(
-        gm_t, normed_t, coef, gains, run, step, slope, bc, sext, skip, decay,
+        gm_t, normed_t, near, gated_w, coef, gains, run, step, slope, bc, sext, skip, decay,
         conv_shared.reshape(CONV + 1, -1, LANES).transpose(1, 0, 2),
         jnp.concatenate([wshared_own, wstep], axis=1), norm_gain[None, :], proj_out, y, gate_in,
-        gate_gain[None, :], gated_w, vext, after, state_in, conv_values, runt, stept, both, hidden,
+        gate_gain[None, :], vext, after, state_in, conv_values, runt, stept, both, hidden,
         cotangent, norm_scale,
     )
     return (
         block_out,
         grad_hidden,
         sums[7],
-        jnp.stack([ggw, gvw], axis=1),
+        jnp.stack([ggw, gvw]).transpose(3, 0, 1, 2, 4).reshape(-1, 2, inner),
         gsmall[:, shared_here : shared_here + heads],
         gsmall[:, :shared_here],
         sums[: CONV + 1],

time: 293 us -> 284 us (0.969)
  Pallas kernels: 262 us -> 250 us
    pallas_call x2, Pallas kernels: 262 us -> 250 us  [the longest x1 180 us: back_call(): pl.pallas_call(functools.partial(back_kernel, bits), grid=(3 * nb + chunk...]
    unnamed x30 -> x29, local copies, waits for them, and re-layouts: 17.8 us -> 20.1 us
where the time goes in v3:
time: 284 us; the launch traced here: 283 us
  Pallas kernels  250 us (88%)
  local copies, waits for them, and re-layouts  28.2 us (10%)
  other arithmetic  3.93 us (1%)
    pallas_call x1, Pallas kernels, back_call(): pl.pallas_call(functools.partial(back_kernel, bits), grid=(3 * nb + chunk...  180 us
    pallas_call x1, Pallas kernels, forward_call(): pl.pallas_call(functools.partial(forward_kernel, size), grid=(2 * nb + ch...  69.9 us
    unnamed x29, local copies, waits for them, and re-layouts  20.1 us

profile of v3, /device:TPU:0, one launch (start us, length us, event | category | flops | bytes accessed | tf_op | source)
XLA Modules:
  0.0 282.9 jit_solution(9395978490296078196)
XLA Ops:
  0.6 1.3 broadcast_in_dim.17.gain_ref
  1.9 0.0 copy-start.4
  1.9 0.0 copy-start.9
  1.9 0.0 copy-start.7
  1.9 0.0 copy-start.8
  2.0 0.0 copy-start.5
  2.0 8.9 %copy.37 = bf16[1536,2,1536]{2,0,1:T(8,128)(2,1)} copy(bf16[1536,2,1536]{2,1,0:T(2,128)(2,1)} %param.16) | data formatting | bytes 18874368 | tf_op args[3]
  10.8 0.0 copy-done.4
  10.8 0.2 copy.30
  11.1 0.8 pad.14.wstep_ref
  11.9 0.0 copy-done.9
  11.9 0.5 pad_bitcast_fusion.2.bias_ref
  12.4 0.0 copy-done.7
  12.4 0.0 copy-done.8
  12.4 0.5 pad_bitcast_fusion
  12.9 0.0 copy-done.5
  12.9 0.6 broadcast_in_dim.21.ggain_ref
  13.5 69.9 %forward.1 = (bf16[1536,512]{1,0:T(8,128)(2,1)}, f32[512,128]{1,0:T(8,128)}, f32[512,1536]{1,0:T(8,128)}, bf16[528,1536]{1,0:T(8,128)(2,1)}, f32[4,128,1536]{2,1...) custom-call(bf16[512,1536]{1,0:T(8,128)(2,1)} %hid_ref.3, ...), custom_call_target="tpu_custom_call" | custom-call | tf_op jit(solution)/shard_map/forward/pallas_call | solution.py:515
  83.5 1.0 constant_dynamic-slice_fusion
  84.5 2.0 pad_maximum_fusion.wsmall_ref
  86.5 180.1 %back.1 = (f32[96,1536]{1,0:T(8,128)}, f32[6,2,96,128]{3,2,1,0:T(8,128)}, f32[6,2,96,128]{3,2,1,0:T(8,128)}, f32[96,256]{1,0:T(8,128)}, f32[512,1536]{1,0:T(8,12...) custom-call(bf16[1536,512]{1,0:T(8,128)(2,1)} %get-tuple-element.41.gmt_ref, bf16[1536,512]{1,0:T(8,128)(2,1)} %get-tuple-element.42.normedt_ref, ...), custom_call_target="tpu_custom_call" | custom-call | tf_op jit(solution)/shard_map/back/pallas_call | solution.py:1217
  266.5 1.6 slice_reduce_fusion
  268.1 1.3 maximum_bitcast_fusion
  269.4 0.9 copy.34
  270.4 0.0 copy-start.2
  270.4 0.0 copy-start.6
  270.4 2.4 reshape.34
  272.7 0.0 copy-done.2
  272.8 0.7 copy.33
  273.4 0.6 slice.29
  274.1 0.0 copy-done.6
  274.1 0.6 slice.31
  274.7 0.5 slice_bitcast_fusion
  275.2 0.1 reshape_squeeze.3
  275.2 0.6 reduce_sum.9
  275.9 0.0 copy-start
  275.9 3.9 %copy.42 = f32[512,1536]{1,0:T(8,128)} copy(f32[512,1536]{1,0:T(8,128)} %get-tuple-element.113) | data formatting | bytes 6291456
  279.8 0.0 copy-done
  279.8 0.0 copy-start.3
  279.8 0.0 copy-start.1
  279.8 1.7 copy.43
  281.5 0.0 copy-done.3
  281.5 0.6 copy.44
  282.1 0.0 copy-done.1
  282.1 0.8 copy.45
  (1 shorter events, 0.0 us)
Async XLA Ops:
  1.9 8.9 %copy-start.4 = (bf16[1536,24]{0,1:T(8,128)(2,1)S(1)}, bf16[1536,24]{0,1:T(8,128)(2,1)}, u32[]{:S(2)}) copy-start(bf16[1536,24]{0,1:T(8,128)(2,1)} %param.17) | copy-start | bytes 221188
  1.9 9.9 %copy-start.9 = (f32[24]{0:T(128)S(1)}, f32[24]{0:T(128)}, u32[]{:S(2)}) copy-start(f32[24]{0:T(128)} %param.21) | copy-start | bytes 292
  1.9 10.5 %copy-start.7 = (f32[24]{0:T(128)S(1)}, f32[24]{0:T(128)}, u32[]{:S(2)}) copy-start(f32[24]{0:T(128)} %param.23) | copy-start | bytes 292
  1.9 10.5 %copy-start.8 = (f32[24]{0:T(128)S(1)}, f32[24]{0:T(128)}, u32[]{:S(2)}) copy-start(f32[24]{0:T(128)} %param.22) | copy-start | bytes 292
  2.0 11.0 %copy-start.5 = (f32[1536]{0:T(1024)S(1)}, f32[1536]{0:T(1024)}, u32[]{:S(2)}) copy-start(f32[1536]{0:T(1024)} %param.24) | copy-start | bytes 18436
  270.4 2.4 copy-start.2
  270.4 3.7 %copy-start.6 = (f32[8,128]{1,0:T(8,128)S(1)}, f32[8,128]{1,0:T(8,128)}, u32[]{:S(2)}) copy-start(f32[8,128]{1,0:T(8,128)} %get-tuple-element.65) | copy-start | bytes 12292
  275.9 3.9 %copy-start = (f32[512,1536]{1,0:T(8,128)S(1)}, f32[512,1536]{1,0:T(8,128)}, u32[]{:S(2)}) copy-start(f32[512,1536]{1,0:T(8,128)} %get-tuple-element.114) | copy-start | bytes 9437188
  279.8 1.7 copy-start.3
  279.8 2.3 copy-start.1

commit v4 on v3

--- a/solution.py
+++ b/solution.py
@@ -59,20 +59,24 @@
     return high, (a - high.astype(f32)).astype(bf16)
 
 
+def along(pieces, dims, side):
+    return jnp.concatenate(pieces, axis=dims[0][side][0])
+
+
 def mm_left(a, b, dims=NN):
-    high, low = parts(a)
-    return mm(high, b, dims) + mm(low, b, dims)
+    return mm(along(parts(a), dims, 0), along([b, b], dims, 1), dims)
 
 
 def mm_right(a, b, dims=NN):
-    high, low = parts(b)
-    return mm(a, high, dims) + mm(a, low, dims)
+    return mm(along([a, a], dims, 0), along(parts(b), dims, 1), dims)
 
 
 def mm_both(a, b, dims=NN):
     a_high, a_low = parts(a)
     b_high, b_low = parts(b)
-    return mm(a_high, b_high, dims) + mm(a_low, b_high, dims) + mm(a_high, b_low, dims)
+    return mm(
+        along([a_high, a_low, a_high], dims, 0), along([b_high, b_high, b_low], dims, 1), dims
+    )
 
 
 def mm_exact(a, b, dims=NN):
@@ -569,8 +573,10 @@
 
 def order_rows(part, bits):
     order = list(range(bits))
-    if part == 1 and bits > 1:
-        order[0], order[1] = 1, 0
+    if part == 1:
+        order[:3] = order[:3][::-1]
+    if part == 2:
+        order[:2] = order[:2][::-1]
     return order
 
 
@@ -613,6 +619,18 @@
 
     def start(self, stage):
         self.copy(stage).start()
+
+    def start_piece(self, piece, pieces):
+        _, give, half = self.place(0)
+        count = half // pieces
+        bit = self.order[0]
+        mine = (self.index // (1 << bit)) % 2
+        send_to(
+            self.held.at[pl.ds(give + piece * count, count)],
+            self.landing[0].at[pl.ds(piece * count, count)],
+            self.sems.at[0, 0], self.sems.at[1, 0],
+            seq=self.index + (1 - 2 * mine) * (1 << bit),
+        ).start()
 
     def advance(self, stage):
         self.copy(stage).wait()
@@ -713,7 +731,7 @@
     rs_gate = [columns_reduction(0, part) for part in range(2)]
     rs_values = [columns_reduction(1, part) for part in range(2)]
     rs_small = Reduction(
-        w_small, list(land_small), order_rows(1, bits), index, rs_sems.at[6], put_small
+        w_small, list(land_small), order_rows(2, bits), index, rs_sems.at[6], put_small
     )
 
     def when_after(step):
@@ -826,7 +844,27 @@
         @when_after(part)
         def _(part=part):
             put_out(part)
-            rs_out[part].start(0)
+
+    pieces = size // 2
+
+    @pl.when((step_id >= 1) & (step_id < nb))
+    def _():
+        for reduction in rs_out:
+            reduction.start_piece(step_id - 1, pieces)
+
+    rest = pieces - (nb - 1)
+
+    @when_after(nb)
+    def _():
+        for piece in range(nb - 1, nb - 1 + (rest + 1) // 2):
+            for reduction in rs_out:
+                reduction.start_piece(piece, pieces)
+
+    @when_after(nb + 1)
+    def _():
+        for piece in range(nb - 1 + (rest + 1) // 2, pieces):
+            for reduction in rs_out:
+                reduction.start_piece(piece, pieces)
 
     @pl.when((step_id >= 2) & (step_id < nb + 2))
     def _():
@@ -842,6 +880,7 @@
         for bit in range(2):
             for copy in near_copies(bit):
                 copy.wait()
+        put_columns(0, 0)
 
     mask = causal()
     rows_i = lax.broadcasted_iota(jnp.int32, (CHUNK, CHUNK), 0)
@@ -872,10 +911,7 @@
         j = step_id - t_scan
         offsets = offsets_of(run_ref, chunks)
         vwide[...] = vext_ref[...].astype(f32)
-        conv = conv_rows(vwide, cv_ref[...], HALO - CONV + 1, tokens)
-        sig_all = 1.0 / (1.0 + jnp.exp(-conv))
-        act = (conv * sig_all).astype(bf16)
-        slope = sig_all * (1.0 + conv * (1.0 - sig_all))
+        taps = [jnp.zeros((1, BLOCK), f32)] * (CONV + 1)
         run_cols = rolled(run_ref[...], j)
         step_cols = rolled(step_ref[...], j)
         end_cols = rolled(end_w[...], j)
@@ -890,7 +926,10 @@
         for c in reversed(range(chunks)):
             rows = slice(c * CHUNK, (c + 1) * CHUNK)
             cols = run_cols[rows, :BLOCK_HEADS]
-            x = act[rows, :]
+            conv = conv_rows(vwide, cv_ref[...], HALO - CONV + 1 + c * CHUNK, CHUNK)
+            sig = 1.0 / (1.0 + jnp.exp(-conv))
+            x = (conv * sig).astype(bf16)
+            slope = sig * (1.0 + conv * (1.0 - sig))
             wide_x = x.astype(f32)
             dy = dys[j, rows, :]
             b_rows = bc_ref[rows, :STATE]
@@ -910,12 +949,10 @@
             dbc[0, rows, :] += mm_both(weighted, dstate, NT)
             dbc[1, rows, :] += mm_both(grown, enter, NT)
             hold = last * jnp.sum(dstate * enter, axis=0, keepdims=True)
-            ends[c : c + 1, :] += mm_exact(
-                jnp.broadcast_to(hold, (8, BLOCK)), pick.astype(f32)
-            )[:1, :]
             dstate = last * dstate + mm_right(ct[:, rows], grown)
             du_pairs = []
             col_sum = jnp.zeros((CHUNK, LANES), f32)
+            dscore = dscores[c]
             for pair in range(BLOCK // LANES):
                 lanes = slice(pair * LANES, (pair + 1) * LANES)
                 low, high = stack_pair(dy[:, lanes])
@@ -929,7 +966,7 @@
                     keep = jnp.exp(jnp.where(mask, col - row, -1e30))
                     piece = dmat[k * CHUNK : (k + 1) * CHUNK, :] * keep
                     piece = piece * stept_ref[0, head : head + 1, rows]
-                    dscores[c] += piece
+                    dscore = dscore + piece
                     full = piece * scores[c]
                     col_sum = jnp.where(
                         lane_row == BLOCK_HEADS * j + head,
@@ -940,29 +977,55 @@
                     keep_t = jnp.exp(jnp.where(mask_t, row - col, -1e30))
                     mats.append(scorest[c] * keep_t)
                 du_pairs.append(mm_both(jnp.concatenate(mats, axis=1), both))
-            dyc[rows, :] += col_sum
+            dscores[c] = dscore
             du = jnp.concatenate(du_pairs, axis=1) + du_state
-            xdu[rows, :] += mm_left(wide_x * du, pick)
-            dyc[rows, :] += mm_left(dy * carried, pick)
-            xdus[rows, :] += mm_left(wide_x * du_state, pick)
+            by_head = mm_left(
+                jnp.concatenate(
+                    [
+                        wide_x * du,
+                        dy * carried,
+                        wide_x * du_state,
+                        jnp.broadcast_to(hold, (HALO, BLOCK)),
+                    ],
+                    axis=0,
+                ),
+                pick,
+            )
+            xdu[rows, :] += by_head[0:CHUNK, :]
+            dyc[rows, :] += by_head[CHUNK : 2 * CHUNK, :] + col_sum
+            xdus[rows, :] += by_head[2 * CHUNK : 3 * CHUNK, :]
+            ends[c : c + 1, :] += by_head[3 * CHUNK : 3 * CHUNK + 1, :]
             dskip = dskip + jnp.sum(dy * wide_x, axis=0, keepdims=True)
-            gext[rows, :] = (step_w * du + skip * dy) * slope[rows, :]
-        gconv = gext[0:tokens, :]
+            gconv = (step_w * du + skip * dy) * slope
+            gext[rows, :] = gconv
+            taps[CONV] = taps[CONV] + jnp.sum(gconv, axis=0, keepdims=True)
+            values = vwide[HALO + c * CHUNK : HALO + (c + 1) * CHUNK, :]
+            total = cv_ref[CONV - 1 : CONV, :] * gconv
+            taps[CONV - 1] = taps[CONV - 1] + jnp.sum(values * gconv, axis=0, keepdims=True)
+            for k in range(CONV - 1):
+                ahead = c * CHUNK + CONV - 1 - k
+                moved = gext[ahead : ahead + CHUNK, :]
+                total = total + cv_ref[k : k + 1, :] * moved
+                taps[k] = taps[k] + jnp.sum(values * moved, axis=0, keepdims=True)
+            gv[j, rows, :] = total.astype(bf16)
+            if c == chunks - 1:
+                edge_tail[j, 0:8, :] = total[CHUNK - 8 :, :]
+        row8 = lax.broadcasted_iota(jnp.int32, (8, BLOCK), 0)
+        ahead_rows = vwide[HALO - CONV + 1 : HALO - CONV + 9, :]
         for k in range(CONV):
-            first = HALO - CONV + 1 + k
-            vec[0, j, k : k + 1, :] = jnp.sum(
-                vwide[first : first + tokens, :] * gconv, axis=0, keepdims=True
-            )
-        vec[0, j, CONV : CONV + 1, :] = jnp.sum(gconv, axis=0, keepdims=True)
+            tap = taps[k]
+            if k < CONV - 1:
+                moved = pltpu.roll(gext[0:8, :], k, 0) if k else gext[0:8, :]
+                inside = (row8 >= k) & (row8 < CONV - 1)
+                tap = tap + jnp.sum(
+                    jnp.where(inside, ahead_rows * moved, 0.0), axis=0, keepdims=True
+                )
+            vec[0, j, k : k + 1, :] = tap
+        vec[0, j, CONV : CONV + 1, :] = taps[CONV]
         vec[0, j, CONV + 1 : CONV + 2, :] = term_gate[j, 0:1, :]
         vec[0, j, CONV + 2 : CONV + 3, :] = dskip
-        total = cv_ref[CONV - 1 : CONV, :] * gconv
-        for k in range(CONV - 1):
-            total = total + cv_ref[k : k + 1, :] * gext[CONV - 1 - k : CONV - 1 - k + tokens, :]
-        gv[j] = total.astype(bf16)
-        edge_tail[j, 0:8, :] = total[tokens - 8 :, :]
         edge_tail[j, 8 : 8 + CONV + 1, :] = cv_ref[...]
-        edge_own[j] = gconv[0:8, :]
+        edge_own[j] = gext[0:8, :]
         send_to(
             edge_own.at[j], edge_land.at[j], edge_sems.at[0, j], edge_sems.at[1, j], seq=before_id
         ).start()
@@ -982,35 +1045,29 @@
         gv[j, tokens - 16 :, :] = both_rows.astype(bf16)
         split_block(1, j, gv[j])
 
-    @pl.when((step_id > t_scan) & (step_id <= t_grad))
-    def _():
-        finish_block(step_id - t_scan - 1)
-
-    @when_after(t_scan)
-    def _():
+    @pl.when((step_id > t_scan + 1) & (step_id < t_grad))
+    def _():
+        finish_block(step_id - t_scan - 2)
+
+    @when_after(t_scan + 1)
+    def _():
+        put_columns(0, 1)
+
+    @when_after(t_scan + 2)
+    def _():
+        rs_gate[0].advance(0)
         rs_out[0].advance(0)
-
-    @when_after(t_scan + 1)
-    def _():
-        put_columns(0, 0)
         rs_out[1].advance(0)
 
-    @when_after(t_scan + 2)
-    def _():
-        put_columns(0, 1)
-
-    @when_after(t_scan + half_nb)
+    @when_after(t_scan + half_nb + 1)
     def _():
         columns_copy(1, 0).start()
+        rs_gate[0].advance(1)
+        rs_gate[1].advance(0)
+
+    @when_after(t_grad - 1)
+    def _():
         rs_out[0].advance(1)
-        rs_out[1].advance(1)
-
-    @when_after(t_grad - 1)
-    def _():
-        rs_gate[0].advance(0)
-        rs_gate[1].advance(0)
-        rs_out[0].advance(2)
-        rs_out[1].advance(2)
 
     @when_after(t_grad - 1)
     def _():
@@ -1050,7 +1107,17 @@
 
     @when_after(t_grad)
     def _():
+        finish_block(nb - 2)
+        finish_block(nb - 1)
         columns_copy(1, 1).start()
+        put_columns(1, 0)
+        rs_gate[0].advance(2)
+        rs_gate[1].advance(1)
+        rs_out[1].advance(1)
+
+    @when_after(t_grad + 1)
+    def _():
+        rs_gate[0].advance(3)
 
     @when_after(t_grad)
     def _():
@@ -1091,7 +1158,7 @@
             def store(slot, value):
                 w_small[slot] = value
 
-            scatter(piece, q, order_rows(1, bits), store)
+            scatter(piece, q, order_rows(2, bits), store)
         rs_small.start(0)
 
     @pl.when((step_id >= t_grad) & (step_id < t_final))
@@ -1111,13 +1178,16 @@
 
     @when_after(t_grad + 2)
     def _():
-        put_columns(1, 0)
-        rs_gate[0].advance(1)
-        rs_gate[1].advance(1)
-
-    @when_after(t_grad + half_nb + 1)
+        rs_out[0].advance(2)
+
+    @when_after(t_grad + 3)
     def _():
         put_columns(1, 1)
+        rs_out[1].advance(2)
+
+    @when_after(t_grad + 4)
+    def _():
+        rs_gate[1].advance(2)
         rest = mm(small[...], wsmall_ref[...], NT)
         for b in range(width // BLOCK):
             dys[b] += rest[:, b * BLOCK : (b + 1) * BLOCK]
@@ -1153,25 +1223,47 @@
         mean = jnp.mean(ghat * hat, axis=1, keepdims=True)
         ghid_ref[...] = cot_ref[...].astype(f32) + scale * (ghat - hat * mean)
 
+    @when_after(t_final)
+    def _():
+        rs_out[0].advance(3)
+
+    @when_after(t_final + 1)
+    def _():
+        rs_values[0].advance(0)
+
     @when_after(t_final + chunks - 1)
     def _():
+        rs_out[1].advance(3)
+
+        def begin(bit):
+            sum_copy(vec, vec_land, bit, index, vec_sems).start()
+
         def add(bit):
             sum_copy(vec, vec_land, bit, index, vec_sems).wait()
             vec[bit + 1] = vec[bit] + vec_land[bit]
-
-        for part in range(2):
-            for stage in range(3, bits):
-                rs_out[part].advance(stage)
+            if bit + 1 < bits:
+                begin(bit + 1)
+
+        begin(0)
+        rs_values[1].advance(0)
+        add(0)
         rs_small.advance(0)
-        for stage in range(bits):
-            sum_copy(vec, vec_land, stage, index, vec_sems).start()
-            if stage + 2 < bits:
-                for part in range(2):
-                    rs_gate[part].advance(stage + 2)
-            for part in range(2):
-                rs_values[part].advance(stage)
-            if stage + 1 < bits:
-                rs_small.advance(stage + 1)
+        rs_gate[1].advance(3)
+        add(1)
+        rs_values[0].advance(1)
+        rs_small.advance(1)
+        rs_values[1].advance(1)
+        add(2)
+        rs_values[0].advance(2)
+        rs_small.advance(2)
+        rs_values[0].advance(3)
+        rs_values[1].advance(2)
+        add(3)
+        rs_values[1].advance(3)
+        rs_small.advance(3)
+        for stage in range(4, bits):
+            for reduction in rs_out + rs_gate + rs_values + [rs_small]:
+                reduction.advance(stage)
             add(stage)
         heads_ref[...] = vec[bits, nb, :, 0:LANES]
         for b in range(nb):

time: 284 us -> 258 us (0.908)
  Pallas kernels: 250 us -> 225 us
    pallas_call x1, Pallas kernels: 180 us -> 155 us  [back_call(): pl.pallas_call(functools.partial(back_kernel, bits), grid=(3 * nb + chunk...]
where the time goes in v4:
time: 258 us; the launch traced here: 257 us
  Pallas kernels  225 us (87%)
  local copies, waits for them, and re-layouts  28.2 us (11%)
  other arithmetic  3.93 us (2%)
    pallas_call x1, Pallas kernels, back_call(): pl.pallas_call(functools.partial(back_kernel, bits), grid=(3 * nb + chunk...  155 us
    pallas_call x1, Pallas kernels, forward_call(): pl.pallas_call(functools.partial(forward_kernel, size), grid=(2 * nb + ch...  70 us
    unnamed x29, local copies, waits for them, and re-layouts  20.1 us

profile of v4, /device:TPU:0, one launch (start us, length us, event | category | flops | bytes accessed | tf_op | source)
XLA Modules:
  0.0 257.5 jit_solution(11194343600332742130)
XLA Ops:
  0.6 1.3 broadcast_in_dim.17.gain_ref
  1.9 0.0 copy-start.4
  1.9 0.0 copy-start.9
  1.9 0.0 copy-start.7
  1.9 0.0 copy-start.8
  2.0 0.0 copy-start.5
  2.0 8.9 %copy.37 = bf16[1536,2,1536]{2,0,1:T(8,128)(2,1)} copy(bf16[1536,2,1536]{2,1,0:T(2,128)(2,1)} %param.16) | data formatting | bytes 18874368 | tf_op args[3]
  10.8 0.0 copy-done.4
  10.8 0.2 copy.30
  11.1 0.8 pad.14.wstep_ref
  11.9 0.0 copy-done.9
  11.9 0.5 pad_bitcast_fusion.2.bias_ref
  12.4 0.0 copy-done.7
  12.4 0.0 copy-done.8
  12.4 0.5 pad_bitcast_fusion
  12.9 0.0 copy-done.5
  12.9 0.6 broadcast_in_dim.21.ggain_ref
  13.5 70.0 %forward.1 = (bf16[1536,512]{1,0:T(8,128)(2,1)}, f32[512,128]{1,0:T(8,128)}, f32[512,1536]{1,0:T(8,128)}, bf16[528,1536]{1,0:T(8,128)(2,1)}, f32[4,128,1536]{2,1...) custom-call(bf16[512,1536]{1,0:T(8,128)(2,1)} %hid_ref.3, ...), custom_call_target="tpu_custom_call" | custom-call | tf_op jit(solution)/shard_map/forward/pallas_call | solution.py:519
  83.5 1.0 constant_dynamic-slice_fusion
  84.5 2.0 pad_maximum_fusion.wsmall_ref
  86.5 154.6 %back.1 = (f32[96,1536]{1,0:T(8,128)}, f32[6,2,96,128]{3,2,1,0:T(8,128)}, f32[6,2,96,128]{3,2,1,0:T(8,128)}, f32[96,256]{1,0:T(8,128)}, f32[512,1536]{1,0:T(8,12...) custom-call(bf16[1536,512]{1,0:T(8,128)(2,1)} %get-tuple-element.41.gmt_ref, bf16[1536,512]{1,0:T(8,128)(2,1)} %get-tuple-element.42.normedt_ref, ...), custom_call_target="tpu_custom_call" | custom-call | tf_op jit(solution)/shard_map/back/pallas_call | solution.py:1309
  241.1 1.6 slice_reduce_fusion
  242.7 1.3 maximum_bitcast_fusion
  244.0 0.9 copy.34
  245.0 0.0 copy-start.2
  245.0 0.0 copy-start.6
  245.0 2.4 reshape.34
  247.3 0.0 copy-done.2
  247.3 0.7 copy.33
  248.0 0.6 slice.29
  248.6 0.0 copy-done.6
  248.6 0.6 slice.31
  249.2 0.5 slice_bitcast_fusion
  249.8 0.1 reshape_squeeze.3
  249.8 0.6 reduce_sum.9
  250.5 0.0 copy-start
  250.5 3.9 %copy.42 = f32[512,1536]{1,0:T(8,128)} copy(f32[512,1536]{1,0:T(8,128)} %get-tuple-element.113) | data formatting | bytes 6291456
  254.4 0.0 copy-done
  254.4 0.0 copy-start.3
  254.4 0.0 copy-start.1
  254.4 1.7 copy.43
  256.0 0.0 copy-done.3
  256.0 0.6 copy.44
  256.7 0.0 copy-done.1
  256.7 0.8 copy.45
  (1 shorter events, 0.0 us)
Async XLA Ops:
  1.9 8.9 %copy-start.4 = (bf16[1536,24]{0,1:T(8,128)(2,1)S(1)}, bf16[1536,24]{0,1:T(8,128)(2,1)}, u32[]{:S(2)}) copy-start(bf16[1536,24]{0,1:T(8,128)(2,1)} %param.17) | copy-start | bytes 221188
  1.9 9.9 %copy-start.9 = (f32[24]{0:T(128)S(1)}, f32[24]{0:T(128)}, u32[]{:S(2)}) copy-start(f32[24]{0:T(128)} %param.21) | copy-start | bytes 292
  1.9 10.5 %copy-start.7 = (f32[24]{0:T(128)S(1)}, f32[24]{0:T(128)}, u32[]{:S(2)}) copy-start(f32[24]{0:T(128)} %param.23) | copy-start | bytes 292
  1.9 10.5 %copy-start.8 = (f32[24]{0:T(128)S(1)}, f32[24]{0:T(128)}, u32[]{:S(2)}) copy-start(f32[24]{0:T(128)} %param.22) | copy-start | bytes 292
  2.0 11.0 %copy-start.5 = (f32[1536]{0:T(1024)S(1)}, f32[1536]{0:T(1024)}, u32[]{:S(2)}) copy-start(f32[1536]{0:T(1024)} %param.24) | copy-start | bytes 18436
  245.0 2.4 copy-start.2
  245.0 3.7 %copy-start.6 = (f32[8,128]{1,0:T(8,128)S(1)}, f32[8,128]{1,0:T(8,128)}, u32[]{:S(2)}) copy-start(f32[8,128]{1,0:T(8,128)} %get-tuple-element.65) | copy-start | bytes 12292
  250.5 3.9 %copy-start = (f32[512,1536]{1,0:T(8,128)S(1)}, f32[512,1536]{1,0:T(8,128)}, u32[]{:S(2)}) copy-start(f32[512,1536]{1,0:T(8,128)} %get-tuple-element.114) | copy-start | bytes 9437188
  254.4 1.7 copy-start.3
  254.4 2.3 copy-start.1

commit v5 on v4

--- a/solution.py
+++ b/solution.py
@@ -189,7 +189,7 @@
     ]
 
 
-def greet(index, core, size):
+def greet_all(index, core, size):
     barrier = pltpu.get_barrier_semaphore()
     for d in range(1, size):
         pl.semaphore_signal(
@@ -199,7 +199,10 @@
     pl.semaphore_signal(
         barrier, inc=1, device_id={"head": 1 - core}, device_id_type=pl.DeviceIdType.MESH
     )
-    pl.semaphore_wait(barrier, size)
+
+
+def await_all(size):
+    pl.semaphore_wait(pltpu.get_barrier_semaphore(), size)
 
 
 def send_to(src, dst, send_sem, recv_sem, **where):
@@ -250,6 +253,8 @@
 
     @pl.when(step_id == 0)
     def _():
+        greet_all(index, core, size)
+
         @pl.loop(0, chunks)
         def _(i):
             start = pl.multiple_of(i * CHUNK, CHUNK)
@@ -259,7 +264,7 @@
                 nx[pl.ds(pl.multiple_of(HALO + at, HALO), 64), :] = rows
                 scale_ref[pl.ds(at, 64), :] = jnp.broadcast_to(scale, (64, LANES))
 
-        greet(index, core, size)
+        await_all(size)
         after_id = lax.rem(index + 1, size)
         halo_copy = send_to(
             hid_ref.at[pl.ds(tokens - HALO, HALO)], halo, halo_sems.at[0], halo_sems.at[1],
@@ -371,18 +376,20 @@
     def _():
         exchange.turn(step_id - 2)
 
-    def neighbour_copy(bit):
+    def neighbour_copy(bit, first, count):
         mine = (index // (1 << bit)) % 2
+        source = pl.multiple_of(core * half_width + first, LANES)
         return send_to(
-            normedt_ref.at[pl.ds(pl.multiple_of(core * half_width, half_width), half_width)],
-            near_land.at[bit], near_sems.at[0, bit], near_sems.at[1, bit],
+            normedt_ref.at[pl.ds(source, count)],
+            near_land.at[bit, pl.ds(first, count)], near_sems.at[0, bit], near_sems.at[1, bit],
             seq=index + (1 - 2 * mine) * (1 << bit),
         )
 
-    @pl.when(step_id == nb + 1)
-    def _():
+    @pl.when((step_id >= 1) & (step_id <= half_width // LANES))
+    def _():
+        first = pl.multiple_of((step_id - 1) * LANES, LANES)
         for bit in range(2):
-            neighbour_copy(bit).start()
+            neighbour_copy(bit, first, LANES).start()
 
     @pl.when((step_id >= t_mix) & (step_id < t_last))
     def _():
@@ -457,7 +464,7 @@
         @pl.when(c == chunks - 1)
         def _():
             for bit in range(2):
-                neighbour_copy(bit).wait()
+                neighbour_copy(bit, 0, half_width).wait()
                 near_ref[bit] = near_land[bit]
 
 
@@ -665,11 +672,11 @@
 def back_kernel(
     bits,
     gmt_ref, normedt_ref, near_ref, gw_ref, coef_ref, gains_ref, run_ref, step_ref, slope_ref,
-    bc_ref, sext_ref, skip_ref, decay_ref, cs_ref, wsmall_ref, gain_ref,
+    bc_ref, sext_ref, skip_ref, decay_ref, cs_ref, wshared_ref, wstep_ref, gain_ref,
     wout_ref, y_ref, gate_ref, ggain_ref, vext_ref, after_ref, in_ref, cv_ref, runt_ref,
     stept_ref, wi_ref,
     hid_ref, cot_ref, scale_ref,
-    gout_ref, ggw_ref, gvw_ref, gsmall_ref, ghid_ref, sums_ref, heads_ref,
+    gout_ref, ginner_ref, gsmall_ref, ghid_ref, sums_ref,
     w_out, w_gate, w_values, w_small,
     land_out, land_gate, land_values, land_small,
     rs_sems, near, near_sems,
@@ -710,12 +717,14 @@
         )
 
     def columns_reduction(g, part):
-        held, landing, out = ((w_gate, land_gate, ggw_ref), (w_values, land_values, gvw_ref))[g]
+        held, landing = ((w_gate, land_gate), (w_values, land_values))[g]
 
         def put_half(half):
             def put(value):
                 for b in range(half_nb):
-                    out[part * half_nb + b, half] = value[:, b * LANES : (b + 1) * LANES]
+                    lane = (part * half_nb + b) * BLOCK + half * LANES
+                    place = pl.ds(pl.multiple_of(lane, LANES), LANES)
+                    ginner_ref[g, :, place] = value[:, b * LANES : (b + 1) * LANES]
 
             return put
 
@@ -753,10 +762,7 @@
 
     @pl.when(step_id == 0)
     def _():
-        greet(index, core, size)
-        for bit in range(2):
-            for copy in near_copies(bit):
-                copy.start()
+        greet_all(index, core, size)
         for c in range(chunks):
             rows = slice(c * CHUNK, (c + 1) * CHUNK)
             ct[:, rows] = transposed(bc_ref[rows, STATE:])
@@ -764,6 +770,10 @@
                 acc_send[c, :, b * LANES : (b + 1) * LANES] = transposed(
                     gmt_ref[b * LANES : (b + 1) * LANES, rows]
                 )
+        await_all(size)
+        for bit in range(2):
+            for copy in near_copies(bit):
+                copy.start()
 
     group = width // 4
     owners = size // 4
@@ -802,8 +812,9 @@
         held = (w_gate, w_values)[g]
         for q in range(4):
             rows = slice(q * group, (q + 1) * group)
-            piece = mm(normedt_ref[rows, :], own_cols[g, part]) + mm(
-                near[part, rows, :], land_cols[g, part]
+            piece = mm(
+                jnp.concatenate([normedt_ref[rows, :], near[part, rows, :]], axis=1),
+                jnp.concatenate([own_cols[g, part], land_cols[g, part]], axis=0),
             )
 
             def store(slot, value):
@@ -834,7 +845,7 @@
             ggate = (gg * y * (sig * (1.0 + gate * (1.0 - sig)))).astype(bf16)
             ggates[j, rows, :] = ggate
             grow = rolled(jnp.exp(run_ref[rows, :] + offsets[c]), j)[:, :BLOCK_HEADS]
-            own = own + mm_right(ct[:, rows], dy * widen(grow))
+            own = own + mm(ct[:, rows], (dy * widen(grow)).astype(bf16))
         term_gate[j, 0:1, :] = term
         exchange.send(j, own)
         split_block(0, j, ggates[j])
@@ -942,8 +953,8 @@
             enter = widen(base) * in_ref[...]
             if c:
                 enter = enter + after_ref[c - 1]
-            du_state = tail * mm_right(b_rows, dstate)
-            carried = grow * mm_right(c_rows, enter)
+            du_state = tail * mm(b_rows, dstate.astype(bf16))
+            carried = grow * mm(c_rows, enter.astype(bf16))
             weighted = wide_x * (tail * step_w)
             grown = dy * grow
             dbc[0, rows, :] += mm_both(weighted, dstate, NT)
@@ -976,16 +987,18 @@
                     dcols[j, head : head + 1, rows] = jnp.sum(full, axis=0, keepdims=True)
                     keep_t = jnp.exp(jnp.where(mask_t, row - col, -1e30))
                     mats.append(scorest[c] * keep_t)
-                du_pairs.append(mm_both(jnp.concatenate(mats, axis=1), both))
+                du_pairs.append(
+                    mm(jnp.concatenate(mats, axis=1).astype(bf16), both.astype(bf16))
+                )
             dscores[c] = dscore
             du = jnp.concatenate(du_pairs, axis=1) + du_state
-            by_head = mm_left(
+            by_head = mm(
                 jnp.concatenate(
                     [
-                        wide_x * du,
-                        dy * carried,
-                        wide_x * du_state,
-                        jnp.broadcast_to(hold, (HALO, BLOCK)),
+                        (wide_x * du).astype(bf16),
+                        (dy * carried).astype(bf16),
+                        (wide_x * du_state).astype(bf16),
+                        *parts(jnp.broadcast_to(hold, (HALO, BLOCK))),
                     ],
                     axis=0,
                 ),
@@ -994,7 +1007,10 @@
             xdu[rows, :] += by_head[0:CHUNK, :]
             dyc[rows, :] += by_head[CHUNK : 2 * CHUNK, :] + col_sum
             xdus[rows, :] += by_head[2 * CHUNK : 3 * CHUNK, :]
-            ends[c : c + 1, :] += by_head[3 * CHUNK : 3 * CHUNK + 1, :]
+            end = 3 * CHUNK
+            ends[c : c + 1, :] += (
+                by_head[end : end + 1, :] + by_head[end + HALO : end + HALO + 1, :]
+            )
             dskip = dskip + jnp.sum(dy * wide_x, axis=0, keepdims=True)
             gconv = (step_w * du + skip * dy) * slope
             gext[rows, :] = gconv
@@ -1164,7 +1180,11 @@
     @pl.when((step_id >= t_grad) & (step_id < t_final))
     def _():
         j = step_id - t_grad
-        part = mm(ggates[j], wi_ref[0], NT) + mm(gv[j], wi_ref[1], NT)
+        part = mm(
+            jnp.concatenate([ggates[j], gv[j]], axis=1),
+            jnp.concatenate([wi_ref[0], wi_ref[1]], axis=1),
+            NT,
+        )
 
         @pl.when(j == 0)
         def _():
@@ -1188,7 +1208,10 @@
     @when_after(t_grad + 4)
     def _():
         rs_gate[1].advance(2)
-        rest = mm(small[...], wsmall_ref[...], NT)
+        own = pl.ds(pl.multiple_of(core * LANES, LANES), LANES)
+        rest = mm(
+            small[...], jnp.concatenate([wshared_ref[:, own], wstep_ref[...]], axis=1), NT
+        )
         for b in range(width // BLOCK):
             dys[b] += rest[:, b * BLOCK : (b + 1) * BLOCK]
 
@@ -1265,14 +1288,14 @@
             for reduction in rs_out + rs_gate + rs_values + [rs_small]:
                 reduction.advance(stage)
             add(stage)
-        heads_ref[...] = vec[bits, nb, :, 0:LANES]
+        sums_ref[8:16, 0:BLOCK] = vec[bits, nb]
         for b in range(nb):
-            sums_ref[:, b * BLOCK : (b + 1) * BLOCK] = vec[bits, b]
+            sums_ref[0:8, b * BLOCK : (b + 1) * BLOCK] = vec[bits, b]
 
 
 def back_call(
     gm_t, normed_t, near, gated_w, coef, gains, run, step, slope, bc, sext, skip, decay,
-    conv_shared, wsmall, gain, wout, y, gate, gate_gain, vext, after, state_in, conv_values, runt, stept, both,
+    conv_shared, wshared, wstep, gain, wout, y, gate, gate_gain, vext, after, state_in, conv_values, runt, stept, both,
     hidden, cotangent, scale,
 ):
     width, tokens = normed_t.shape
@@ -1325,6 +1348,7 @@
             full((1, LANES)),
             full((2, CONV + 1, LANES)),
             full((width, 2 * LANES)),
+            full((width, LANES)),
             full((1, width)),
             cols(width, 0),
             cols(tokens, 0),
@@ -1347,21 +1371,17 @@
         ],
         out_shape=[
             jax.ShapeDtypeStruct((rows_own, inner), f32),
-            jax.ShapeDtypeStruct((nb, 2, rows_own, LANES), f32),
-            jax.ShapeDtypeStruct((nb, 2, rows_own, LANES), f32),
+            jax.ShapeDtypeStruct((2, rows_own, inner), f32),
             jax.ShapeDtypeStruct((rows_own, 2 * LANES), f32),
             jax.ShapeDtypeStruct((tokens, width), f32),
-            jax.ShapeDtypeStruct((8, inner), f32),
-            jax.ShapeDtypeStruct((8, LANES), f32),
+            jax.ShapeDtypeStruct((16, inner), f32),
         ],
         out_specs=[
             full((rows_own, inner)),
-            full((nb, 2, rows_own, LANES)),
-            full((nb, 2, rows_own, LANES)),
+            full((2, rows_own, inner)),
             full((rows_own, 2 * LANES)),
             row_block(width),
-            pl.BlockSpec((8, inner), lambda s: (0, 0)),
-            pl.BlockSpec((8, LANES), lambda s: (0, 0)),
+            pl.BlockSpec((16, inner), lambda s: (0, 0)),
         ],
         scratch_shapes=[
             held(inner // 2), held(inner // 4), held(inner // 4),
@@ -1411,7 +1431,8 @@
         name="back",
     )(
         gm_t, normed_t, near, gated_w, coef, gains, run, step, slope, bc, sext, skip, decay,
-        conv_shared, wsmall, gain, wout, y, gate, gate_gain, vext, after, state_in, conv_values,
+        conv_shared, wshared, wstep, gain, wout, y, gate, gate_gain, vext, after, state_in,
+        conv_values,
         runt, stept,
         both, hidden, cotangent, scale,
     )
@@ -1429,10 +1450,11 @@
     shared_here = conv_shared.shape[1] // lax.axis_size("head")
     shared_start = lax.axis_index("head") * shared_here
     both = jnp.transpose(proj_inner, (1, 0, 2))
-    lanes = lambda v: jnp.pad(v, (0, LANES - heads))[None, :]
+    rows = [jnp.pad(v, (0, width - v.shape[0])) for v in (step_bias, decay_log, skip_gain)]
+    rows = jnp.stack(rows + [norm_gain])
     wstep = jnp.pad(proj_step, ((0, 0), (0, LANES - heads)))
-    bias, decay, skip = lanes(step_bias), lanes(decay_log), lanes(skip_gain)
-    wshared_own = lax.dynamic_slice_in_dim(proj_shared, shared_start, shared_here, 1)
+    bias, decay, skip, gain = (rows[i : i + 1] for i in range(4))
+    bias, decay, skip = bias[:, :LANES], decay[:, :LANES], skip[:, :LANES]
     (
         normed_t, norm_scale, gate_in, vext, after, y, gated_w, state_in, step, slope, run, runt,
         stept, sext, bc, gains, block_out, gm_t, coef, near,
@@ -1440,10 +1462,10 @@
         hidden, cotangent, norm_gain[None, :], both, wstep, proj_shared, conv_values, conv_shared,
         bias, decay, skip, gate_gain[None, :], proj_out,
     )
-    (gout, ggw, gvw, gsmall, grad_hidden, sums, head_sums) = back_call(
+    (gout, ginner, gsmall, grad_hidden, sums) = back_call(
         gm_t, normed_t, near, gated_w, coef, gains, run, step, slope, bc, sext, skip, decay,
         conv_shared.reshape(CONV + 1, -1, LANES).transpose(1, 0, 2),
-        jnp.concatenate([wshared_own, wstep], axis=1), norm_gain[None, :], proj_out, y, gate_in,
+        proj_shared, wstep, norm_gain[None, :], proj_out, y, gate_in,
         gate_gain[None, :], vext, after, state_in, conv_values, runt, stept, both, hidden,
         cotangent, norm_scale,
     )
@@ -1451,13 +1473,13 @@
         block_out,
         grad_hidden,
         sums[7],
-        jnp.stack([ggw, gvw]).transpose(3, 0, 1, 2, 4).reshape(-1, 2, inner),
+        ginner.transpose(1, 0, 2),
         gsmall[:, shared_here : shared_here + heads],
         gsmall[:, :shared_here],
         sums[: CONV + 1],
-        head_sums[2 : 3 + CONV],
-        head_sums[0, :heads],
-        head_sums[1, :heads],
+        sums[10 : 11 + CONV, :LANES],
+        sums[8, :heads],
+        sums[9, :heads],
         jnp.sum(sums[CONV + 2].reshape(heads, HEAD_DIM), axis=1),
         sums[CONV + 1],
         gout,

time: 258 us -> 252 us (0.977)
  Pallas kernels: 225 us -> 218 us
  local copies, waits for them, and re-layouts: 28.2 us -> 31.5 us
  other arithmetic: 3.93 us -> 0.63 us
    pallas_call x1, Pallas kernels: 70 us -> 64.6 us  [forward_call(): pl.pallas_call(functools.partial(forward_kernel, size), grid=(2 * nb + ch...]
    slice x1 -> x5, local copies, waits for them, and re-layouts: 0.6 us -> 4.23 us  [the longest x3 1.54 us: body(): bias, decay, skip = (bias[:, :LANES], decay[:, :LANES], skip[:, :LANES])]
    unnamed x29 -> x21, local copies, waits for them, and re-layouts: 20.1 us -> 19.4 us
where the time goes in v5:
time: 252 us; the launch traced here: 251 us
  Pallas kernels  218 us (87%)
  local copies, waits for them, and re-layouts  31.5 us (12%)
    pallas_call x1, Pallas kernels, back_call(): pl.pallas_call(functools.partial(back_kernel, bits), grid=(3 * nb + chunk...  154 us
    pallas_call x1, Pallas kernels, forward_call(): pl.pallas_call(functools.partial(forward_kernel, size), grid=(2 * nb + ch...  64.6 us
    unnamed x21, local copies, waits for them, and re-layouts  19.4 us

profile of v5, /device:TPU:0, one launch (start us, length us, event | category | flops | bytes accessed | tf_op | source)
XLA Modules:
  0.0 251.0 jit_solution(12457808974669813322)
XLA Ops:
  0.6 1.3 broadcast_in_dim.8.gain_ref
  1.9 0.0 copy-start.2
  1.9 0.0 copy-start.4
  1.9 0.0 copy-start.5
  1.9 0.0 copy-start.6
  1.9 0.0 copy-start.3
  2.0 8.9 %copy.31 = bf16[1536,2,1536]{2,0,1:T(8,128)(2,1)} copy(bf16[1536,2,1536]{2,1,0:T(2,128)(2,1)} %param.16) | data formatting | bytes 18874368 | tf_op args[3]
  10.8 0.0 copy-done.2
  10.8 0.2 copy.27
  11.1 0.8 pad.14.wstep_ref
  11.9 0.0 copy-done.4
  11.9 0.5 slice.48.bias_ref
  12.4 0.0 copy-done.5
  12.4 0.5 slice.49.decay_ref
  12.9 0.0 copy-done.6
  13.0 0.5 slice.50.skip_ref
  13.5 0.0 copy-done.3
  13.5 0.6 broadcast_in_dim.9.ggain_ref
  14.1 64.6 %forward.1 = (bf16[1536,512]{1,0:T(8,128)(2,1)}, f32[512,128]{1,0:T(8,128)}, f32[512,1536]{1,0:T(8,128)}, bf16[528,1536]{1,0:T(8,128)(2,1)}, f32[4,128,1536]{2,1...) custom-call(bf16[512,1536]{1,0:T(8,128)(2,1)} %hid_ref.3, ...), custom_call_target="tpu_custom_call" | custom-call | tf_op jit(solution)/shard_map/forward/pallas_call | solution.py:526
  78.6 153.6 %back.1 = (f32[96,1536]{1,0:T(8,128)}, f32[2,96,1536]{2,1,0:T(8,128)}, f32[96,256]{1,0:T(8,128)}, f32[512,1536]{1,0:T(8,128)}, f32[16,1536]{1,0:T(8,128)}) custom-call(bf16[1536,512]{1,0:T(8,128)(2,1)} %get-tuple-element.39.gmt_ref, bf16[1536,512]{1,0:T(8,128)(2,1)} %get-tuple-element.40.normedt_ref, bf16[2,768,512]{2,1,0:T(8,128)(2,1)} %get-tuple-element.41.near_ref, ...), custom_call_target="tpu_custom_call" | custom-call | tf_op jit(solution)/shard_map/back/pallas_call | solution.py:1332
  232.3 1.6 slice_reduce_fusion
  233.8 3.2 %copy.28 = f32[96,2,1536]{2,1,0:T(2,128)} copy(f32[96,2,1536]{2,0,1:T(8,128)} %bitcast.13) | data formatting | bytes 2359296
  237.0 0.8 slice.40
  237.8 0.7 copy.29
  238.5 1.4 slice.41
  239.9 1.4 slice.42
  241.3 1.3 slice.43
  242.6 1.3 slice_bitcast_fusion
  243.9 0.1 reshape_squeeze.3
  243.9 0.6 reduce_sum.9
  244.6 0.0 copy-start
  244.6 3.9 %copy.35 = f32[512,1536]{1,0:T(8,128)} copy(f32[512,1536]{1,0:T(8,128)} %get-tuple-element.94) | data formatting | bytes 6291456
  248.5 0.0 copy-done
  248.5 0.0 copy-start.1
  248.5 1.7 copy.36
  250.1 0.0 copy-done.1
  250.2 0.8 copy.37
  (6 shorter events, 0.0 us)
Async XLA Ops:
  1.9 8.9 %copy-start.2 = (bf16[1536,24]{0,1:T(8,128)(2,1)S(1)}, bf16[1536,24]{0,1:T(8,128)(2,1)}, u32[]{:S(2)}) copy-start(bf16[1536,24]{0,1:T(8,128)(2,1)} %param.17) | copy-start | bytes 221188
  1.9 10.0 %copy-start.4 = (f32[24]{0:T(128)S(1)}, f32[24]{0:T(128)}, u32[]{:S(2)}) copy-start(f32[24]{0:T(128)} %param.21) | copy-start | bytes 292
  1.9 10.5 %copy-start.5 = (f32[24]{0:T(128)S(1)}, f32[24]{0:T(128)}, u32[]{:S(2)}) copy-start(f32[24]{0:T(128)} %param.22) | copy-start | bytes 292
  1.9 11.0 %copy-start.6 = (f32[24]{0:T(128)S(1)}, f32[24]{0:T(128)}, u32[]{:S(2)}) copy-start(f32[24]{0:T(128)} %param.23) | copy-start | bytes 292
  1.9 11.5 %copy-start.3 = (f32[1536]{0:T(1024)S(1)}, f32[1536]{0:T(1024)}, u32[]{:S(2)}) copy-start(f32[1536]{0:T(1024)} %param.24) | copy-start | bytes 18436
  244.6 3.9 %copy-start = (f32[512,1536]{1,0:T(8,128)S(1)}, f32[512,1536]{1,0:T(8,128)}, u32[]{:S(2)}) copy-start(f32[512,1536]{1,0:T(8,128)} %get-tuple-element.95) | copy-start | bytes 9437188
  248.5 1.7 copy-start.1

commit v6 on v5

--- a/solution.py
+++ b/solution.py
@@ -222,7 +222,7 @@
     skip_ref, ggain_ref, wout_ref, hrow_ref, crow_ref,
     normedt_ref, scale_ref, gate_ref, vext_ref, after_ref, y_ref, gw_ref, in_ref, step_ref,
     slope_ref, run_ref, runt_ref, stept_ref, sext_ref, bc_ref, gains_ref, out_ref, gmt_ref,
-    coef_ref, near_ref,
+    coef_ref, near_ref, rows_ref,
     nx, halo, halo_sems, scores, bt, end_w, vwide, gates, ys, states, acc, acc_send,
     acc_land, acc_sems, squares, sq_land, sq_sems, totals, totals_land, totals_sems,
     near_land, near_sems, ex_own, ex_landing, ex_mixed, ex_result, ex_sems,
@@ -243,7 +243,7 @@
     def norm_rows(rows):
         wide = rows.astype(f32)
         scale = lax.rsqrt(jnp.mean(wide * wide, axis=1, keepdims=True) + norm_eps)
-        return (wide * scale * gain_ref[...]).astype(bf16), scale
+        return (wide * scale * gain_ref[...][None, :]).astype(bf16), scale
 
     def totals_copy(d):
         return send_to(
@@ -276,12 +276,18 @@
                 normedt_ref[b * LANES : (b + 1) * LANES, c * CHUNK : (c + 1) * CHUNK] = transposed(
                     nx[HALO + c * CHUNK : HALO + (c + 1) * CHUNK, b * LANES : (b + 1) * LANES]
                 )
-        raw = mm(nx[HALO:, :], wstep_ref[...]) + bias_ref[...]
+        rows_ref[...] = jnp.zeros_like(rows_ref)
+        heads = bias_ref.shape[0]
+        for i, ref in enumerate((bias_ref, decay_ref, skip_ref)):
+            rows_ref[i, 0:heads] = ref[...]
+        raw = mm(nx[HALO:, :], wstep_ref[...])
+        raw = jnp.concatenate([raw, jnp.zeros((tokens, LANES - heads), f32)], axis=1)
+        raw = raw + rows_ref[0:1, :]
         small = jnp.exp(-jnp.abs(raw))
         step = jnp.maximum(raw, 0.0) + jnp.log1p(small)
         step_ref[...] = step
         slope_ref[...] = 1.0 / (1.0 + jnp.exp(-raw))
-        rate = -step * jnp.exp(decay_ref[...])
+        rate = -step * jnp.exp(rows_ref[1:2, :])
         tri = causal().astype(f32)
         total = jnp.zeros((1, LANES), f32)
         for c in range(chunks):
@@ -340,7 +346,7 @@
         gate_ref[...] = gate
         gates[j] = gate
         mask = causal()
-        skip = widen(rolled(skip_ref[...], j)[:, :BLOCK_HEADS])
+        skip = widen(rolled(rows_ref[2:3, :], j)[:, :BLOCK_HEADS])
         for c in range(chunks):
             rows = slice(c * CHUNK, (c + 1) * CHUNK)
             cols = run_cols[rows, :BLOCK_HEADS]
@@ -521,6 +527,7 @@
         ((width, tokens), bf16, pl.BlockSpec((width, CHUNK), lambda s: (0, row_of(s)))),
         ((tokens, LANES), f32, row_block(LANES)),
         ((2, width // 2, tokens), bf16, full((2, width // 2, tokens))),
+        ((8, LANES), f32, full((8, LANES))),
     ]
     sem = pltpu.SemaphoreType.DMA
     return pl.pallas_call(
@@ -528,15 +535,15 @@
         grid=(2 * nb + chunks,),
         in_specs=[
             full((tokens, width)),
-            full((1, width)),
+            full((width,)),
             pl.BlockSpec((2, width, BLOCK), lambda s: (0, 0, at(0)(s))),
-            full((width, LANES)),
+            full(wstep.shape),
             full((width, 2 * STATE)),
             cols(CONV + 1, 0),
             full((CONV + 1, 2 * STATE)),
-            full((1, LANES)),
-            full((1, LANES)),
-            full((1, LANES)),
+            full(bias.shape),
+            full(decay.shape),
+            full(skip.shape),
             cols(1, t_mix),
             cols(width, t_mix),
             row_block(width),
@@ -672,7 +679,7 @@
 def back_kernel(
     bits,
     gmt_ref, normedt_ref, near_ref, gw_ref, coef_ref, gains_ref, run_ref, step_ref, slope_ref,
-    bc_ref, sext_ref, skip_ref, decay_ref, cs_ref, wshared_ref, wstep_ref, gain_ref,
+    bc_ref, sext_ref, rows_ref, cs_ref, wshared_ref, wstep_ref, gain_ref,
     wout_ref, y_ref, gate_ref, ggain_ref, vext_ref, after_ref, in_ref, cv_ref, runt_ref,
     stept_ref, wi_ref,
     hid_ref, cot_ref, scale_ref,
@@ -926,7 +933,7 @@
         run_cols = rolled(run_ref[...], j)
         step_cols = rolled(step_ref[...], j)
         end_cols = rolled(end_w[...], j)
-        skip = widen(rolled(skip_ref[...], j)[:, :BLOCK_HEADS])
+        skip = widen(rolled(rows_ref[2:3, :], j)[:, :BLOCK_HEADS])
         channel = lax.broadcasted_iota(jnp.int32, (BLOCK, LANES), 0) // HEAD_DIM
         lane = lax.broadcasted_iota(jnp.int32, (BLOCK, LANES), 1)
         pick = (lane == BLOCK_HEADS * j + channel).astype(bf16)
@@ -1039,7 +1046,8 @@
             vec[0, j, k : k + 1, :] = tap
         vec[0, j, CONV : CONV + 1, :] = taps[CONV]
         vec[0, j, CONV + 1 : CONV + 2, :] = term_gate[j, 0:1, :]
-        vec[0, j, CONV + 2 : CONV + 3, :] = dskip
+        by_head = mm(jnp.concatenate(parts(jnp.broadcast_to(dskip, (HALO, BLOCK))), axis=0), pick)
+        vec[0, nb, 7:8, 0:LANES] += by_head[0:1, :] + by_head[HALO : HALO + 1, :]
         edge_tail[j, 8 : 8 + CONV + 1, :] = cv_ref[...]
         edge_own[j] = gext[0:8, :]
         send_to(
@@ -1090,7 +1098,7 @@
         tri = mask.astype(f32)
         tri_t = mask_t.astype(f32)
         strict = (rows_i > cols_i).astype(f32)
-        decay = jnp.exp(decay_ref[...])
+        decay = jnp.exp(rows_ref[1:2, :])
         bias_sum = jnp.zeros((1, LANES), f32)
         decay_sum = jnp.zeros((1, LANES), f32)
         for c in range(chunks):
@@ -1209,8 +1217,9 @@
     def _():
         rs_gate[1].advance(2)
         own = pl.ds(pl.multiple_of(core * LANES, LANES), LANES)
-        rest = mm(
-            small[...], jnp.concatenate([wshared_ref[:, own], wstep_ref[...]], axis=1), NT
+        heads = wstep_ref.shape[1]
+        rest = mm(small[:, 0:LANES], wshared_ref[:, own], NT) + mm(
+            small[:, LANES : LANES + heads], wstep_ref[...], NT
         )
         for b in range(width // BLOCK):
             dys[b] += rest[:, b * BLOCK : (b + 1) * BLOCK]
@@ -1242,7 +1251,7 @@
             piece = term[:, b * BLOCK : (b + 1) * BLOCK]
             vec[0, b, 7:8, :] = vec[0, b, 7:8, :] + piece
 
-        ghat = total * gain_ref[...]
+        ghat = total * gain_ref[...][None, :]
         mean = jnp.mean(ghat * hat, axis=1, keepdims=True)
         ghid_ref[...] = cot_ref[...].astype(f32) + scale * (ghat - hat * mean)
 
@@ -1294,7 +1303,7 @@
 
 
 def back_call(
-    gm_t, normed_t, near, gated_w, coef, gains, run, step, slope, bc, sext, skip, decay,
+    gm_t, normed_t, near, gated_w, coef, gains, run, step, slope, bc, sext, rows,
     conv_shared, wshared, wstep, gain, wout, y, gate, gate_gain, vext, after, state_in, conv_values, runt, stept, both,
     hidden, cotangent, scale,
 ):
@@ -1344,12 +1353,11 @@
             full((tokens, LANES)),
             full((tokens, 2 * STATE)),
             full((2, HALO + tokens, LANES)),
-            full((1, LANES)),
-            full((1, LANES)),
+            full((8, LANES)),
             full((2, CONV + 1, LANES)),
             full((width, 2 * LANES)),
-            full((width, LANES)),
-            full((1, width)),
+            full(wstep.shape),
+            full((width,)),
             cols(width, 0),
             cols(tokens, 0),
             cols(tokens, 0),
@@ -1430,12 +1438,60 @@
         ),
         name="back",
     )(
-        gm_t, normed_t, near, gated_w, coef, gains, run, step, slope, bc, sext, skip, decay,
+        gm_t, normed_t, near, gated_w, coef, gains, run, step, slope, bc, sext, rows,
         conv_shared, wshared, wstep, gain, wout, y, gate, gate_gain, vext, after, state_in,
         conv_values,
         runt, stept,
         both, hidden, cotangent, scale,
     )
+
+
+def final_kernel(
+    heads, out_ref, ghid_ref, gout_ref, ginner_ref, gsmall_ref, sums_ref,
+    out_to, ghid_to, gout_to, inner_to, step_to, shared_to, norm_to, gate_to, taps_to, staps_to,
+    bias_to, decay_to, skip_to,
+):
+    out_to[...] = out_ref[...]
+    ghid_to[...] = ghid_ref[...]
+
+    @pl.when(pl.program_id(0) == 0)
+    def _():
+        gout_to[...] = gout_ref[...]
+        for g in range(2):
+            inner_to[:, g, :] = ginner_ref[g]
+        shared_to[...] = gsmall_ref[:, 0:LANES]
+        step_to[...] = gsmall_ref[:, LANES : LANES + heads]
+        taps_to[...] = sums_ref[0 : CONV + 1, :]
+        gate_to[...] = sums_ref[CONV + 1, :]
+        norm_to[...] = sums_ref[7, :]
+        bias_to[...] = sums_ref[8, 0:heads]
+        decay_to[...] = sums_ref[9, 0:heads]
+        staps_to[...] = sums_ref[10 : 11 + CONV, 0:LANES]
+        skip_to[...] = sums_ref[15, 0:heads]
+
+
+def final_call(heads, block_out, grad_hidden, gout, ginner, gsmall, sums):
+    tokens, width = block_out.shape
+    rows_own, inner = gout.shape
+    rows = 64
+    shapes = [
+        (tokens, width), (tokens, width), (rows_own, inner), (rows_own, 2, inner),
+        (rows_own, heads), (rows_own, LANES), (width,), (inner,), (CONV + 1, inner),
+        (CONV + 1, LANES), (heads,), (heads,), (heads,),
+    ]
+
+    def full(shape):
+        return pl.BlockSpec(shape, lambda i: (0,) * len(shape), pipeline_mode=pl.Buffered(1))
+
+    block = lambda: pl.BlockSpec((rows, width), lambda i: (i, 0))
+    return pl.pallas_call(
+        functools.partial(final_kernel, heads),
+        grid=(tokens // rows,),
+        in_specs=[block(), block()] + [full(a.shape) for a in (gout, ginner, gsmall, sums)],
+        out_shape=[jax.ShapeDtypeStruct(shape, f32) for shape in shapes],
+        out_specs=[block(), block()] + [full(shape) for shape in shapes[2:]],
+        name="final",
+    )(block_out, grad_hidden, gout, ginner, gsmall, sums)
 
 
 def body(
@@ -1447,42 +1503,28 @@
     heads = proj_step.shape[1]
     width = hidden.shape[1]
     size = lax.axis_size("seq")
-    shared_here = conv_shared.shape[1] // lax.axis_size("head")
-    shared_start = lax.axis_index("head") * shared_here
     both = jnp.transpose(proj_inner, (1, 0, 2))
-    rows = [jnp.pad(v, (0, width - v.shape[0])) for v in (step_bias, decay_log, skip_gain)]
-    rows = jnp.stack(rows + [norm_gain])
-    wstep = jnp.pad(proj_step, ((0, 0), (0, LANES - heads)))
-    bias, decay, skip, gain = (rows[i : i + 1] for i in range(4))
-    bias, decay, skip = bias[:, :LANES], decay[:, :LANES], skip[:, :LANES]
     (
         normed_t, norm_scale, gate_in, vext, after, y, gated_w, state_in, step, slope, run, runt,
         stept, sext, bc, gains, block_out, gm_t, coef, near,
+        rows,
     ) = forward_call(
-        hidden, cotangent, norm_gain[None, :], both, wstep, proj_shared, conv_values, conv_shared,
-        bias, decay, skip, gate_gain[None, :], proj_out,
+        hidden, cotangent, norm_gain, both, proj_step, proj_shared, conv_values, conv_shared,
+        step_bias, decay_log, skip_gain, gate_gain[None, :], proj_out,
     )
     (gout, ginner, gsmall, grad_hidden, sums) = back_call(
-        gm_t, normed_t, near, gated_w, coef, gains, run, step, slope, bc, sext, skip, decay,
-        conv_shared.reshape(CONV + 1, -1, LANES).transpose(1, 0, 2),
-        proj_shared, wstep, norm_gain[None, :], proj_out, y, gate_in,
-        gate_gain[None, :], vext, after, state_in, conv_values, runt, stept, both, hidden,
-        cotangent, norm_scale,
+        gm_t, normed_t, near, gated_w, coef, gains, run, step, slope, bc, sext, rows,
+        conv_shared.reshape(CONV + 1, -1, LANES).transpose(1, 0, 2), proj_shared, proj_step,
+        norm_gain, proj_out, y, gate_in, gate_gain[None, :], vext, after, state_in, conv_values,
+        runt, stept, both, hidden, cotangent, norm_scale,
     )
+    (
+        block_out, grad_hidden, gout, ginner, gstep, gshared, gnorm, ggain, gtaps, gstaps, gbias,
+        gdecay, gskip,
+    ) = final_call(heads, block_out, grad_hidden, gout, ginner, gsmall, sums)
     return (
-        block_out,
-        grad_hidden,
-        sums[7],
-        ginner.transpose(1, 0, 2),
-        gsmall[:, shared_here : shared_here + heads],
-        gsmall[:, :shared_here],
-        sums[: CONV + 1],
-        sums[10 : 11 + CONV, :LANES],
-        sums[8, :heads],
-        sums[9, :heads],
-        jnp.sum(sums[CONV + 2].reshape(heads, HEAD_DIM), axis=1),
-        sums[CONV + 1],
-        gout,
+        block_out, grad_hidden, gnorm, ginner, gstep, gshared, gtaps, gstaps, gbias, gdecay, gskip,
+        ggain, gout,
     )
 
 

time: 252 us -> 241 us (0.956)
  local copies, waits for them, and re-layouts: 31.5 us -> 11.8 us
  Pallas kernels: 218 us -> 228 us
    pallas_call x0 -> x1, Pallas kernels: none -> 9.24 us  [final_call(): pl.pallas_call(functools.partial(final_kernel, heads), grid=(tokens // ro...]
    unnamed x21 -> x7, local copies, waits for them, and re-layouts: 19.4 us -> 11.2 us
    slice x8 -> x0, local copies, waits for them, and re-layouts: 8.02 us -> none  [the longest x1 1.57 us: body(): sums[CONV + 1]]
where the time goes in v6:
time: 241 us; the launch traced here: 240 us
  Pallas kernels  228 us (95%)
  local copies, waits for them, and re-layouts  11.8 us (5%)
    pallas_call x1, Pallas kernels, back_call(): pl.pallas_call(functools.partial(back_kernel, bits), grid=(3 * nb + chunk...  154 us
    pallas_call x1, Pallas kernels, forward_call(): pl.pallas_call(functools.partial(forward_kernel, size), grid=(2 * nb + ch...  64.7 us
    unnamed x7, local copies, waits for them, and re-layouts  11.2 us
    pallas_call x1, Pallas kernels, final_call(): pl.pallas_call(functools.partial(final_kernel, heads), grid=(tokens // ro...  9.24 us

profile of v6, /device:TPU:0, one launch (start us, length us, event | category | flops | bytes accessed | tf_op | source)
XLA Modules:
  0.0 240.2 jit_solution(18348843448872802012)
XLA Ops:
  0.6 0.0 copy-start
  0.7 0.0 copy-start.1
  0.7 8.8 %copy.31 = bf16[1536,2,1536]{2,0,1:T(8,128)(2,1)} copy(bf16[1536,2,1536]{2,1,0:T(2,128)(2,1)} %param.16) | data formatting | bytes 18874368 | tf_op args[3]
  9.5 0.0 copy-done
  9.5 0.9 copy.27.wstep_ref
  10.4 0.0 copy-done.1
  10.4 0.6 broadcast_in_dim.4.ggain_ref
  11.0 64.7 %forward.1 = (bf16[1536,512]{1,0:T(8,128)(2,1)}, f32[512,128]{1,0:T(8,128)}, f32[512,1536]{1,0:T(8,128)}, bf16[528,1536]{1,0:T(8,128)(2,1)}, f32[4,128,1536]{2,1...) custom-call(bf16[512,1536]{1,0:T(8,128)(2,1)} %hid_ref.3, ...), custom_call_target="tpu_custom_call" | custom-call | tf_op jit(solution)/shard_map/forward/pallas_call | solution.py:533
  75.7 153.7 %back.1 = (f32[96,1536]{1,0:T(8,128)}, f32[2,96,1536]{2,1,0:T(8,128)}, f32[96,256]{1,0:T(8,128)}, f32[512,1536]{1,0:T(8,128)}, f32[16,1536]{1,0:T(8,128)}) custom-call(bf16[1536,512]{1,0:T(8,128)(2,1)} %get-tuple-element.53.gmt_ref, bf16[1536,512]{1,0:T(8,128)(2,1)} %get-tuple-element.54.normedt_ref, bf16[2,768,512]{2,1,0:T(8,128)(2,1)} %get-tuple-element.55.near_ref, ...), custom_call_target="tpu_custom_call" | custom-call | tf_op jit(solution)/shard_map/back/pallas_call | solution.py:1341
  229.5 9.2 %final.1 = (f32[512,1536]{1,0:T(8,128)}, f32[512,1536]{1,0:T(8,128)}, f32[96,1536]{1,0:T(8,128)}, f32[96,2,1536]{2,1,0:T(2,128)}, f32[96,24]{1,0:T(8,128)}, /*in...) custom-call(f32[512,1536]{1,0:T(8,128)} %get-tuple-element.52.out_re, ...), custom_call_target="tpu_custom_call" | custom-call | tf_op jit(solution)/shard_map/final/pallas_call | solution.py:1487
  238.7 1.5 copy.29
Async XLA Ops:
  0.6 8.8 %copy-start = (bf16[1536,24]{0,1:T(8,128)(2,1)S(1)}, bf16[1536,24]{0,1:T(8,128)(2,1)}, u32[]{:S(2)}) copy-start(bf16[1536,24]{0,1:T(8,128)(2,1)} %param.17) | copy-start | bytes 221188
  0.7 9.8 %copy-start.1 = (f32[1536]{0:T(1024)S(1)}, f32[1536]{0:T(1024)}, u32[]{:S(2)}) copy-start(f32[1536]{0:T(1024)} %param.24) | copy-start | bytes 18436

commit v7 on v6

--- a/solution.py
+++ b/solution.py
@@ -809,19 +809,26 @@
     def split_block(g, j, value):
         part = j // half_nb
         mine = jnp.where(part == 0, bit_of(0), bit_of(1))
-        place = pl.ds(pl.multiple_of((j % half_nb) * LANES, LANES), LANES)
+        place = j % half_nb
         first, second = value[:, :LANES], value[:, LANES:]
-        own_cols[g, part, :, place] = jnp.where(mine == 0, first, second)
-        other_cols[g, part, :, place] = jnp.where(mine == 0, second, first)
+        own_cols[g, part, place] = jnp.where(mine == 0, first, second)
+        other_cols[g, part, place] = jnp.where(mine == 0, second, first)
+        partner = flip_of(0) + part * (flip_of(1) - flip_of(0))
+        send_to(
+            other_cols.at[g, part, place], land_cols.at[g, part, place],
+            cols_sems.at[0, g, part], cols_sems.at[1, g, part], seq=partner,
+        ).start()
 
     def put_columns(g, part):
         columns_copy(g, part).wait()
+        side = lambda ref: jnp.concatenate([ref[g, part, b] for b in range(half_nb)], axis=1)
+        right = jnp.concatenate([side(own_cols), side(land_cols)], axis=0)
         held = (w_gate, w_values)[g]
         for q in range(4):
             rows = slice(q * group, (q + 1) * group)
             piece = mm(
                 jnp.concatenate([normedt_ref[rows, :], near[part, rows, :]], axis=1),
-                jnp.concatenate([own_cols[g, part], land_cols[g, part]], axis=0),
+                right,
             )
 
             def store(slot, value):
@@ -888,13 +895,8 @@
     def _():
         exchange.turn(step_id - 2)
 
-    @when_after(half_nb - 1)
-    def _():
-        columns_copy(0, 0).start()
-
     @when_after(nb - 1)
     def _():
-        columns_copy(0, 1).start()
         for bit in range(2):
             for copy in near_copies(bit):
                 copy.wait()
@@ -1085,7 +1087,6 @@
 
     @when_after(t_scan + half_nb + 1)
     def _():
-        columns_copy(1, 0).start()
         rs_gate[0].advance(1)
         rs_gate[1].advance(0)
 
@@ -1133,7 +1134,6 @@
     def _():
         finish_block(nb - 2)
         finish_block(nb - 1)
-        columns_copy(1, 1).start()
         put_columns(1, 0)
         rs_gate[0].advance(2)
         rs_gate[1].advance(1)
@@ -1259,9 +1259,13 @@
     def _():
         rs_out[0].advance(3)
 
-    @when_after(t_final + 1)
+    @when_after(t_final - 1)
     def _():
         rs_values[0].advance(0)
+
+    @when_after(t_final + 2)
+    def _():
+        rs_values[0].advance(1)
 
     @when_after(t_final + chunks - 1)
     def _():
@@ -1282,7 +1286,6 @@
         rs_small.advance(0)
         rs_gate[1].advance(3)
         add(1)
-        rs_values[0].advance(1)
         rs_small.advance(1)
         rs_values[1].advance(1)
         add(2)
@@ -1336,7 +1339,7 @@
     landing = lambda cols: tuple(
         pltpu.VMEM((2, size >> (s + 1), rows_own, cols), bf16) for s in range(bits)
     )
-    columns = lambda: pltpu.VMEM((2, 2, tokens, inner // 4), bf16)
+    columns = lambda: pltpu.VMEM((2, 2, nb // 2, tokens, LANES), bf16)
     sem = pltpu.SemaphoreType.DMA
     return pl.pallas_call(
         functools.partial(back_kernel, bits),

time: 241 us -> 233 us (0.967)
  Pallas kernels: 228 us -> 220 us
    pallas_call x1, Pallas kernels: 154 us -> 146 us  [back_call(): pl.pallas_call(functools.partial(back_kernel, bits), grid=(3 * nb + chunk...]
where the time goes in v7:
time: 233 us; the launch traced here: 232 us
  Pallas kernels  220 us (94%)
  local copies, waits for them, and re-layouts  11.8 us (5%)
    pallas_call x1, Pallas kernels, back_call(): pl.pallas_call(functools.partial(back_kernel, bits), grid=(3 * nb + chunk...  146 us
    pallas_call x1, Pallas kernels, forward_call(): pl.pallas_call(functools.partial(forward_kernel, size), grid=(2 * nb + ch...  64.7 us
    unnamed x7, local copies, waits for them, and re-layouts  11.2 us
    pallas_call x1, Pallas kernels, final_call(): pl.pallas_call(functools.partial(final_kernel, heads), grid=(tokens // ro...  9.24 us

profile of v7, /device:TPU:0, one launch (start us, length us, event | category | flops | bytes accessed | tf_op | source)
XLA Modules:
  0.0 232.2 jit_solution(14943066358770908959)
XLA Ops:
  0.6 0.0 copy-start
  0.7 0.0 copy-start.1
  0.7 8.8 %copy.31 = bf16[1536,2,1536]{2,0,1:T(8,128)(2,1)} copy(bf16[1536,2,1536]{2,1,0:T(2,128)(2,1)} %param.16) | data formatting | bytes 18874368 | tf_op args[3]
  9.5 0.0 copy-done
  9.5 0.9 copy.27.wstep_ref
  10.4 0.0 copy-done.1
  10.4 0.6 broadcast_in_dim.4.ggain_ref
  11.0 64.7 %forward.1 = (bf16[1536,512]{1,0:T(8,128)(2,1)}, f32[512,128]{1,0:T(8,128)}, f32[512,1536]{1,0:T(8,128)}, bf16[528,1536]{1,0:T(8,128)(2,1)}, f32[4,128,1536]{2,1...) custom-call(bf16[512,1536]{1,0:T(8,128)(2,1)} %hid_ref.3, ...), custom_call_target="tpu_custom_call" | custom-call | tf_op jit(solution)/shard_map/forward/pallas_call | solution.py:533
  75.7 145.7 %back.1 = (f32[96,1536]{1,0:T(8,128)}, f32[2,96,1536]{2,1,0:T(8,128)}, f32[96,256]{1,0:T(8,128)}, f32[512,1536]{1,0:T(8,128)}, f32[16,1536]{1,0:T(8,128)}) custom-call(bf16[1536,512]{1,0:T(8,128)(2,1)} %get-tuple-element.53.gmt_ref, bf16[1536,512]{1,0:T(8,128)(2,1)} %get-tuple-element.54.normedt_ref, bf16[2,768,512]{2,1,0:T(8,128)(2,1)} %get-tuple-element.55.near_ref, ...), custom_call_target="tpu_custom_call" | custom-call | tf_op jit(solution)/shard_map/back/pallas_call | solution.py:1344
  221.5 9.2 %final.1 = (f32[512,1536]{1,0:T(8,128)}, f32[512,1536]{1,0:T(8,128)}, f32[96,1536]{1,0:T(8,128)}, f32[96,2,1536]{2,1,0:T(2,128)}, f32[96,24]{1,0:T(8,128)}, /*in...) custom-call(f32[512,1536]{1,0:T(8,128)} %get-tuple-element.52.out_re, ...), custom_call_target="tpu_custom_call" | custom-call | tf_op jit(solution)/shard_map/final/pallas_call | solution.py:1490
  230.7 1.5 copy.29
Async XLA Ops:
  0.6 8.8 %copy-start = (bf16[1536,24]{0,1:T(8,128)(2,1)S(1)}, bf16[1536,24]{0,1:T(8,128)(2,1)}, u32[]{:S(2)}) copy-start(bf16[1536,24]{0,1:T(8,128)(2,1)} %param.17) | copy-start | bytes 221188
  0.7 9.8 %copy-start.1 = (f32[1536]{0:T(1024)S(1)}, f32[1536]{0:T(1024)}, u32[]{:S(2)}) copy-start(f32[1536]{0:T(1024)} %param.24) | copy-start | bytes 18436

commit v8 on v7

--- a/solution.py
+++ b/solution.py
@@ -1208,9 +1208,12 @@
     def _():
         rs_out[0].advance(2)
 
+    @when_after(t_grad + 2)
+    def _():
+        put_columns(1, 1)
+
     @when_after(t_grad + 3)
     def _():
-        put_columns(1, 1)
         rs_out[1].advance(2)
 
     @when_after(t_grad + 4)
@@ -1263,9 +1266,13 @@
     def _():
         rs_values[0].advance(0)
 
+    @when_after(t_final + 1)
+    def _():
+        rs_values[0].advance(1)
+
     @when_after(t_final + 2)
     def _():
-        rs_values[0].advance(1)
+        rs_values[1].advance(0)
 
     @when_after(t_final + chunks - 1)
     def _():
@@ -1281,7 +1288,6 @@
                 begin(bit + 1)
 
         begin(0)
-        rs_values[1].advance(0)
         add(0)
         rs_small.advance(0)
         rs_gate[1].advance(3)
@@ -1476,7 +1482,7 @@
 def final_call(heads, block_out, grad_hidden, gout, ginner, gsmall, sums):
     tokens, width = block_out.shape
     rows_own, inner = gout.shape
-    rows = 64
+    rows = 256
     shapes = [
         (tokens, width), (tokens, width), (rows_own, inner), (rows_own, 2, inner),
         (rows_own, heads), (rows_own, LANES), (width,), (inner,), (CONV + 1, inner),

time: 233 us -> 228 us (0.979)
  Pallas kernels: 220 us -> 215 us
    pallas_call x1, Pallas kernels: 9.24 us -> 6.15 us  [final_call(): pl.pallas_call(functools.partial(final_kernel, heads), grid=(tokens // ro...]
where the time goes in v8:
time: 228 us; the launch traced here: 227 us
  Pallas kernels  215 us (94%)
  local copies, waits for them, and re-layouts  11.8 us (5%)
    pallas_call x1, Pallas kernels, back_call(): pl.pallas_call(functools.partial(back_kernel, bits), grid=(3 * nb + chunk...  144 us
    pallas_call x1, Pallas kernels, forward_call(): pl.pallas_call(functools.partial(forward_kernel, size), grid=(2 * nb + ch...  64.7 us
    unnamed x7, local copies, waits for them, and re-layouts  11.2 us
    pallas_call x1, Pallas kernels, final_call(): pl.pallas_call(functools.partial(final_kernel, heads), grid=(tokens // ro...  6.15 us

profile of v8, /device:TPU:0, one launch (start us, length us, event | category | flops | bytes accessed | tf_op | source)
XLA Modules:
  0.0 227.2 jit_solution(14786327144743822223)
XLA Ops:
  0.6 0.0 copy-start
  0.7 0.0 copy-start.1
  0.7 8.8 %copy.31 = bf16[1536,2,1536]{2,0,1:T(8,128)(2,1)} copy(bf16[1536,2,1536]{2,1,0:T(2,128)(2,1)} %param.16) | data formatting | bytes 18874368 | tf_op args[3]
  9.5 0.0 copy-done
  9.5 0.9 copy.27.wstep_ref
  10.4 0.0 copy-done.1
  10.4 0.6 broadcast_in_dim.4.ggain_ref
  11.0 64.7 %forward.1 = (bf16[1536,512]{1,0:T(8,128)(2,1)}, f32[512,128]{1,0:T(8,128)}, f32[512,1536]{1,0:T(8,128)}, bf16[528,1536]{1,0:T(8,128)(2,1)}, f32[4,128,1536]{2,1...) custom-call(bf16[512,1536]{1,0:T(8,128)(2,1)} %hid_ref.3, ...), custom_call_target="tpu_custom_call" | custom-call | tf_op jit(solution)/shard_map/forward/pallas_call | solution.py:533
  75.7 143.9 %back.1 = (f32[96,1536]{1,0:T(8,128)}, f32[2,96,1536]{2,1,0:T(8,128)}, f32[96,256]{1,0:T(8,128)}, f32[512,1536]{1,0:T(8,128)}, f32[16,1536]{1,0:T(8,128)}) custom-call(bf16[1536,512]{1,0:T(8,128)(2,1)} %get-tuple-element.53.gmt_ref, bf16[1536,512]{1,0:T(8,128)(2,1)} %get-tuple-element.54.normedt_ref, bf16[2,768,512]{2,1,0:T(8,128)(2,1)} %get-tuple-element.55.near_ref, ...), custom_call_target="tpu_custom_call" | custom-call | tf_op jit(solution)/shard_map/back/pallas_call | solution.py:1350
  219.6 6.1 %final.1 = (f32[512,1536]{1,0:T(8,128)}, f32[512,1536]{1,0:T(8,128)}, f32[96,1536]{1,0:T(8,128)}, f32[96,2,1536]{2,1,0:T(2,128)}, f32[96,24]{1,0:T(8,128)}, /*in...) custom-call(f32[512,1536]{1,0:T(8,128)} %get-tuple-element.52.out_re, ...), custom_call_target="tpu_custom_call" | custom-call | tf_op jit(solution)/shard_map/final/pallas_call | solution.py:1496
  225.8 1.5 copy.29
Async XLA Ops:
  0.6 8.8 %copy-start = (bf16[1536,24]{0,1:T(8,128)(2,1)S(1)}, bf16[1536,24]{0,1:T(8,128)(2,1)}, u32[]{:S(2)}) copy-start(bf16[1536,24]{0,1:T(8,128)(2,1)} %param.17) | copy-start | bytes 221188
  0.7 9.8 %copy-start.1 = (f32[1536]{0:T(1024)S(1)}, f32[1536]{0:T(1024)}, u32[]{:S(2)}) copy-start(f32[1536]{0:T(1024)} %param.24) | copy-start | bytes 18436
